TPU v7x, 32 devices: a whole 2x2x4 slice. The times are simulated.
32 devices in a mesh: tm: 8 (over z, core), bank: 4 (over y, x).
Axes of the slice: x: 2, y: 2, z: 4, core: 2. Of those that a mesh axis runs over, the one named last changes fastest.
Arguments:
- strain: float32 [16, 131072], P('tm', 'bank'), may hold values from -40 to 40
- lengths: int32 [16], P('tm'), may hold values from 65536 to 131072
- templates: bfloat16 [2, 16, 512, 512], P(None, 'bank'), may hold values from -6 to 6
Outputs:
- snr: float32 [16, 2097152], P('bank', 'tm')
All inputs are finite; a program needn't handle non-finite values.
Results may differ from a plain program's by a relative error of at most 0.014.
Values may be sent and summed in bfloat16 or wider, within the bound.
No kernel may reach another device: no remote copies, remote signals or barrier semaphores. Data moves between devices by JAX's collectives and lax.ppermute only.
A program may use at most 128 MiB of HBM per device.

v0:
```python
import functools
import math

import jax
import jax.numpy as jnp
import numpy as np
from jax import lax
from jax.experimental import pallas as pl
from jax.experimental.pallas import tpu as pltpu
from jax.sharding import PartitionSpec as P

epsilon = 1e-06
bf16 = jnp.bfloat16
f32 = jnp.float32


def dot(a, b):
    return jnp.dot(a, b, preferred_element_type=f32)


def tables(order):
    half = order // 2
    rows = half + 16
    a = np.arange(rows)
    keep = (a <= half)[:, None]
    turn = 2.0 * math.pi / order

    def angle(left, right):
        return turn * ((left[:, None] * right[None, :]) % order)

    u, v = np.arange(half), np.arange(order)
    first = np.concatenate([np.cos(angle(a, u)) * keep, -np.sin(angle(a, u)) * keep])
    twist = (2.0 * math.pi / order**2) * (a[:, None] * v[None, :])
    even, odd = angle(u, 2 * u), angle(u, 2 * u + 1)
    sections = [np.cos(even), np.sin(even), np.cos(odd), np.sin(odd), np.cos(odd).T, np.sin(odd).T]
    last_cos, last_sin = np.cos(angle(u, u)), -np.sin(angle(u, u))
    last_cos[:, 0] = 0.5
    last_sin[:, 0] = 0.5 * (1.0 - 2.0 * (u % 2))
    return dict(
        first=first.astype(bf16),
        twist=np.stack([np.cos(twist), np.sin(twist)]).astype(np.float32),
        sections=np.stack(sections).astype(bf16),
        last=np.concatenate([last_cos, last_sin], axis=1).astype(bf16),
    )


def fill_sections(dest, cosine, sine, sign):
    half = cosine.shape[0]
    positive, negative = (sine, -sine) if sign > 0 else (-sine, sine)
    dest[:half, :half] = cosine
    dest[:half, half:] = positive
    dest[half:, :half] = negative
    dest[half:, half:] = cosine


def spectrum(samples, first, twist, even_table, odd_table):
    rows = first.shape[0] // 2
    half = first.shape[1]
    out = dot(first[...], samples)
    real, imag = out[:rows], out[rows:]
    tc, ts = twist[0], twist[1]
    tr = real * tc + imag * ts
    ti = imag * tc - real * ts
    plus = jnp.concatenate([tr[:, :half] + tr[:, half:], ti[:, :half] + ti[:, half:]], axis=1)
    minus = jnp.concatenate([tr[:, :half] - tr[:, half:], ti[:, :half] - ti[:, half:]], axis=1)
    return dot(plus.astype(bf16), even_table[...]), dot(minus.astype(bf16), odd_table[...])


def alternate(values):
    row = lax.broadcasted_iota(jnp.int32, values.shape, 0)
    return jnp.where(row % 2 == 0, values, -values)


def spectrum_kernel(
    place, *refs, shards
):
    pieces = refs[:shards]
    first, twist, sections = refs[shards : shards + 3]
    kept, summed, power, last_block, samples, even_table, odd_table = refs[shards + 3 :]
    rows = first.shape[0] // 2
    half = first.shape[1]
    piece_rows = pieces[0].shape[1]
    for s in range(shards):
        at = pl.multiple_of((place[0] ^ s) * piece_rows, piece_rows)
        samples[:, pl.ds(at, piece_rows), :] = pieces[s][...]
    fill_sections(even_table, sections[0], sections[1], -1)
    fill_sections(odd_table, sections[2], sections[3], -1)
    last_block[...] = samples[1]
    even0, odd0 = spectrum(samples[0], first, twist, even_table, odd_table)
    even1, odd1 = spectrum(samples[1], first, twist, even_table, odd_table)
    for side, (one, two) in enumerate(((even0, even1), (odd0, odd1))):
        at = side * half
        for part in range(2):
            x0 = one[:, part * half : (part + 1) * half]
            x1 = two[:, part * half : (part + 1) * half]
            kept[part, :, at : at + half] = x0
            summed[part, :, at : at + half] = x1 + alternate(x0)
        total = (
            one[:, :half] * one[:, :half]
            + one[:, half:] * one[:, half:]
            + two[:, :half] * two[:, :half]
            + two[:, half:] * two[:, half:]
        )
        for lane in range(half // 128):
            row = (side * (half // 128) + lane) * rows
            power[row : row + rows, :] = total[:, lane * 128 : (lane + 1) * 128].astype(bf16)


def previous_kernel(samples, kept, first, twist, sections, summed, even_table, odd_table):
    half = first.shape[1]
    fill_sections(even_table, sections[0], sections[1], -1)
    fill_sections(odd_table, sections[2], sections[3], -1)
    sides = spectrum(samples[...], first, twist, even_table, odd_table)
    for side in range(2):
        at = side * half
        for part in range(2):
            x = sides[side][:, part * half : (part + 1) * half]
            summed[part, :, at : at + half] = kept[part, :, at : at + half] + alternate(x)


def template_kernel(templates, folded, factor):
    order = templates.shape[-1]
    half = order // 2
    quarter = half // 2
    rows = folded.shape[2]
    a = lax.broadcasted_iota(jnp.int32, (rows, half), 0)
    r = lax.broadcasted_iota(jnp.int32, (rows, half), 1)
    flip = jnp.where((r == half - a) & (a >= 1), 1.0, 0.0).astype(bf16)
    m = lax.broadcasted_iota(jnp.int32, (half, half), 0)
    q = lax.broadcasted_iota(jnp.int32, (half, half), 1)
    source = jnp.where(q < quarter, 2 * q, 2 * (q - quarter) + 1)
    order_up = jnp.where(m == source, 1.0, 0.0).astype(bf16)
    order_down = jnp.where(m == half - 1 - source, 1.0, 0.0).astype(bf16)
    top_row = lax.broadcasted_iota(jnp.int32, (8, half), 0) == 0
    energy = jnp.zeros((8, order), f32)
    for part in range(2):
        whole = templates[part, 0]
        square = whole.astype(f32) * whole.astype(f32)
        energy = energy + jnp.sum(square.reshape(order // 8, 8, order), axis=0)
        upper = whole[:rows]
        lower = dot(flip, whole[half:])
        first = lax.broadcasted_iota(jnp.int32, (rows, order), 0) == 0
        lower = jnp.where(first, whole[0:1].astype(f32), lower).astype(bf16)
        up = [dot(upper[:, :half], order_up), dot(upper[:, half:], order_up)]
        down = [dot(lower[:, half:], order_down), dot(lower[:, :half], order_down)]

        def sides(pair):
            return [
                jnp.concatenate([pair[0][:, at : at + quarter], pair[1][:, at : at + quarter]], axis=1)
                for at in (0, quarter)
            ]

        up_even, up_odd = sides(up)
        down_even, down_odd = sides(down)
        fixed_even = jnp.where(top_row, pltpu.roll(down_odd[:8], 1, 1), down_even[:8])
        fixed_odd = jnp.where(top_row, down_even[:8], down_odd[:8])
        down_even = jnp.concatenate([fixed_even, down_even[8:]], axis=0)
        down_odd = jnp.concatenate([fixed_odd, down_odd[8:]], axis=0)
        sign = 1.0 if part == 0 else -1.0
        folded[0, part, :, :half] = (up_even + sign * down_even).astype(bf16)
        folded[0, part, :, half:] = (up_odd + sign * down_odd).astype(bf16)
    total = jnp.sum(jnp.sum(energy, axis=1, keepdims=True), axis=0, keepdims=True)
    factor[0] = jnp.broadcast_to(lax.rsqrt(total), factor.shape[1:])


def filter_kernel(
    place, mine, theirs, earlier, later, folded, factor, twist, sections, last, out,
    weight, white, even_table, odd_table, back, *, blocks
):
    half = last.shape[0]
    rows = twist.shape[1]
    count = pl.num_programs(1)
    block, template = pl.program_id(0), pl.program_id(1)

    @pl.when((block == 0) & (template == 0))
    def _():
        fill_sections(even_table, sections[0], sections[1], 1)
        fill_sections(odd_table, sections[4], sections[5], 1)
        chunk = mine.shape[1]
        for s in range(mine.shape[0]):
            for pieces, core in ((mine, place[1]), (theirs, 1 - place[1])):
                at = pl.multiple_of(((place[0] ^ s) * 2 + core) * chunk, 8)
                total = pieces[s].astype(f32)
                weight[pl.ds(at, chunk), :] = lax.rsqrt(total / blocks + epsilon)

    def whiten(spectra):
        for part in range(2):
            for lane in range(2 * half // 128):
                cols = slice(lane * 128, (lane + 1) * 128)
                white[part, :, cols] = spectra[part, :, cols] * weight[lane * rows : (lane + 1) * rows, :]

    @pl.when((block == 0) & (template == 0))
    def _():
        whiten(earlier)

    @pl.when((block == 1) & (template == 0))
    def _():
        whiten(later)

    vr, vi = white[0], white[1]
    gr, gi = folded[0, 0].astype(f32), folded[0, 1].astype(f32)
    pr = (gr * vr + gi * vi).astype(bf16)
    pi = (gr * vi - gi * vr).astype(bf16)
    even = dot(jnp.concatenate([pr[:, :half], pi[:, :half]], axis=1), even_table[...])
    odd = dot(jnp.concatenate([pr[:, half:], pi[:, half:]], axis=1), odd_table[...])
    er, ei, orr, oi = even[:, :half], even[:, half:], odd[:, :half], odd[:, half:]
    for side, (ir, ii) in enumerate(((er + orr, ei + oi), (er - orr, ei - oi))):
        cols = slice(side * half, (side + 1) * half)
        tc, ts = twist[0, :, cols], twist[1, :, cols]
        br = ir * tc - ii * ts
        bi = ii * tc + ir * ts
        back[:half, cols] = br[:half].astype(bf16)
        back[half:, cols] = bi[:half].astype(bf16)
        first = lax.broadcasted_iota(jnp.int32, (16, half), 0) == 0
        back[half : half + 16, cols] = jnp.where(first, br[half : half + 1], bi[:16]).astype(bf16)
    scale = factor[0, 0:1, :]
    result = dot(last[...], back[...])
    lanes = 2 * half // 128
    for lane in range(lanes):
        piece = result[:, lane * 128 : (lane + 1) * 128] * scale
        out[pl.ds(lane * count + template, half, stride=lanes * count), :] = piece


def exchange(values, axis, pairs_of):
    size = lax.axis_size(axis)
    return lax.ppermute(values, axis, [(i, pairs_of(i)) for i in range(size)])


def body(strain, lengths, templates):
    blocks_here, local = strain.shape
    count, order = templates.shape[1], templates.shape[-1]
    half = order // 2
    rows = half + 16
    banks, groups = lax.axis_size("bank"), lax.axis_size("tm")
    bank, group = lax.axis_index("bank"), lax.axis_index("tm")
    core = group % 2
    place = jnp.stack([bank, core]).astype(jnp.int32)
    table = tables(order)
    vmem = pl.BlockSpec(memory_space=pltpu.VMEM)
    smem = pl.BlockSpec(memory_space=pltpu.SMEM)
    limit = pltpu.CompilerParams(vmem_limit_bytes=60 * 1024 * 1024)

    index = bank * local + jnp.arange(local, dtype=jnp.int32)
    valid = index[None, :] < lengths[:, None]
    gated = jnp.where(valid, strain, 0.0).astype(bf16).reshape(blocks_here, local // order, order)
    pieces = [gated] + [exchange(gated, "bank", lambda i, s=s: i ^ s) for s in range(1, banks)]

    folded, factor = pl.pallas_call(
        template_kernel,
        grid=(count,),
        in_specs=[pl.BlockSpec((2, 1, order, order), lambda t: (0, t, 0, 0))],
        out_specs=[
            pl.BlockSpec((1, 2, rows, order), lambda t: (t, 0, 0, 0)),
            pl.BlockSpec((1, 8, 128), lambda t: (t, 0, 0)),
        ],
        out_shape=[
            jax.ShapeDtypeStruct((count, 2, rows, order), bf16),
            jax.ShapeDtypeStruct((count, 8, 128), f32),
        ],
        cost_estimate=pl.CostEstimate(flops=int(6e9), bytes_accessed=int(6.5e6), transcendentals=0),
        compiler_params=limit,
        name="fold_templates",
    )(templates)

    plane = jax.ShapeDtypeStruct((2, rows, order), f32)
    square = pltpu.VMEM((order, order), bf16)
    kept, later, power, last_block = pl.pallas_call(
        functools.partial(spectrum_kernel, shards=banks),
        in_specs=[smem] + [vmem] * (banks + 3),
        out_specs=[vmem] * 4,
        out_shape=[
            plane,
            plane,
            jax.ShapeDtypeStruct((rows * order // 128, 128), bf16),
            jax.ShapeDtypeStruct((half, order), bf16),
        ],
        scratch_shapes=[pltpu.VMEM((blocks_here, half, order), bf16), square, square],
        cost_estimate=pl.CostEstimate(flops=int(2e9), bytes_accessed=int(5e6), transcendentals=0),
        compiler_params=limit,
        name="spectra",
    )(place, *pieces, table["first"], table["twist"], table["sections"])

    chunk = power.shape[0] // (2 * banks)
    own_part = lax.dynamic_index_in_dim(power.reshape(banks, 2, chunk, 128), bank, 0, False)
    mine = lax.dynamic_index_in_dim(own_part, core, 0, False)
    other = lax.dynamic_index_in_dim(own_part, 1 - core, 0, False)
    partner = exchange(other, "tm", lambda i: i ^ 1)
    chip = (mine.astype(f32) + partner.astype(f32)).astype(bf16)
    share = chip.astype(f32)
    for step in range(1, groups // 2):
        share = share + exchange(chip, "tm", lambda i, s=step: i ^ (2 * s)).astype(f32)
    share = share.astype(bf16)
    last_block, share = lax.optimization_barrier((last_block, share))
    mine = jnp.stack([share] + [exchange(share, "bank", lambda i, s=s: i ^ s) for s in range(1, banks)])
    theirs = exchange(mine, "tm", lambda i: i ^ 1)

    before = lax.ppermute(last_block, "tm", [(i, i + 1) for i in range(groups - 1)])
    earlier = pl.pallas_call(
        previous_kernel,
        in_specs=[vmem] * 5,
        out_specs=vmem,
        out_shape=plane,
        scratch_shapes=[square, square],
        cost_estimate=pl.CostEstimate(flops=int(1e9), bytes_accessed=int(4e6), transcendentals=0),
        compiler_params=limit,
        name="previous",
    )(before, kept, table["first"], table["twist"], table["sections"])

    lines = count * half * order // 128
    out = pl.pallas_call(
        functools.partial(filter_kernel, blocks=float(blocks_here * groups)),
        grid=(blocks_here, count),
        in_specs=[smem, vmem, vmem, vmem, vmem]
        + [
            pl.BlockSpec((1, 2, rows, order), lambda c, t: (t, 0, 0, 0)),
            pl.BlockSpec((1, 8, 128), lambda c, t: (t, 0, 0)),
        ]
        + [vmem] * 3,
        out_specs=pl.BlockSpec((lines, 128), lambda c, t: (c, 0)),
        out_shape=jax.ShapeDtypeStruct((blocks_here * lines, 128), f32),
        scratch_shapes=[
            pltpu.VMEM((rows * order // 128, 128), f32),
            pltpu.VMEM((2, rows, order), f32),
            square,
            square,
            square,
        ],
        cost_estimate=pl.CostEstimate(flops=int(6e9), bytes_accessed=int(1.2e7), transcendentals=0),
        compiler_params=limit,
        name="filter",
    )(place, mine, theirs, earlier, later, folded, factor, table["twist"], table["sections"], table["last"])
    split = out.reshape(blocks_here * half * order // 128, count, 128)
    return jnp.swapaxes(split, 0, 1).reshape(count, blocks_here * half * order)


def solution(mesh):
    in_specs = (P("tm", "bank"), P("tm"), P(None, "bank", None, None))
    out_specs = P("bank", "tm")
    return jax.shard_map(body, mesh=mesh, in_specs=in_specs, out_specs=out_specs, check_vma=False)
```

profile of v0, /device:TPU:1, one launch (start us, length us, event | category | flops | bytes accessed | tf_op | source)
XLA Modules:
  0.0 58.9 jit_solution(6470974819794171501)
XLA Ops:
  0.0 1.2 %fusion = bf16[2,32768]{1,0:T(2,128)(2,1)S(1)} fusion(f32[2,32768]{1,0:T(2,128)} %param.7, s32[32768]{0:T(1024)S(1)} %iota_add_fusion, s32[2]{0:T(128)} %param.8), kind=kLoop, calls=%fused_computation.1 | loop fusion | flops 131072 | bytes 524296 | tf_op jit(solution)/shard_map/convert_element_type | solution.py:245
  1.2 0.0 copy-start.2
  1.2 3.0 %collective-permute-start.2 = (bf16[2,64,512]{2,1,0:T(8,128)(2,1)S(1)}, bf16[2,64,512]{2,1,0:T(8,128)(2,1)S(1)}, u32[]{:S(2)}, u32[]{:S(2)}) collective-permute-start(bf16[2,64,512]{2,1,0:T(8,128)(2,1)S(1)} %bitcast.23), channel_id=1, source_target_pairs={{0,3},{1,2},{2,1},{3,0},{4,7},{5,6},{6,5},{7,4},{8,11},{9,10},{10,... | collective-permute-start | bytes 393224 | tf_op jit(solution)/shard_map/ppermute | solution.py:226
  4.3 0.2 collective-permute-start.1
  4.5 0.1 collective-permute-start
  4.7 0.6 %pad_add_fusion.place = s32[2]{0:T(128)} fusion(s32[1]{0:T(128)} %bitcast.1, s32[1]{0:T(128)} %bitcast), kind=kLoop, calls=%fused_computation.9 | loop fusion | flops 2 | bytes 16 | tf_op jit(solution)/shard_map/stack | solution.py:237
  5.3 2.2 %collective-permute-done.2.refs_3_ = bf16[2,64,512]{2,1,0:T(8,128)(2,1)S(1)} collective-permute-done((bf16[2,64,512]{2,1,0:T(8,128)(2,1)S(1)}, bf16[2,64,512]{2,1,0:T(8,128)(2,1)S(1)}, u32[]{:S(2)}, u32[]{:S(2)}) %collective-permute-start.2) | collective-permute-done | bytes 131104 | tf_op jit(solution)/shard_map/ppermute | solution.py:226
  7.5 0.0 copy-start.4
  7.5 3.5 %collective-permute-done.1.refs_2_ = bf16[2,64,512]{2,1,0:T(8,128)(2,1)S(1)} collective-permute-done((bf16[2,64,512]{2,1,0:T(8,128)(2,1)S(1)}, bf16[2,64,512]{2,1,0:T(8,128)(2,1)S(1)}, u32[]{:S(2)}, u32[]{:S(2)}) %collective-permute-start.1) | collective-permute-done | bytes 131104 | tf_op jit(solution)/shard_map/ppermute | solution.py:226
  11.0 0.0 copy-start.5
  11.0 0.0 collective-permute-done.refs_1_
  11.0 0.0 copy-done.2
  11.0 0.0 copy-done.4
  11.1 0.6 %copy-done.5 = bf16[2,64,512]{2,1,0:T(8,128)(2,1)} copy-done((bf16[2,64,512]{2,1,0:T(8,128)(2,1)}, bf16[2,64,512]{2,1,0:T(8,128)(2,1)S(1)}, u32[]{:S(2)}) %copy-start.5) | copy-done | bytes 131096
  11.7 0.0 copy-start.6
  11.7 0.6 %copy-done.6 = bf16[2,64,512]{2,1,0:T(8,128)(2,1)} copy-done((bf16[2,64,512]{2,1,0:T(8,128)(2,1)}, bf16[2,64,512]{2,1,0:T(8,128)(2,1)S(1)}, u32[]{:S(2)}) %copy-start.6) | copy-done | bytes 131096
  12.3 4.3 %spectra.1 = (f32[2,272,512]{2,1,0:T(8,128)}, f32[2,272,512]{2,1,0:T(8,128)}, bf16[1088,128]{1,0:T(8,128)(2,1)}, bf16[256,512]{1,0:T(8,128)(2,1)}) custom-call(s32[2]{0:T(128)} %pad_add_fusion.place, bf16[2,64,512]{2,1,0:T(8,128)(2,1)} %bitcast.26, bf16[2,64,512]{2,1,0:T(8,128)(2,1)} %copy-done.6, bf16[2,64,512]{2,1,0:T(8,128)(2,1)} %copy-done.5, ...), custom_call_target="tpu_custom_call" | custom-call | flops 2000000000 | bytes 5000000 | tf_op jit(solution)/shard_map/spectra/pallas_call | solution.py:267
  16.7 0.8 %dynamic-slice_bitcast_fusion = bf16[136,128]{1,0:T(8,128)(2,1)S(1)} fusion(bf16[4,2,136,128]{3,2,1,0:T(8,128)(2,1)} %bitcast.30, s32[]{:T(128)S(6)} %select_n.31, s32[]{:T(128)S(6)} %select_n.35), kind=kLoop, calls=%fused_computation.8 | loop fusion | bytes 69640 | tf_op jit(solution)/shard_map/jit(dynamic_index_in_dim)/squeeze | solution.py:286
  17.4 0.5 collective-permute-start.3
  17.9 0.9 %collective-permute-done.3 = bf16[136,128]{1,0:T(8,128)(2,1)S(1)} collective-permute-done((bf16[136,128]{1,0:T(8,128)(2,1)S(1)}, bf16[136,128]{1,0:T(8,128)(2,1)S(1)}, u32[]{:S(2)}, u32[]{:S(2)}) %collective-permute-start.3) | collective-permute-done | bytes 34848 | tf_op jit(solution)/shard_map/ppermute | solution.py:226
  18.8 0.8 %fusion.1 = bf16[136,128]{1,0:T(8,128)(2,1)S(1)} fusion(bf16[136,128]{1,0:T(8,128)(2,1)S(1)} %collective-permute-done.3, bf16[4,2,136,128]{3,2,1,0:T(8,128)(2,1)} %bitcast.31, s32[]{:T(128)S(6)} %select_n.31, s32[]{:T(128)S(6)} %select_n.33), kind=kLoop, calls=%fused_computation.6 | loop fusion | flops 69632 | bytes 104456 | tf_op jit(solution)/shard_map/convert_element_type | solution.py:288
  19.6 3.6 %collective-permute-start.6 = (bf16[136,128]{1,0:T(8,128)(2,1)S(1)}, bf16[136,128]{1,0:T(8,128)(2,1)S(1)}, u32[]{:S(2)}, u32[]{:S(2)}) collective-permute-start(bf16[136,128]{1,0:T(8,128)(2,1)S(1)} %fusion.1), channel_id=1, source_target_pairs={{0,24},{4,28},{8,16},{12,20},{16,8},{20,12},{24,0},{28,4},{1,25},{... | collective-permute-start | bytes 104456 | tf_op jit(solution)/shard_map/ppermute | solution.py:226
  23.2 0.0 collective-permute-start.5
  23.2 0.4 collective-permute-start.4
  23.5 1.1 %collective-permute-done.6 = bf16[136,128]{1,0:T(8,128)(2,1)S(1)} collective-permute-done((bf16[136,128]{1,0:T(8,128)(2,1)S(1)}, bf16[136,128]{1,0:T(8,128)(2,1)S(1)}, u32[]{:S(2)}, u32[]{:S(2)}) %collective-permute-start.6) | collective-permute-done | bytes 34848 | tf_op jit(solution)/shard_map/ppermute | solution.py:226
  24.6 2.6 %collective-permute-done.5 = bf16[136,128]{1,0:T(8,128)(2,1)S(1)} collective-permute-done((bf16[136,128]{1,0:T(8,128)(2,1)S(1)}, bf16[136,128]{1,0:T(8,128)(2,1)S(1)}, u32[]{:S(2)}, u32[]{:S(2)}) %collective-permute-start.5) | collective-permute-done | bytes 34848 | tf_op jit(solution)/shard_map/ppermute | solution.py:226
  27.2 0.0 collective-permute-done.4
  27.3 1.5 %collective-permute-start.9 = (bf16[136,128]{1,0:T(8,128)(2,1)S(1)}, bf16[136,128]{1,0:T(8,128)(2,1)S(1)}, u32[]{:S(2)}, u32[]{:S(2)}) collective-permute-start(bf16[136,128]{1,0:T(8,128)(2,1)S(1)} %add_convert_fusion), channel_id=1, source_target_pairs={{0,3},{1,2},{2,1},{3,0},{4,7},{5,6},{6,5},{7,4},{8,11},{9,10},{10,... | collective-permute-start | bytes 104456 | tf_op jit(solution)/shard_map/ppermute | solution.py:226
  28.8 0.9 %collective-permute-start.8 = (bf16[136,128]{1,0:T(8,128)(2,1)S(1)}, bf16[136,128]{1,0:T(8,128)(2,1)S(1)}, u32[]{:S(2)}, u32[]{:S(2)}) collective-permute-start(bf16[136,128]{1,0:T(8,128)(2,1)S(1)} %add_convert_fusion), channel_id=1, source_target_pairs={{0,2},{1,3},{2,0},{3,1},{4,6},{5,7},{6,4},{7,5},{8,10},{9,11},{10,... | collective-permute-start | bytes 104456 | tf_op jit(solution)/shard_map/ppermute | solution.py:226
  29.7 0.3 collective-permute-start.7
  30.0 3.9 %collective-permute-start.11 = (bf16[256,512]{1,0:T(8,128)(2,1)}, bf16[256,512]{1,0:T(8,128)(2,1)S(1)}, u32[]{:S(2)}, u32[]{:S(2)}) collective-permute-start(bf16[256,512]{1,0:T(8,128)(2,1)} %get-tuple-element.16), channel_id=1, source_target_pairs={{0,4},{4,8},{8,12},{12,16},{16,20},{20,24},{24,28},{1,5},{5,9},{9,... | collective-permute-start | bytes 786440 | tf_op jit(solution)/shard_map/ppermute | solution.py:297
  33.9 0.0 collective-permute-done.9
  33.9 0.0 collective-permute-done.8
  33.9 0.0 collective-permute-done.7
  33.9 0.0 copy-start.1
  34.0 1.8 %collective-permute-start.10 = (bf16[4,136,128]{2,1,0:T(8,128)(2,1)S(1)}, bf16[4,136,128]{2,1,0:T(8,128)(2,1)S(1)}, u32[]{:S(2)}, u32[]{:S(2)}) collective-permute-start(bf16[4,136,128]{2,1,0:T(8,128)(2,1)S(1)} %pad_maximum_fusion.mine), channel_id=1, source_target_pairs={{0,4},{4,0},{8,12},{12,8},{16,20},{20,16},{24,28},{28,24},{1,5},{5... | collective-permute-start | bytes 417800 | tf_op jit(solution)/shard_map/ppermute | solution.py:226
  35.7 5.4 %fold_templates.1 = (bf16[4,2,272,512]{3,2,1,0:T(8,128)(2,1)}, f32[4,8,128]{2,1,0:T(8,128)}) custom-call(bf16[2,4,512,512]{3,2,1,0:T(8,128)(2,1)} %templates.1), custom_call_target="tpu_custom_call" | custom-call | flops 6000000000 | bytes 6500000 | tf_op jit(solution)/shard_map/fold_templates/pallas_call | solution.py:248
  41.1 0.0 copy-done.1
  41.1 0.0 collective-permute-done.11.samples
  41.1 0.0 copy-start
  41.1 0.7 %copy-done = bf16[256,512]{1,0:T(8,128)(2,1)} copy-done((bf16[256,512]{1,0:T(8,128)(2,1)}, bf16[256,512]{1,0:T(8,128)(2,1)S(1)}, u32[]{:S(2)}) %copy-start) | copy-done | bytes 262168
  41.9 3.8 %previous.1.earlier = f32[2,272,512]{2,1,0:T(8,128)} custom-call(bf16[256,512]{1,0:T(8,128)(2,1)} %copy-done, f32[2,272,512]{2,1,0:T(8,128)} %get-tuple-element.17.kept, bf16[544,256]{1,0:T(8,128)(2,1)} %constant.88.clone.refs_4_.first, f32[2,272,512]{2,1,0:T(8,128)} %constant.89.clone.refs_5_.twist, bf16[6,256,256]{2,1,0:T(8,128)(2,1)} %constant.90.clone.refs_6_.sections), custom_call_target="tpu_custom_call" | custom-call | flops 1000000000 | bytes 4000000 | tf_op jit(solution)/shard_map/previous/pallas_call | solution.py:298
  45.6 0.0 collective-permute-done.10.theirs
  45.6 0.0 copy-start.3
  45.6 0.6 %copy-done.3 = bf16[4,136,128]{2,1,0:T(8,128)(2,1)} copy-done((bf16[4,136,128]{2,1,0:T(8,128)(2,1)}, bf16[4,136,128]{2,1,0:T(8,128)(2,1)S(1)}, u32[]{:S(2)}) %copy-start.3) | copy-done | bytes 139288
  46.3 12.6 %filter.1 = f32[8192,128]{1,0:T(8,128)} custom-call(s32[2]{0:T(128)} %pad_add_fusion.place, bf16[4,136,128]{2,1,0:T(8,128)(2,1)} %copy-done.1, bf16[4,136,128]{2,1,0:T(8,128)(2,1)} %copy-done.3, f32[2,272,512]{2,1,0:T(8,128)} %previous.1.earlier, f32[2,272,512]{2,1,0:T(8,128)} %get-tuple-element.18.later, bf16[4,2,272,512]{3,2,1,0:T(8,128)(2,1)} %get-tuple-element.19.folded, ...), custom_call_target="tpu_custom_call" | custom-call | flops 6000000000 | bytes 12000000 | tf_op jit(solution)/shard_map/filter/pallas_call | solution.py:310
  (4 shorter events, 0.1 us)
Async XLA Ops:
  1.2 9.8 %copy-start.2 = (bf16[1,2,64,512]{3,2,1,0:T(8,128)(2,1)}, bf16[1,2,64,512]{3,2,1,0:T(8,128)(2,1)S(1)}, u32[]{:S(2)}) copy-start(bf16[1,2,64,512]{3,2,1,0:T(8,128)(2,1)S(1)} %copy.11) | copy-start | bytes 393220
  1.2 6.3 %collective-permute-start.2 = (bf16[2,64,512]{2,1,0:T(8,128)(2,1)S(1)}, bf16[2,64,512]{2,1,0:T(8,128)(2,1)S(1)}, u32[]{:S(2)}, u32[]{:S(2)}) collective-permute-start(bf16[2,64,512]{2,1,0:T(8,128)(2,1)S(1)} %bitcast.23), channel_id=1, source_target_pairs={{0,3},{1,2},{2,1},{3,0},{4,7},{5,6},{6,5},{7,4},{8,11},{9,10},{10,... | collective-permute-start | bytes 393224 | tf_op jit(solution)/shard_map/ppermute | solution.py:226
  4.3 6.7 %collective-permute-start.1 = (bf16[2,64,512]{2,1,0:T(8,128)(2,1)S(1)}, bf16[2,64,512]{2,1,0:T(8,128)(2,1)S(1)}, u32[]{:S(2)}, u32[]{:S(2)}) collective-permute-start(bf16[2,64,512]{2,1,0:T(8,128)(2,1)S(1)} %bitcast.24), channel_id=1, source_target_pairs={{0,2},{1,3},{2,0},{3,1},{4,6},{5,7},{6,4},{7,5},{8,10},{9,11},{10,... | collective-permute-start | bytes 393224 | tf_op jit(solution)/shard_map/ppermute | solution.py:226
  4.5 6.5 %collective-permute-start = (bf16[2,64,512]{2,1,0:T(8,128)(2,1)S(1)}, bf16[2,64,512]{2,1,0:T(8,128)(2,1)S(1)}, u32[]{:S(2)}, u32[]{:S(2)}) collective-permute-start(bf16[2,64,512]{2,1,0:T(8,128)(2,1)S(1)} %bitcast.25), channel_id=1, source_target_pairs={{0,1},{1,0},{2,3},{3,2},{4,5},{5,4},{6,7},{7,6},{8,9},{9,8},{10,11... | collective-permute-start | bytes 393224 | tf_op jit(solution)/shard_map/ppermute | solution.py:226
  7.5 3.6 %copy-start.4 = (bf16[2,64,512]{2,1,0:T(8,128)(2,1)}, bf16[2,64,512]{2,1,0:T(8,128)(2,1)S(1)}, u32[]{:S(2)}) copy-start(bf16[2,64,512]{2,1,0:T(8,128)(2,1)S(1)} %collective-permute-done.2.refs_3_) | copy-start | bytes 393220
  11.0 0.7 %copy-start.5 = (bf16[2,64,512]{2,1,0:T(8,128)(2,1)}, bf16[2,64,512]{2,1,0:T(8,128)(2,1)S(1)}, u32[]{:S(2)}) copy-start(bf16[2,64,512]{2,1,0:T(8,128)(2,1)S(1)} %collective-permute-done.1.refs_2_) | copy-start | bytes 393220
  11.7 0.6 %copy-start.6 = (bf16[2,64,512]{2,1,0:T(8,128)(2,1)}, bf16[2,64,512]{2,1,0:T(8,128)(2,1)S(1)}, u32[]{:S(2)}) copy-start(bf16[2,64,512]{2,1,0:T(8,128)(2,1)S(1)} %collective-permute-done.refs_1_) | copy-start | bytes 393220
  17.4 1.4 %collective-permute-start.3 = (bf16[136,128]{1,0:T(8,128)(2,1)S(1)}, bf16[136,128]{1,0:T(8,128)(2,1)S(1)}, u32[]{:S(2)}, u32[]{:S(2)}) collective-permute-start(bf16[136,128]{1,0:T(8,128)(2,1)S(1)} %dynamic-slice_bitcast_fusion), channel_id=1, source_target_pairs={{0,4},{4,0},{8,12},{12,8},{16,20},{20,16},{24,28},{28,24},{1,5},{5... | collective-permute-start | bytes 104456 | tf_op jit(solution)/shard_map/ppermute | solution.py:226
  19.6 5.0 %collective-permute-start.6 = (bf16[136,128]{1,0:T(8,128)(2,1)S(1)}, bf16[136,128]{1,0:T(8,128)(2,1)S(1)}, u32[]{:S(2)}, u32[]{:S(2)}) collective-permute-start(bf16[136,128]{1,0:T(8,128)(2,1)S(1)} %fusion.1), channel_id=1, source_target_pairs={{0,24},{4,28},{8,16},{12,20},{16,8},{20,12},{24,0},{28,4},{1,25},{... | collective-permute-start | bytes 104456 | tf_op jit(solution)/shard_map/ppermute | solution.py:226
  23.2 4.1 %collective-permute-start.5 = (bf16[136,128]{1,0:T(8,128)(2,1)S(1)}, bf16[136,128]{1,0:T(8,128)(2,1)S(1)}, u32[]{:S(2)}, u32[]{:S(2)}) collective-permute-start(bf16[136,128]{1,0:T(8,128)(2,1)S(1)} %fusion.1), channel_id=1, source_target_pairs={{0,16},{4,20},{8,24},{12,28},{16,0},{20,4},{24,8},{28,12},{1,17},{... | collective-permute-start | bytes 104456 | tf_op jit(solution)/shard_map/ppermute | solution.py:226
  23.2 4.1 %collective-permute-start.4 = (bf16[136,128]{1,0:T(8,128)(2,1)S(1)}, bf16[136,128]{1,0:T(8,128)(2,1)S(1)}, u32[]{:S(2)}, u32[]{:S(2)}) collective-permute-start(bf16[136,128]{1,0:T(8,128)(2,1)S(1)} %fusion.1), channel_id=1, source_target_pairs={{0,8},{4,12},{8,0},{12,4},{16,24},{20,28},{24,16},{28,20},{1,9},{5... | collective-permute-start | bytes 104456 | tf_op jit(solution)/shard_map/ppermute | solution.py:226
  27.3 6.6 %collective-permute-start.9 = (bf16[136,128]{1,0:T(8,128)(2,1)S(1)}, bf16[136,128]{1,0:T(8,128)(2,1)S(1)}, u32[]{:S(2)}, u32[]{:S(2)}) collective-permute-start(bf16[136,128]{1,0:T(8,128)(2,1)S(1)} %add_convert_fusion), channel_id=1, source_target_pairs={{0,3},{1,2},{2,1},{3,0},{4,7},{5,6},{6,5},{7,4},{8,11},{9,10},{10,... | collective-permute-start | bytes 104456 | tf_op jit(solution)/shard_map/ppermute | solution.py:226
  28.8 5.1 %collective-permute-start.8 = (bf16[136,128]{1,0:T(8,128)(2,1)S(1)}, bf16[136,128]{1,0:T(8,128)(2,1)S(1)}, u32[]{:S(2)}, u32[]{:S(2)}) collective-permute-start(bf16[136,128]{1,0:T(8,128)(2,1)S(1)} %add_convert_fusion), channel_id=1, source_target_pairs={{0,2},{1,3},{2,0},{3,1},{4,6},{5,7},{6,4},{7,5},{8,10},{9,11},{10,... | collective-permute-start | bytes 104456 | tf_op jit(solution)/shard_map/ppermute | solution.py:226
  29.7 4.2 %collective-permute-start.7 = (bf16[136,128]{1,0:T(8,128)(2,1)S(1)}, bf16[136,128]{1,0:T(8,128)(2,1)S(1)}, u32[]{:S(2)}, u32[]{:S(2)}) collective-permute-start(bf16[136,128]{1,0:T(8,128)(2,1)S(1)} %add_convert_fusion), channel_id=1, source_target_pairs={{0,1},{1,0},{2,3},{3,2},{4,5},{5,4},{6,7},{7,6},{8,9},{9,8},{10,11... | collective-permute-start | bytes 104456 | tf_op jit(solution)/shard_map/ppermute | solution.py:226
  30.0 11.1 %collective-permute-start.11 = (bf16[256,512]{1,0:T(8,128)(2,1)}, bf16[256,512]{1,0:T(8,128)(2,1)S(1)}, u32[]{:S(2)}, u32[]{:S(2)}) collective-permute-start(bf16[256,512]{1,0:T(8,128)(2,1)} %get-tuple-element.16), channel_id=1, source_target_pairs={{0,4},{4,8},{8,12},{12,16},{16,20},{20,24},{24,28},{1,5},{5,9},{9,... | collective-permute-start | bytes 786440 | tf_op jit(solution)/shard_map/ppermute | solution.py:297
  33.9 7.2 %copy-start.1 = (bf16[4,136,128]{2,1,0:T(8,128)(2,1)}, bf16[4,136,128]{2,1,0:T(8,128)(2,1)S(1)}, u32[]{:S(2)}) copy-start(bf16[4,136,128]{2,1,0:T(8,128)(2,1)S(1)} %pad_maximum_fusion.mine) | copy-start | bytes 417796
  34.0 11.7 %collective-permute-start.10 = (bf16[4,136,128]{2,1,0:T(8,128)(2,1)S(1)}, bf16[4,136,128]{2,1,0:T(8,128)(2,1)S(1)}, u32[]{:S(2)}, u32[]{:S(2)}) collective-permute-start(bf16[4,136,128]{2,1,0:T(8,128)(2,1)S(1)} %pad_maximum_fusion.mine), channel_id=1, source_target_pairs={{0,4},{4,0},{8,12},{12,8},{16,20},{20,16},{24,28},{28,24},{1,5},{5... | collective-permute-start | bytes 417800 | tf_op jit(solution)/shard_map/ppermute | solution.py:226
  41.1 0.7 %copy-start = (bf16[256,512]{1,0:T(8,128)(2,1)}, bf16[256,512]{1,0:T(8,128)(2,1)S(1)}, u32[]{:S(2)}) copy-start(bf16[256,512]{1,0:T(8,128)(2,1)S(1)} %collective-permute-done.11.samples) | copy-start | bytes 786436
  45.6 0.6 %copy-start.3 = (bf16[4,136,128]{2,1,0:T(8,128)(2,1)}, bf16[4,136,128]{2,1,0:T(8,128)(2,1)S(1)}, u32[]{:S(2)}) copy-start(bf16[4,136,128]{2,1,0:T(8,128)(2,1)S(1)} %collective-permute-done.10.theirs) | copy-start | bytes 417796
where the time goes:
time: 59.4 us; the launch traced here: 58.9 us
  Pallas kernels  26.1 us (44%)
  starting transfers between devices  16.2 us (27%)
  waiting for transfers between devices  10.4 us (18%)
  local copies, waits for them, and re-layouts  3.43 us (6%)
  other arithmetic  2.62 us (4%)
    pallas_call x1, Pallas kernels, body(): pl.pallas_call(functools.partial(filter_kernel, blocks=float(blocks_here...  12.6 us
    ppermute x11, starting transfers between devices, exchange(): return lax.ppermute(values, axis, [(i, pairs_of(i)) for i in range(size)])  12.3 us
    ppermute x11, waiting for transfers between devices, exchange(): return lax.ppermute(values, axis, [(i, pairs_of(i)) for i in range(size)])  10.4 us
    pallas_call x1, Pallas kernels, body(): pl.pallas_call(template_kernel, grid=(count,), in_specs=[pl.BlockSpec((2,...  5.41 us
    pallas_call x1, Pallas kernels, body(): pl.pallas_call(functools.partial(spectrum_kernel, shards=banks), in_specs...  4.34 us
    ppermute x1, starting transfers between devices, body(): lax.ppermute(last_block, 'tm', [(i, i + 1) for i in range(groups - 1)])  3.88 us
    pallas_call x1, Pallas kernels, body(): pl.pallas_call(previous_kernel, in_specs=[vmem] * 5, out_specs=vmem, out_...  3.77 us
    unnamed x15, local copies, waits for them, and re-layouts  2.67 us
  transfers between devices with their start and end apart: 12, of which 5 were waited for; matrix products, arithmetic and copies ran while one was open for 1% of the time, Pallas kernels for 16%

commit v1 on v0

--- a/solution.py
+++ b/solution.py
@@ -71,17 +71,16 @@
     return jnp.where(row % 2 == 0, values, -values)
 
 
-def spectrum_kernel(
-    place, *refs, shards
-):
+def spectrum_kernel(*refs, shards):
     pieces = refs[:shards]
     first, twist, sections = refs[shards : shards + 3]
-    kept, summed, power, last_block, samples, even_table, odd_table = refs[shards + 3 :]
+    kept, summed, mine, other, last_block, samples, power, even_table, odd_table = refs[shards + 3 :]
     rows = first.shape[0] // 2
     half = first.shape[1]
     piece_rows = pieces[0].shape[1]
+    bank, core = lax.axis_index("bank"), lax.rem(lax.axis_index("tm"), 2)
     for s in range(shards):
-        at = pl.multiple_of((place[0] ^ s) * piece_rows, piece_rows)
+        at = pl.multiple_of((bank ^ s) * piece_rows, piece_rows)
         samples[:, pl.ds(at, piece_rows), :] = pieces[s][...]
     fill_sections(even_table, sections[0], sections[1], -1)
     fill_sections(odd_table, sections[2], sections[3], -1)
@@ -93,8 +92,8 @@
         for part in range(2):
             x0 = one[:, part * half : (part + 1) * half]
             x1 = two[:, part * half : (part + 1) * half]
-            kept[part, :, at : at + half] = x0
-            summed[part, :, at : at + half] = x1 + alternate(x0)
+            kept[part, :, at : at + half] = x0.astype(bf16)
+            summed[part, :, at : at + half] = (x1 + alternate(x0)).astype(bf16)
         total = (
             one[:, :half] * one[:, :half]
             + one[:, half:] * one[:, half:]
@@ -103,7 +102,11 @@
         )
         for lane in range(half // 128):
             row = (side * (half // 128) + lane) * rows
-            power[row : row + rows, :] = total[:, lane * 128 : (lane + 1) * 128].astype(bf16)
+            power[row : row + rows, :] = total[:, lane * 128 : (lane + 1) * 128]
+    chunk = mine.shape[0]
+    for dest, which in ((mine, core), (other, 1 - core)):
+        at = pl.multiple_of((bank * 2 + which) * chunk, 8)
+        dest[...] = power[pl.ds(at, chunk), :].astype(bf16)
 
 
 def previous_kernel(samples, kept, first, twist, sections, summed, even_table, odd_table):
@@ -115,7 +118,8 @@
         at = side * half
         for part in range(2):
             x = sides[side][:, part * half : (part + 1) * half]
-            summed[part, :, at : at + half] = kept[part, :, at : at + half] + alternate(x)
+            x = kept[part, :, at : at + half].astype(f32) + alternate(x)
+            summed[part, :, at : at + half] = x.astype(bf16)
 
 
 def template_kernel(templates, folded, factor):
@@ -164,66 +168,76 @@
 
 
 def filter_kernel(
-    place, mine, theirs, earlier, later, folded, factor, twist, sections, last, out,
-    weight, white, even_table, odd_table, back, *, blocks
+    mine, theirs, earlier, later, folded, factor, twist, sections, last, out,
+    weight, white, even_table, odd_table, back, result, sems, *, blocks
 ):
     half = last.shape[0]
     rows = twist.shape[1]
-    count = pl.num_programs(1)
-    block, template = pl.program_id(0), pl.program_id(1)
-
-    @pl.when((block == 0) & (template == 0))
-    def _():
-        fill_sections(even_table, sections[0], sections[1], 1)
-        fill_sections(odd_table, sections[4], sections[5], 1)
-        chunk = mine.shape[1]
-        for s in range(mine.shape[0]):
-            for pieces, core in ((mine, place[1]), (theirs, 1 - place[1])):
-                at = pl.multiple_of(((place[0] ^ s) * 2 + core) * chunk, 8)
-                total = pieces[s].astype(f32)
-                weight[pl.ds(at, chunk), :] = lax.rsqrt(total / blocks + epsilon)
-
-    def whiten(spectra):
+    count = folded.shape[0]
+    lanes = 2 * half // 128
+    fill_sections(even_table, sections[0], sections[1], 1)
+    fill_sections(odd_table, sections[4], sections[5], 1)
+    chunk = mine.shape[1]
+    bank, own = lax.axis_index("bank"), lax.rem(lax.axis_index("tm"), 2)
+    for s in range(mine.shape[0]):
+        for pieces, core in ((mine, own), (theirs, 1 - own)):
+            at = pl.multiple_of(((bank ^ s) * 2 + core) * chunk, 8)
+            total = pieces[s].astype(f32)
+            weight[pl.ds(at, chunk), :] = lax.rsqrt(total / blocks + epsilon)
+
+    def copies(block, template):
+        slot = block * count + template
+        return [
+            pltpu.make_async_copy(
+                result.at[slot, :, pl.ds(lane * 128, 128)],
+                out.at[pl.ds(block * half, half), lane * count + template, 0, :],
+                sems.at[slot],
+            )
+            for lane in range(lanes)
+        ]
+
+    for block, spectra in enumerate((earlier, later)):
         for part in range(2):
-            for lane in range(2 * half // 128):
+            for lane in range(lanes):
                 cols = slice(lane * 128, (lane + 1) * 128)
-                white[part, :, cols] = spectra[part, :, cols] * weight[lane * rows : (lane + 1) * rows, :]
-
-    @pl.when((block == 0) & (template == 0))
-    def _():
-        whiten(earlier)
-
-    @pl.when((block == 1) & (template == 0))
-    def _():
-        whiten(later)
-
-    vr, vi = white[0], white[1]
-    gr, gi = folded[0, 0].astype(f32), folded[0, 1].astype(f32)
-    pr = (gr * vr + gi * vi).astype(bf16)
-    pi = (gr * vi - gi * vr).astype(bf16)
-    even = dot(jnp.concatenate([pr[:, :half], pi[:, :half]], axis=1), even_table[...])
-    odd = dot(jnp.concatenate([pr[:, half:], pi[:, half:]], axis=1), odd_table[...])
-    er, ei, orr, oi = even[:, :half], even[:, half:], odd[:, :half], odd[:, half:]
-    for side, (ir, ii) in enumerate(((er + orr, ei + oi), (er - orr, ei - oi))):
-        cols = slice(side * half, (side + 1) * half)
-        tc, ts = twist[0, :, cols], twist[1, :, cols]
-        br = ir * tc - ii * ts
-        bi = ii * tc + ir * ts
-        back[:half, cols] = br[:half].astype(bf16)
-        back[half:, cols] = bi[:half].astype(bf16)
-        first = lax.broadcasted_iota(jnp.int32, (16, half), 0) == 0
-        back[half : half + 16, cols] = jnp.where(first, br[half : half + 1], bi[:16]).astype(bf16)
-    scale = factor[0, 0:1, :]
-    result = dot(last[...], back[...])
-    lanes = 2 * half // 128
-    for lane in range(lanes):
-        piece = result[:, lane * 128 : (lane + 1) * 128] * scale
-        out[pl.ds(lane * count + template, half, stride=lanes * count), :] = piece
+                scaled = spectra[part, :, cols].astype(f32) * weight[lane * rows : (lane + 1) * rows, :]
+                white[block, part, :, cols] = scaled.astype(bf16)
+        for template in range(count):
+            slot = block * count + template
+            vr, vi = white[block, 0], white[block, 1]
+            gr, gi = folded[template, 0], folded[template, 1]
+            pr = gr * vr + gi * vi
+            pi = gr * vi - gi * vr
+            even = dot(jnp.concatenate([pr[:, :half], pi[:, :half]], axis=1), even_table[...]).astype(bf16)
+            odd = dot(jnp.concatenate([pr[:, half:], pi[:, half:]], axis=1), odd_table[...]).astype(bf16)
+            er, ei, orr, oi = even[:, :half], even[:, half:], odd[:, :half], odd[:, half:]
+            for side, (ir, ii) in enumerate(((er + orr, ei + oi), (er - orr, ei - oi))):
+                cols = slice(side * half, (side + 1) * half)
+                tc, ts = twist[0, :, cols].astype(bf16), twist[1, :, cols].astype(bf16)
+                br = ir * tc - ii * ts
+                bi = ii * tc + ir * ts
+                back[slot, :half, cols] = br[:half]
+                back[slot, half:, cols] = bi[:half]
+                first = lax.broadcasted_iota(jnp.int32, (16, half), 0) == 0
+                middle = jnp.broadcast_to(br[half : half + 1].astype(f32), (16, half))
+                back[slot, half : half + 16, cols] = jnp.where(first, middle, bi[:16].astype(f32)).astype(bf16)
+            scale = factor[template, 0:1, 0:1]
+            result[slot] = dot(last[...], back[slot]) * scale
+            for copy in copies(block, template):
+                copy.start()
+    for block in range(2):
+        for template in range(count):
+            for copy in copies(block, template):
+                copy.wait()
 
 
 def exchange(values, axis, pairs_of):
     size = lax.axis_size(axis)
     return lax.ppermute(values, axis, [(i, pairs_of(i)) for i in range(size)])
+
+
+def near(value):
+    return pltpu.with_memory_space_constraint(value, pltpu.VMEM)
 
 
 def body(strain, lengths, templates):
@@ -232,13 +246,10 @@
     half = order // 2
     rows = half + 16
     banks, groups = lax.axis_size("bank"), lax.axis_size("tm")
-    bank, group = lax.axis_index("bank"), lax.axis_index("tm")
-    core = group % 2
-    place = jnp.stack([bank, core]).astype(jnp.int32)
+    bank = lax.axis_index("bank")
     table = tables(order)
     vmem = pl.BlockSpec(memory_space=pltpu.VMEM)
-    smem = pl.BlockSpec(memory_space=pltpu.SMEM)
-    limit = pltpu.CompilerParams(vmem_limit_bytes=60 * 1024 * 1024)
+    limit = pltpu.CompilerParams(vmem_limit_bytes=20 * 1024 * 1024)
 
     index = bank * local + jnp.arange(local, dtype=jnp.int32)
     valid = index[None, :] < lengths[:, None]
@@ -261,38 +272,35 @@
         compiler_params=limit,
         name="fold_templates",
     )(templates)
-
-    plane = jax.ShapeDtypeStruct((2, rows, order), f32)
+    *pieces, factor = lax.optimization_barrier((*pieces, factor))
+
+    plane = pltpu.VMEM((2, rows, order), bf16)
     square = pltpu.VMEM((order, order), bf16)
-    kept, later, power, last_block = pl.pallas_call(
+    chunk = rows * order // 128 // (2 * banks)
+    kept, later, mine, other, last_block = pl.pallas_call(
         functools.partial(spectrum_kernel, shards=banks),
-        in_specs=[smem] + [vmem] * (banks + 3),
-        out_specs=[vmem] * 4,
-        out_shape=[
-            plane,
-            plane,
-            jax.ShapeDtypeStruct((rows * order // 128, 128), bf16),
-            jax.ShapeDtypeStruct((half, order), bf16),
+        in_specs=[vmem] * (banks + 3),
+        out_specs=[vmem] * 5,
+        out_shape=[plane, plane]
+        + [pltpu.VMEM((chunk, 128), bf16)] * 2
+        + [pltpu.VMEM((half, order), bf16)],
+        scratch_shapes=[
+            pltpu.VMEM((blocks_here, half, order), bf16),
+            pltpu.VMEM((rows * order // 128, 128), f32),
+            square,
+            square,
         ],
-        scratch_shapes=[pltpu.VMEM((blocks_here, half, order), bf16), square, square],
         cost_estimate=pl.CostEstimate(flops=int(2e9), bytes_accessed=int(5e6), transcendentals=0),
         compiler_params=limit,
         name="spectra",
-    )(place, *pieces, table["first"], table["twist"], table["sections"])
-
-    chunk = power.shape[0] // (2 * banks)
-    own_part = lax.dynamic_index_in_dim(power.reshape(banks, 2, chunk, 128), bank, 0, False)
-    mine = lax.dynamic_index_in_dim(own_part, core, 0, False)
-    other = lax.dynamic_index_in_dim(own_part, 1 - core, 0, False)
+    )(*map(near, pieces), table["first"], table["twist"], table["sections"])
+
     partner = exchange(other, "tm", lambda i: i ^ 1)
     chip = (mine.astype(f32) + partner.astype(f32)).astype(bf16)
     share = chip.astype(f32)
     for step in range(1, groups // 2):
         share = share + exchange(chip, "tm", lambda i, s=step: i ^ (2 * s)).astype(f32)
     share = share.astype(bf16)
-    last_block, share = lax.optimization_barrier((last_block, share))
-    mine = jnp.stack([share] + [exchange(share, "bank", lambda i, s=s: i ^ s) for s in range(1, banks)])
-    theirs = exchange(mine, "tm", lambda i: i ^ 1)
 
     before = lax.ppermute(last_block, "tm", [(i, i + 1) for i in range(groups - 1)])
     earlier = pl.pallas_call(
@@ -304,32 +312,37 @@
         cost_estimate=pl.CostEstimate(flops=int(1e9), bytes_accessed=int(4e6), transcendentals=0),
         compiler_params=limit,
         name="previous",
-    )(before, kept, table["first"], table["twist"], table["sections"])
-
-    lines = count * half * order // 128
+    )(near(before), near(kept), table["first"], table["twist"], table["sections"])
+
+    shares = [share] + [exchange(share, "bank", lambda i, s=s: i ^ s) for s in range(1, banks)]
+    *shares, earlier = lax.optimization_barrier((*shares, earlier))
+    mine = jnp.stack(shares)
+    theirs = exchange(mine, "tm", lambda i: i ^ 1)
+
+    lanes = order // 128
+    pairs = blocks_here * count
     out = pl.pallas_call(
         functools.partial(filter_kernel, blocks=float(blocks_here * groups)),
-        grid=(blocks_here, count),
-        in_specs=[smem, vmem, vmem, vmem, vmem]
-        + [
-            pl.BlockSpec((1, 2, rows, order), lambda c, t: (t, 0, 0, 0)),
-            pl.BlockSpec((1, 8, 128), lambda c, t: (t, 0, 0)),
-        ]
-        + [vmem] * 3,
-        out_specs=pl.BlockSpec((lines, 128), lambda c, t: (c, 0)),
-        out_shape=jax.ShapeDtypeStruct((blocks_here * lines, 128), f32),
+        in_specs=[vmem] * 9,
+        out_specs=pl.BlockSpec(memory_space=pl.ANY),
+        out_shape=jax.ShapeDtypeStruct((blocks_here * half, lanes * count, 1, 128), f32),
         scratch_shapes=[
-            pltpu.VMEM((rows * order // 128, 128), f32),
-            pltpu.VMEM((2, rows, order), f32),
+            pltpu.VMEM((rows * lanes, 128), f32),
+            pltpu.VMEM((blocks_here, 2, rows, order), bf16),
             square,
             square,
-            square,
+            pltpu.VMEM((pairs, order, order), bf16),
+            pltpu.VMEM((pairs, half, order), f32),
+            pltpu.SemaphoreType.DMA((pairs,)),
         ],
         cost_estimate=pl.CostEstimate(flops=int(6e9), bytes_accessed=int(1.2e7), transcendentals=0),
         compiler_params=limit,
         name="filter",
-    )(place, mine, theirs, earlier, later, folded, factor, table["twist"], table["sections"], table["last"])
-    split = out.reshape(blocks_here * half * order // 128, count, 128)
+    )(
+        near(mine), near(theirs), near(earlier), near(later), near(folded), near(factor),
+        table["twist"], table["sections"], table["last"],
+    )
+    split = out.reshape(blocks_here * half * lanes, count, 128)
     return jnp.swapaxes(split, 0, 1).reshape(count, blocks_here * half * order)
 
 

time: 59.4 us -> 38.6 us (0.65)
  Pallas kernels: 26.1 us -> 12 us
  waiting for transfers between devices: 10.4 us -> 5.44 us
  other arithmetic: 2.62 us -> 1.25 us
  local copies, waits for them, and re-layouts: 3.43 us -> 2.22 us
  starting transfers between devices: 16.2 us -> 17.1 us
    pallas_call x1, Pallas kernels: 12.6 us -> 6.87 us  [body(): pl.pallas_call(functools.partial(filter_kernel, blocks=float(blocks_here...]
    ppermute x11, waiting for transfers between devices: 10.4 us -> 4.93 us  [exchange(): return lax.ppermute(values, axis, [(i, pairs_of(i)) for i in range(size)])]
    pallas_call x1, Pallas kernels: 3.77 us -> 0.82 us  [body(): pl.pallas_call(previous_kernel, in_specs=[vmem] * 5, out_specs=vmem, out_...]
    pallas_call x1, Pallas kernels: 4.34 us -> 1.49 us  [body(): pl.pallas_call(functools.partial(spectrum_kernel, shards=banks), in_specs...]
    pallas_call x1, Pallas kernels: 5.41 us -> 2.81 us  [body(): pl.pallas_call(template_kernel, grid=(count,), in_specs=[pl.BlockSpec((2,...]
    ppermute x11, starting transfers between devices: 12.3 us -> 13.3 us  [exchange(): return lax.ppermute(values, axis, [(i, pairs_of(i)) for i in range(size)])]
    squeeze x1 -> x0, local copies, waits for them, and re-layouts: 0.77 us -> none  [body(): other = lax.dynamic_index_in_dim(own_part, 1 - core, 0, False)]
    convert_element_type x1, other arithmetic: 0.77 us -> 0.01 us  [body(): chip = (mine.astype(f32) + partner.astype(f32)).astype(bf16)]
  transfers between devices with their start and end apart: 12 -> 12, of which waited for: 5 -> 6; matrix products, arithmetic and copies ran while one was open for 1% -> 0% of each run, Pallas kernels for 16% -> 10%
where the time goes in v1:
time: 38.6 us; the launch traced here: 38.1 us
  starting transfers between devices  17.1 us (44%)
  Pallas kernels  12 us (31%)
  waiting for transfers between devices  5.44 us (14%)
  local copies, waits for them, and re-layouts  2.22 us (6%)
  other arithmetic  1.25 us (3%)
    ppermute x11, starting transfers between devices, exchange(): return lax.ppermute(values, axis, [(i, pairs_of(i)) for i in range(size)])  13.3 us
    pallas_call x1, Pallas kernels, body(): pl.pallas_call(functools.partial(filter_kernel, blocks=float(blocks_here...  6.87 us
    ppermute x11, waiting for transfers between devices, exchange(): return lax.ppermute(values, axis, [(i, pairs_of(i)) for i in range(size)])  4.93 us
    ppermute x1, starting transfers between devices, body(): lax.ppermute(last_block, 'tm', [(i, i + 1) for i in range(groups - 1)])  3.8 us
    pallas_call x1, Pallas kernels, body(): pl.pallas_call(template_kernel, grid=(count,), in_specs=[pl.BlockSpec((2,...  2.81 us
    unnamed x11, local copies, waits for them, and re-layouts  2.22 us
    pallas_call x1, Pallas kernels, body(): pl.pallas_call(functools.partial(spectrum_kernel, shards=banks), in_specs...  1.49 us
    convert_element_type x1, other arithmetic, body(): jnp.where(valid, strain, 0.0).astype(bf16)  1.18 us
  transfers between devices with their start and end apart: 12, of which 6 were waited for; matrix products, arithmetic and copies ran while one was open for 0% of the time, Pallas kernels for 10%

profile of v1, /device:TPU:1, one launch (start us, length us, event | category | flops | bytes accessed | tf_op | source)
XLA Modules:
  0.0 38.1 jit_solution(14460908021461171531)
XLA Ops:
  0.0 1.2 %fusion = bf16[2,32768]{1,0:T(2,128)(2,1)S(1)} fusion(f32[2,32768]{1,0:T(2,128)} %param.7, s32[32768]{0:T(1024)S(1)} %iota_add_fusion, s32[2]{0:T(128)} %param.8), kind=kLoop, calls=%fused_computation.1 | loop fusion | flops 131072 | bytes 524296 | tf_op jit(solution)/shard_map/convert_element_type | solution.py:256
  1.2 3.0 %collective-permute-start.2 = (bf16[2,64,512]{2,1,0:T(8,128)(2,1)S(1)}, bf16[2,64,512]{2,1,0:T(8,128)(2,1)S(1)}, u32[]{:S(2)}, u32[]{:S(2)}) collective-permute-start(bf16[2,64,512]{2,1,0:T(8,128)(2,1)S(1)} %bitcast.13), channel_id=1, source_target_pairs={{0,3},{1,2},{2,1},{3,0},{4,7},{5,6},{6,5},{7,4},{8,11},{9,10},{10,... | collective-permute-start | bytes 393224 | tf_op jit(solution)/shard_map/ppermute | solution.py:236
  4.3 0.2 collective-permute-start.1
  4.5 0.1 collective-permute-start
  4.6 0.0 copy-start
  4.6 2.2 %copy-done = bf16[2,4,512,512]{3,2,1,0:T(8,128)(2,1)S(1)} copy-done((bf16[2,4,512,512]{3,2,1,0:T(8,128)(2,1)S(1)}, bf16[2,4,512,512]{3,2,1,0:T(8,128)(2,1)}, u32[]{:S(2)}) %copy-start) | copy-done | bytes 4194328
  6.8 0.0 copy-start.1
  6.8 0.0 copy-start.2
  6.8 0.0 copy-start.3
  6.8 2.8 %fold_templates.1 = (bf16[4,2,272,512]{3,2,1,0:T(8,128)(2,1)S(1)}, f32[4,8,128]{2,1,0:T(8,128)S(1)}) custom-call(bf16[2,4,512,512]{3,2,1,0:T(8,128)(2,1)S(1)} %copy-done), custom_call_target="tpu_custom_call" | custom-call | flops 6000000000 | bytes 6500000 | tf_op jit(solution)/shard_map/fold_templates/pallas_call | solution.py:259
  9.7 0.0 collective-permute-done.2.refs_3_
  9.7 1.4 %collective-permute-done.1.refs_2_ = bf16[2,64,512]{2,1,0:T(8,128)(2,1)S(1)} collective-permute-done((bf16[2,64,512]{2,1,0:T(8,128)(2,1)S(1)}, bf16[2,64,512]{2,1,0:T(8,128)(2,1)S(1)}, u32[]{:S(2)}, u32[]{:S(2)}) %collective-permute-start.1) | collective-permute-done | bytes 131104 | tf_op jit(solution)/shard_map/ppermute | solution.py:236
  11.0 0.0 collective-permute-done.refs_1_
  11.0 0.0 copy-done.1
  11.0 0.0 copy-done.2
  11.0 0.0 copy-done.3
  11.0 0.0 copy-start.4
  11.1 1.5 %spectra.1 = (bf16[2,272,512]{2,1,0:T(8,128)(2,1)S(1)}, bf16[2,272,512]{2,1,0:T(8,128)(2,1)S(1)}, bf16[136,128]{1,0:T(8,128)(2,1)S(1)}, bf16[136,128]{1,0:T(8,128)(2,1)S(1)}, bf16[256,512]{1,0:T(8,128)(2,1)S(1)}) custom-call(bf16[2,64,512]{2,1,0:T(8,128)(2,1)S(1)} %bitcast.16, bf16[2,64,512]{2,1,0:T(8,128)(2,1)S(1)} %collective-permute-done.refs_1_, ...), custom_call_target="tpu_custom_call" | custom-call | flops 2000000000 | bytes 5000000 | tf_op jit(solution)/shard_map/spectra/pallas_call | solution.py:280
  12.6 0.8 %collective-permute-start.3 = (bf16[136,128]{1,0:T(8,128)(2,1)S(1)}, bf16[136,128]{1,0:T(8,128)(2,1)S(1)}, u32[]{:S(2)}, u32[]{:S(2)}) collective-permute-start(bf16[136,128]{1,0:T(8,128)(2,1)S(1)} %get-tuple-element.28), channel_id=1, source_target_pairs={{0,4},{4,0},{8,12},{12,8},{16,20},{20,16},{24,28},{28,24},{1,5},{5... | collective-permute-start | bytes 104456 | tf_op jit(solution)/shard_map/ppermute | solution.py:236
  13.4 0.9 %collective-permute-done.3 = bf16[136,128]{1,0:T(8,128)(2,1)S(1)} collective-permute-done((bf16[136,128]{1,0:T(8,128)(2,1)S(1)}, bf16[136,128]{1,0:T(8,128)(2,1)S(1)}, u32[]{:S(2)}, u32[]{:S(2)}) %collective-permute-start.3) | collective-permute-done | bytes 34848 | tf_op jit(solution)/shard_map/ppermute | solution.py:236
  14.3 3.4 %collective-permute-start.6 = (bf16[136,128]{1,0:T(8,128)(2,1)S(1)}, bf16[136,128]{1,0:T(8,128)(2,1)S(1)}, u32[]{:S(2)}, u32[]{:S(2)}) collective-permute-start(bf16[136,128]{1,0:T(8,128)(2,1)S(1)} %add_convert_fusion.1), channel_id=1, source_target_pairs={{0,24},{4,28},{8,16},{12,20},{16,8},{20,12},{24,0},{28,4},{1,25},{... | collective-permute-start | bytes 104456 | tf_op jit(solution)/shard_map/ppermute | solution.py:236
  17.6 0.0 collective-permute-start.5
  17.6 0.4 collective-permute-start.4
  18.0 3.8 %collective-permute-start.10 = (bf16[256,512]{1,0:T(8,128)(2,1)S(1)}, bf16[256,512]{1,0:T(8,128)(2,1)S(1)}, u32[]{:S(2)}, u32[]{:S(2)}) collective-permute-start(bf16[256,512]{1,0:T(8,128)(2,1)S(1)} %get-tuple-element.29), channel_id=1, source_target_pairs={{0,4},{4,8},{8,12},{12,16},{16,20},{20,24},{24,28},{1,5},{5,9},{9,... | collective-permute-start | bytes 786440 | tf_op jit(solution)/shard_map/ppermute | solution.py:305
  21.8 0.0 collective-permute-done.6
  21.8 0.0 collective-permute-done.5
  21.8 0.0 collective-permute-done.4
  21.9 1.8 %collective-permute-start.9 = (bf16[136,128]{1,0:T(8,128)(2,1)S(1)}, bf16[136,128]{1,0:T(8,128)(2,1)S(1)}, u32[]{:S(2)}, u32[]{:S(2)}) collective-permute-start(bf16[136,128]{1,0:T(8,128)(2,1)S(1)} %add_convert_fusion), channel_id=1, source_target_pairs={{0,3},{1,2},{2,1},{3,0},{4,7},{5,6},{6,5},{7,4},{8,11},{9,10},{10,... | collective-permute-start | bytes 104456 | tf_op jit(solution)/shard_map/ppermute | solution.py:236
  23.7 0.7 %collective-permute-start.8 = (bf16[136,128]{1,0:T(8,128)(2,1)S(1)}, bf16[136,128]{1,0:T(8,128)(2,1)S(1)}, u32[]{:S(2)}, u32[]{:S(2)}) collective-permute-start(bf16[136,128]{1,0:T(8,128)(2,1)S(1)} %add_convert_fusion), channel_id=1, source_target_pairs={{0,2},{1,3},{2,0},{3,1},{4,6},{5,7},{6,4},{7,5},{8,10},{9,11},{10,... | collective-permute-start | bytes 104456 | tf_op jit(solution)/shard_map/ppermute | solution.py:236
  24.4 0.2 collective-permute-start.7
  24.6 0.5 %collective-permute-done.10.samples = bf16[256,512]{1,0:T(8,128)(2,1)S(1)} collective-permute-done((bf16[256,512]{1,0:T(8,128)(2,1)S(1)}, bf16[256,512]{1,0:T(8,128)(2,1)S(1)}, u32[]{:S(2)}, u32[]{:S(2)}) %collective-permute-start.10) | collective-permute-done | bytes 262176 | tf_op jit(solution)/shard_map/ppermute | solution.py:305
  25.1 0.8 %previous.1.earlier = bf16[2,272,512]{2,1,0:T(8,128)(2,1)S(1)} custom-call(bf16[256,512]{1,0:T(8,128)(2,1)S(1)} %collective-permute-done.10.samples, bf16[2,272,512]{2,1,0:T(8,128)(2,1)S(1)} %get-tuple-element.30.kept, bf16[544,256]{1,0:T(8,128)(2,1)S(1)} %copy-done.3, f32[2,272,512]{2,1,0:T(8,128)S(1)} %copy-done.1, bf16[6,256,256]{2,1,0:T(8,128)(2,1)S(1)} %copy-done.2), custom_call_target="tpu_custom_call" | custom-call | flops 1000000000 | bytes 4000000 | tf_op jit(solution)/shard_map/previous/pallas_call | solution.py:306
  25.9 0.0 collective-permute-done.9
  25.9 0.5 %collective-permute-done.8 = bf16[136,128]{1,0:T(8,128)(2,1)S(1)} collective-permute-done((bf16[136,128]{1,0:T(8,128)(2,1)S(1)}, bf16[136,128]{1,0:T(8,128)(2,1)S(1)}, u32[]{:S(2)}, u32[]{:S(2)}) %collective-permute-start.8) | collective-permute-done | bytes 34848 | tf_op jit(solution)/shard_map/ppermute | solution.py:236
  26.4 1.2 %collective-permute-done.7 = bf16[136,128]{1,0:T(8,128)(2,1)S(1)} collective-permute-done((bf16[136,128]{1,0:T(8,128)(2,1)S(1)}, bf16[136,128]{1,0:T(8,128)(2,1)S(1)}, u32[]{:S(2)}, u32[]{:S(2)}) %collective-permute-start.7) | collective-permute-done | bytes 34848 | tf_op jit(solution)/shard_map/ppermute | solution.py:236
  27.7 2.6 %collective-permute-start.11 = (bf16[4,136,128]{2,1,0:T(8,128)(2,1)S(1)}, bf16[4,136,128]{2,1,0:T(8,128)(2,1)S(1)}, u32[]{:S(2)}, u32[]{:S(2)}) collective-permute-start(bf16[4,136,128]{2,1,0:T(8,128)(2,1)S(1)} %pad_maximum_fusion.mine), channel_id=1, source_target_pairs={{0,4},{4,0},{8,12},{12,8},{16,20},{20,16},{24,28},{28,24},{1,5},{5... | collective-permute-start | bytes 417800 | tf_op jit(solution)/shard_map/ppermute | solution.py:236
  30.2 1.0 %collective-permute-done.11.theirs = bf16[4,136,128]{2,1,0:T(8,128)(2,1)S(1)} collective-permute-done((bf16[4,136,128]{2,1,0:T(8,128)(2,1)S(1)}, bf16[4,136,128]{2,1,0:T(8,128)(2,1)S(1)}, u32[]{:S(2)}, u32[]{:S(2)}) %collective-permute-start.11) | collective-permute-done | bytes 139296 | tf_op jit(solution)/shard_map/ppermute | solution.py:236
  31.2 0.0 copy-done.4
  31.2 6.9 %filter.1 = f32[512,16,1,128]{3,2,1,0:T(1,128)} custom-call(bf16[4,136,128]{2,1,0:T(8,128)(2,1)S(1)} %pad_maximum_fusion.mine, bf16[4,136,128]{2,1,0:T(8,128)(2,1)S(1)} %collective-permute-done.11.theirs, bf16[2,272,512]{2,1,0:T(8,128)(2,1)S(1)} %previous.1.earlier, bf16[2,272,512]{2,1,0:T(8,128)(2,1)S(1)} %get-tuple-element.36.later, ...), custom_call_target="tpu_custom_call" | custom-call | flops 6000000000 | bytes 12000000 | tf_op jit(solution)/shard_map/filter/pallas_call | solution.py:324
  (5 shorter events, 0.1 us)
Async XLA Ops:
  1.2 8.4 %collective-permute-start.2 = (bf16[2,64,512]{2,1,0:T(8,128)(2,1)S(1)}, bf16[2,64,512]{2,1,0:T(8,128)(2,1)S(1)}, u32[]{:S(2)}, u32[]{:S(2)}) collective-permute-start(bf16[2,64,512]{2,1,0:T(8,128)(2,1)S(1)} %bitcast.13), channel_id=1, source_target_pairs={{0,3},{1,2},{2,1},{3,0},{4,7},{5,6},{6,5},{7,4},{8,11},{9,10},{10,... | collective-permute-start | bytes 393224 | tf_op jit(solution)/shard_map/ppermute | solution.py:236
  4.3 6.7 %collective-permute-start.1 = (bf16[2,64,512]{2,1,0:T(8,128)(2,1)S(1)}, bf16[2,64,512]{2,1,0:T(8,128)(2,1)S(1)}, u32[]{:S(2)}, u32[]{:S(2)}) collective-permute-start(bf16[2,64,512]{2,1,0:T(8,128)(2,1)S(1)} %bitcast.14), channel_id=1, source_target_pairs={{0,2},{1,3},{2,0},{3,1},{4,6},{5,7},{6,4},{7,5},{8,10},{9,11},{10,... | collective-permute-start | bytes 393224 | tf_op jit(solution)/shard_map/ppermute | solution.py:236
  4.5 6.5 %collective-permute-start = (bf16[2,64,512]{2,1,0:T(8,128)(2,1)S(1)}, bf16[2,64,512]{2,1,0:T(8,128)(2,1)S(1)}, u32[]{:S(2)}, u32[]{:S(2)}) collective-permute-start(bf16[2,64,512]{2,1,0:T(8,128)(2,1)S(1)} %bitcast.15), channel_id=1, source_target_pairs={{0,1},{1,0},{2,3},{3,2},{4,5},{5,4},{6,7},{7,6},{8,9},{9,8},{10,11... | collective-permute-start | bytes 393224 | tf_op jit(solution)/shard_map/ppermute | solution.py:236
  4.6 2.2 %copy-start = (bf16[2,4,512,512]{3,2,1,0:T(8,128)(2,1)S(1)}, bf16[2,4,512,512]{3,2,1,0:T(8,128)(2,1)}, u32[]{:S(2)}) copy-start(bf16[2,4,512,512]{3,2,1,0:T(8,128)(2,1)} %templates.1) | copy-start | bytes 12582916
  6.8 4.2 %copy-start.1 = (f32[2,272,512]{2,1,0:T(8,128)S(1)}, f32[2,272,512]{2,1,0:T(8,128)}, u32[]{:S(2)}) copy-start(f32[2,272,512]{2,1,0:T(8,128)} %constant.17.clone.refs_5_.twist) | copy-start | bytes 3342340
  6.8 4.2 %copy-start.2 = (bf16[6,256,256]{2,1,0:T(8,128)(2,1)S(1)}, bf16[6,256,256]{2,1,0:T(8,128)(2,1)}, u32[]{:S(2)}) copy-start(bf16[6,256,256]{2,1,0:T(8,128)(2,1)} %constant.18.clone.refs_6_.sections) | copy-start | bytes 2359300
  6.8 4.2 %copy-start.3 = (bf16[544,256]{1,0:T(8,128)(2,1)S(1)}, bf16[544,256]{1,0:T(8,128)(2,1)}, u32[]{:S(2)}) copy-start(bf16[544,256]{1,0:T(8,128)(2,1)} %constant.16.clone.refs_4_.first) | copy-start | bytes 835588
  11.0 20.2 %copy-start.4 = (bf16[256,512]{1,0:T(8,128)(2,1)S(1)}, bf16[256,512]{1,0:T(8,128)(2,1)}, u32[]{:S(2)}) copy-start(bf16[256,512]{1,0:T(8,128)(2,1)} %constant.19.clone.last) | copy-start | bytes 786436
  12.6 1.7 %collective-permute-start.3 = (bf16[136,128]{1,0:T(8,128)(2,1)S(1)}, bf16[136,128]{1,0:T(8,128)(2,1)S(1)}, u32[]{:S(2)}, u32[]{:S(2)}) collective-permute-start(bf16[136,128]{1,0:T(8,128)(2,1)S(1)} %get-tuple-element.28), channel_id=1, source_target_pairs={{0,4},{4,0},{8,12},{12,8},{16,20},{20,16},{24,28},{28,24},{1,5},{5... | collective-permute-start | bytes 104456 | tf_op jit(solution)/shard_map/ppermute | solution.py:236
  14.3 7.6 %collective-permute-start.6 = (bf16[136,128]{1,0:T(8,128)(2,1)S(1)}, bf16[136,128]{1,0:T(8,128)(2,1)S(1)}, u32[]{:S(2)}, u32[]{:S(2)}) collective-permute-start(bf16[136,128]{1,0:T(8,128)(2,1)S(1)} %add_convert_fusion.1), channel_id=1, source_target_pairs={{0,24},{4,28},{8,16},{12,20},{16,8},{20,12},{24,0},{28,4},{1,25},{... | collective-permute-start | bytes 104456 | tf_op jit(solution)/shard_map/ppermute | solution.py:236
  17.6 4.2 %collective-permute-start.5 = (bf16[136,128]{1,0:T(8,128)(2,1)S(1)}, bf16[136,128]{1,0:T(8,128)(2,1)S(1)}, u32[]{:S(2)}, u32[]{:S(2)}) collective-permute-start(bf16[136,128]{1,0:T(8,128)(2,1)S(1)} %add_convert_fusion.1), channel_id=1, source_target_pairs={{0,16},{4,20},{8,24},{12,28},{16,0},{20,4},{24,8},{28,12},{1,17},{... | collective-permute-start | bytes 104456 | tf_op jit(solution)/shard_map/ppermute | solution.py:236
  17.6 4.2 %collective-permute-start.4 = (bf16[136,128]{1,0:T(8,128)(2,1)S(1)}, bf16[136,128]{1,0:T(8,128)(2,1)S(1)}, u32[]{:S(2)}, u32[]{:S(2)}) collective-permute-start(bf16[136,128]{1,0:T(8,128)(2,1)S(1)} %add_convert_fusion.1), channel_id=1, source_target_pairs={{0,8},{4,12},{8,0},{12,4},{16,24},{20,28},{24,16},{28,20},{1,9},{5... | collective-permute-start | bytes 104456 | tf_op jit(solution)/shard_map/ppermute | solution.py:236
  18.0 7.1 %collective-permute-start.10 = (bf16[256,512]{1,0:T(8,128)(2,1)S(1)}, bf16[256,512]{1,0:T(8,128)(2,1)S(1)}, u32[]{:S(2)}, u32[]{:S(2)}) collective-permute-start(bf16[256,512]{1,0:T(8,128)(2,1)S(1)} %get-tuple-element.29), channel_id=1, source_target_pairs={{0,4},{4,8},{8,12},{12,16},{16,20},{20,24},{24,28},{1,5},{5,9},{9,... | collective-permute-start | bytes 786440 | tf_op jit(solution)/shard_map/ppermute | solution.py:305
  21.9 4.1 %collective-permute-start.9 = (bf16[136,128]{1,0:T(8,128)(2,1)S(1)}, bf16[136,128]{1,0:T(8,128)(2,1)S(1)}, u32[]{:S(2)}, u32[]{:S(2)}) collective-permute-start(bf16[136,128]{1,0:T(8,128)(2,1)S(1)} %add_convert_fusion), channel_id=1, source_target_pairs={{0,3},{1,2},{2,1},{3,0},{4,7},{5,6},{6,5},{7,4},{8,11},{9,10},{10,... | collective-permute-start | bytes 104456 | tf_op jit(solution)/shard_map/ppermute | solution.py:236
  23.7 2.8 %collective-permute-start.8 = (bf16[136,128]{1,0:T(8,128)(2,1)S(1)}, bf16[136,128]{1,0:T(8,128)(2,1)S(1)}, u32[]{:S(2)}, u32[]{:S(2)}) collective-permute-start(bf16[136,128]{1,0:T(8,128)(2,1)S(1)} %add_convert_fusion), channel_id=1, source_target_pairs={{0,2},{1,3},{2,0},{3,1},{4,6},{5,7},{6,4},{7,5},{8,10},{9,11},{10,... | collective-permute-start | bytes 104456 | tf_op jit(solution)/shard_map/ppermute | solution.py:236
  24.4 3.3 %collective-permute-start.7 = (bf16[136,128]{1,0:T(8,128)(2,1)S(1)}, bf16[136,128]{1,0:T(8,128)(2,1)S(1)}, u32[]{:S(2)}, u32[]{:S(2)}) collective-permute-start(bf16[136,128]{1,0:T(8,128)(2,1)S(1)} %add_convert_fusion), channel_id=1, source_target_pairs={{0,1},{1,0},{2,3},{3,2},{4,5},{5,4},{6,7},{7,6},{8,9},{9,8},{10,11... | collective-permute-start | bytes 104456 | tf_op jit(solution)/shard_map/ppermute | solution.py:236
  27.7 3.6 %collective-permute-start.11 = (bf16[4,136,128]{2,1,0:T(8,128)(2,1)S(1)}, bf16[4,136,128]{2,1,0:T(8,128)(2,1)S(1)}, u32[]{:S(2)}, u32[]{:S(2)}) collective-permute-start(bf16[4,136,128]{2,1,0:T(8,128)(2,1)S(1)} %pad_maximum_fusion.mine), channel_id=1, source_target_pairs={{0,4},{4,0},{8,12},{12,8},{16,20},{20,16},{24,28},{28,24},{1,5},{5... | collective-permute-start | bytes 417800 | tf_op jit(solution)/shard_map/ppermute | solution.py:236

commit v2 on v1

v2 whole, which is shorter than its diff:
```python
import functools
import math

import jax
import jax.numpy as jnp
import numpy as np
from jax import lax
from jax.experimental import pallas as pl
from jax.experimental.pallas import tpu as pltpu
from jax.sharding import PartitionSpec as P

epsilon = 1e-06
bf16 = jnp.bfloat16
f32 = jnp.float32
group_order = (0, 2, 1, 3)


def dot(a, b):
    return jnp.dot(a, b, preferred_element_type=f32)


def tables(order):
    half, group = order // 2, order // 4
    rows = half + 16
    a = np.concatenate([np.arange(group), half - np.arange(group), [group], np.zeros(15, np.int64)])
    keep = (np.arange(rows) <= half)[:, None]
    turn = 2.0 * math.pi / order

    def angle(left, right):
        return turn * ((left[:, None] * right[None, :]) % order)

    u, v, g = np.arange(half), np.arange(order), np.arange(group)
    first = np.concatenate([np.cos(angle(a, u)) * keep, -np.sin(angle(a, u)) * keep])
    twist = (2.0 * math.pi / order**2) * (a[:, None] * v[None, :])
    forward, inverse = [], []
    for q in range(4):
        c, s = np.cos(angle(g, 4 * g + q)), np.sin(angle(g, 4 * g + q))
        forward.append(np.block([[c, -s], [s, c]]))
        inverse.append(np.block([[c.T, s.T], [-s.T, c.T]]))
    last = []
    for parity in range(2):
        w = 2 * g + parity
        c, s = np.cos(angle(w, g)), -np.sin(angle(w, g))
        c[:, 0] = 0.5
        s[:, 0] = (1.0 - 2.0 * parity) * (1.0 - 2.0 * (g % 2))
        last.append(np.concatenate([c, s], axis=1))
    return dict(
        first=first.astype(bf16),
        twist=np.stack([np.cos(twist), np.sin(twist)]).astype(np.float32),
        forward=np.stack(forward).astype(bf16),
        inverse=np.stack(inverse).astype(bf16),
        last=np.stack(last).astype(bf16),
    )


def quarters(value):
    group = value.shape[1] // 4
    return [value[:, q * group : (q + 1) * group] for q in range(4)]


def spectrum(samples, first, twist, forward):
    rows = first.shape[0] // 2
    out = dot(first[...], samples)
    real, imag = out[:rows], out[rows:]
    tc, ts = twist[0], twist[1]
    r = quarters(real * tc + imag * ts)
    i = quarters(imag * tc - real * ts)
    ar, ai, br, bi = r[0] + r[2], i[0] + i[2], r[1] + r[3], i[1] + i[3]
    cr, ci, dr, di = r[0] - r[2], i[0] - i[2], r[1] - r[3], i[1] - i[3]
    parts = [(ar + br, ai + bi), (cr + di, ci - dr), (ar - br, ai - bi), (cr - di, ci + dr)]
    return [
        dot(jnp.concatenate(part, axis=1).astype(bf16), forward[q]) for q, part in enumerate(parts)
    ]


def alternate(values):
    row = lax.broadcasted_iota(jnp.int32, values.shape, 0)
    return jnp.where(row % 2 == 0, values, -values)


def spectrum_kernel(*refs, shards):
    pieces = refs[:shards]
    first, twist, forward = refs[shards : shards + 3]
    kept, summed, mine, other, last_block, samples, power = refs[shards + 3 :]
    rows = first.shape[0] // 2
    group = forward.shape[1] // 2
    piece_rows = pieces[0].shape[1]
    bank, core = lax.axis_index("bank"), lax.rem(lax.axis_index("tm"), 2)
    for s in range(shards):
        at = pl.multiple_of((bank ^ s) * piece_rows, piece_rows)
        samples[:, pl.ds(at, piece_rows), :] = pieces[s][...]
    last_block[...] = samples[1]
    ones = spectrum(samples[0], first, twist, forward)
    twos = spectrum(samples[1], first, twist, forward)
    for place, q in enumerate(group_order):
        one, two = ones[q], twos[q]
        cols = slice(place * group, (place + 1) * group)
        for part in range(2):
            x0 = one[:, part * group : (part + 1) * group]
            x1 = two[:, part * group : (part + 1) * group]
            kept[part, :, cols] = x0.astype(bf16)
            summed[part, :, cols] = (x1 + alternate(x0)).astype(bf16)
        total = one * one + two * two
        total = total[:, :group] + total[:, group:]
        lanes = group // 128
        for lane in range(lanes):
            row = (place * lanes + lane) * rows
            power[row : row + rows, :] = total[:, lane * 128 : (lane + 1) * 128]
    chunk = mine.shape[0]
    for dest, which in ((mine, core), (other, 1 - core)):
        at = pl.multiple_of((bank * 2 + which) * chunk, 8)
        dest[...] = power[pl.ds(at, chunk), :].astype(bf16)


def previous_kernel(samples, kept, first, twist, forward, summed):
    group = forward.shape[1] // 2
    parts = spectrum(samples[...], first, twist, forward)
    for place, q in enumerate(group_order):
        x = parts[q]
        cols = slice(place * group, (place + 1) * group)
        for part in range(2):
            added = alternate(x[:, part * group : (part + 1) * group])
            summed[part, :, cols] = (kept[part, :, cols].astype(f32) + added).astype(bf16)


def template_kernel(templates, folded, factor, select):
    order = templates.shape[-1]
    half, group = order // 2, order // 4

    @pl.when(pl.program_id(0) == 0)
    def _():
        m = lax.broadcasted_iota(jnp.int32, (order, order), 0)
        n = lax.broadcasted_iota(jnp.int32, (order, order), 1)
        place = n // group
        source = 4 * (n % group) + jnp.where((place == 1) | (place == 2), 3 - place, place)
        select[:order] = jnp.where(m == source, 1.0, 0.0).astype(bf16)
        select[order:] = jnp.where(m == order - 1 - source, 1.0, 0.0).astype(bf16)

    i = lax.broadcasted_iota(jnp.int32, (group, group), 0)
    r = lax.broadcasted_iota(jnp.int32, (group, group), 1)
    flip = jnp.where(r == group - i, 1.0, 0.0).astype(bf16)
    start = lax.broadcasted_iota(jnp.int32, (group, order), 0) == 0
    energy = jnp.zeros((8, order), f32)
    for part in range(2):
        whole = templates[part, 0]
        wide = whole.astype(f32)
        energy = energy + jnp.sum((wide * wide).reshape(order // 8, 8, order), axis=0)

        def flipped(at, head):
            return jnp.where(start, head, dot(flip, whole[at : at + group])).astype(bf16)

        turned = pltpu.roll(wide[:8], order - 1, 1)[:1]
        upper = [whole[:group], flipped(group, wide[half : half + 1]), whole[group : group + 16]]
        lower = [flipped(half + group, turned), whole[half : half + group], whole[half + group : half + group + 16]]
        lower = jnp.concatenate(lower)
        if part == 1:
            lower = -lower
        both = jnp.concatenate([jnp.concatenate(upper), lower], axis=1)
        for k in range(0, order, half):
            folded[0, part, :, k : k + half] = dot(both, select[:, k : k + half]).astype(bf16)
    total = jnp.sum(jnp.sum(energy, axis=1, keepdims=True), axis=0, keepdims=True)
    factor[0] = jnp.broadcast_to(lax.rsqrt(total), factor.shape[1:])


def filter_scratch(blocks, count, rows, order):
    half, pairs = order // 2, blocks * count
    return [
        pltpu.VMEM((rows * order // 128, 128), f32),
        pltpu.VMEM((blocks, 2, rows, order), bf16),
        pltpu.VMEM((2, rows, order), bf16),
        pltpu.VMEM((2, 4, rows, half), bf16),
        pltpu.VMEM((2, 2, 2, half, half), bf16),
        pltpu.VMEM((pairs, 2, half // 2, order), f32),
        pltpu.SemaphoreType.DMA((pairs,)),
    ]


def filter_kernel(
    mine, theirs, earlier, later, folded, factor, twist, inverse, last, out,
    weight, white, turn, sums, back, result, sems, *, blocks
):
    group = last.shape[1]
    half, order = 2 * group, 4 * group
    rows = twist.shape[1]
    count = folded.shape[0]
    lanes = order // 128
    chunk = mine.shape[1]
    bank, own = lax.axis_index("bank"), lax.rem(lax.axis_index("tm"), 2)
    for s in range(mine.shape[0]):
        for pieces, core in ((mine, own), (theirs, 1 - own)):
            at = pl.multiple_of(((bank ^ s) * 2 + core) * chunk, 8)
            total = pieces[s].astype(f32)
            weight[pl.ds(at, chunk), :] = lax.rsqrt(total / blocks + epsilon)
    turn[...] = twist[...].astype(bf16)

    def copies(slot):
        block, template = divmod(slot, count)
        return [
            pltpu.make_async_copy(
                result.at[slot, parity, :, pl.ds(lane * 128, 128)],
                out.at[pl.ds(block * group, group), parity, lane * count + template, 0, :],
                sems.at[slot],
            )
            for parity in range(2)
            for lane in range(lanes)
        ]

    def whiten(block, side):
        spectra = (earlier, later)[block]
        cols = slice(side * half, (side + 1) * half)
        tiles = range(side * half // 128, (side + 1) * half // 128)
        scale = jnp.concatenate([weight[t * rows : (t + 1) * rows, :] for t in tiles], axis=1)
        for part in range(2):
            white[block, part, :, cols] = (spectra[part, :, cols].astype(f32) * scale).astype(bf16)

    def products(slot, side):
        block, template = divmod(slot, count)
        if template == 0:
            whiten(block, side)
        cols = slice(side * half, (side + 1) * half)
        vr, vi = white[block, 0, :, cols], white[block, 1, :, cols]
        gr, gi = folded[template, 0, :, cols], folded[template, 1, :, cols]
        pr = gr * vr + gi * vi
        pi = gr * vi - gi * vr
        one, two = (
            dot(jnp.concatenate([pr[:, here], pi[:, here]], axis=1), inverse[group_order[2 * side + k]])
            for k, here in enumerate((slice(0, group), slice(group, half)))
        )
        plus, minus = one + two, one - two
        if side == 0:
            real, imag = (plus[:, :group], minus[:, :group]), (plus[:, group:], minus[:, group:])
        else:
            real, imag = (plus[:, :group], two[:, group:] - one[:, group:]), (plus[:, group:], minus[:, :group])
        sums[slot % 2, 2 * side] = jnp.concatenate(real, axis=1).astype(bf16)
        sums[slot % 2, 2 * side + 1] = jnp.concatenate(imag, axis=1).astype(bf16)

    def turned(slot, at, size):
        here = slice(at, at + size)
        r0, i0, r1, i1 = (sums[slot % 2, plane, here] for plane in range(4))
        values = []
        for side, (ir, ii) in enumerate(((r0 + r1, i0 + i1), (r0 - r1, i0 - i1))):
            cols = slice(side * half, (side + 1) * half)
            tc, ts = turn[0, here, cols], turn[1, here, cols]
            values.append((ir * tc - ii * ts, ii * tc + ir * ts))
        return values

    def twists(slot, part, parts):
        step = 16
        first = lax.broadcasted_iota(jnp.int32, (step, half), 0) == 0
        span = group // parts
        for at in range(part * span, (part + 1) * span, step):
            near_rows, far_rows = turned(slot, at, step), turned(slot, group + at, step)
            middle = turned(slot, half, step) if at == 0 else None
            for side in range(2):
                (r0, i0), (r1, i1) = near_rows[side], far_rows[side]
                for parity in range(2):
                    re, im = (r0 + r1, i0 - i1) if parity == 0 else (r0 - r1, i0 + i1)
                    if at == 0:
                        row = middle[side][parity][:1].astype(f32)
                        im = jnp.where(first, jnp.broadcast_to(row, im.shape), im.astype(f32)).astype(bf16)
                    back[slot % 2, parity, side, at : at + step] = re
                    back[slot % 2, parity, side, group + at : group + at + step] = im

    def finish(slot, parity, side):
        scale = factor[slot % count, 0:1, 0:1]
        value = dot(last[parity], back[slot % 2, parity, side])
        result[slot, parity, :, side * half : (side + 1) * half] = value * scale

    total = 2 * count
    for step in range(total + 2):
        for j in range(2):
            if step < total:
                products(step, j)
            if 0 <= step - 2:
                finish(step - 2, j, 0)
                finish(step - 2, j, 1)
            if 0 <= step - 1 < total:
                twists(step - 1, j, 2)
        if 0 <= step - 2:
            for copy in copies(step - 2):
                copy.start()
    for slot in range(total):
        for copy in copies(slot):
            copy.wait()


def exchange(values, axis, pairs_of):
    size = lax.axis_size(axis)
    return lax.ppermute(values, axis, [(i, pairs_of(i)) for i in range(size)])


def near(value):
    return pltpu.with_memory_space_constraint(value, pltpu.VMEM)


def body(strain, lengths, templates):
    blocks_here, local = strain.shape
    count, order = templates.shape[1], templates.shape[-1]
    half = order // 2
    rows = half + 16
    banks, groups = lax.axis_size("bank"), lax.axis_size("tm")
    bank = lax.axis_index("bank")
    table = tables(order)
    vmem = pl.BlockSpec(memory_space=pltpu.VMEM)
    limit = pltpu.CompilerParams(vmem_limit_bytes=20 * 1024 * 1024)

    index = bank * local + jnp.arange(local, dtype=jnp.int32)
    valid = index[None, :] < lengths[:, None]
    gated = jnp.where(valid, strain, 0.0).astype(bf16).reshape(blocks_here, local // order, order)
    pieces = [gated] + [exchange(gated, "bank", lambda i, s=s: i ^ s) for s in range(1, banks)]

    folded, factor = pl.pallas_call(
        template_kernel,
        grid=(count,),
        in_specs=[pl.BlockSpec((2, 1, order, order), lambda t: (0, t, 0, 0))],
        out_specs=[
            pl.BlockSpec((1, 2, rows, order), lambda t: (t, 0, 0, 0)),
            pl.BlockSpec((1, 8, 128), lambda t: (t, 0, 0)),
        ],
        out_shape=[
            jax.ShapeDtypeStruct((count, 2, rows, order), bf16),
            jax.ShapeDtypeStruct((count, 8, 128), f32),
        ],
        scratch_shapes=[pltpu.VMEM((2 * order, order), bf16)],
        cost_estimate=pl.CostEstimate(flops=int(6e9), bytes_accessed=int(6.5e6), transcendentals=0),
        compiler_params=limit,
        name="fold_templates",
    )(pltpu.with_memory_space_constraint(templates, pltpu.HBM))
    *pieces, factor = lax.optimization_barrier((*pieces, factor))

    plane = pltpu.VMEM((2, rows, order), bf16)
    chunk = rows * order // 128 // (2 * banks)
    kept, later, mine, other, last_block = pl.pallas_call(
        functools.partial(spectrum_kernel, shards=banks),
        in_specs=[vmem] * (banks + 3),
        out_specs=[vmem] * 5,
        out_shape=[plane, plane]
        + [pltpu.VMEM((chunk, 128), bf16)] * 2
        + [pltpu.VMEM((half, order), bf16)],
        scratch_shapes=[
            pltpu.VMEM((blocks_here, half, order), bf16),
            pltpu.VMEM((rows * order // 128, 128), f32),
        ],
        cost_estimate=pl.CostEstimate(flops=int(2e9), bytes_accessed=int(5e6), transcendentals=0),
        compiler_params=limit,
        name="spectra",
    )(*map(near, pieces), table["first"], table["twist"], table["forward"])

    partner = exchange(other, "tm", lambda i: i ^ 1)
    chip = (mine.astype(f32) + partner.astype(f32)).astype(bf16)
    share = chip.astype(f32)
    for step in range(1, groups // 2):
        share = share + exchange(chip, "tm", lambda i, s=step: i ^ (2 * s)).astype(f32)
    share = share.astype(bf16)

    before = lax.ppermute(last_block, "tm", [(i, i + 1) for i in range(groups - 1)])
    earlier = pl.pallas_call(
        previous_kernel,
        in_specs=[vmem] * 5,
        out_specs=vmem,
        out_shape=plane,
        cost_estimate=pl.CostEstimate(flops=int(1e9), bytes_accessed=int(4e6), transcendentals=0),
        compiler_params=limit,
        name="previous",
    )(near(before), near(kept), table["first"], table["twist"], table["forward"])

    shares = [share] + [exchange(share, "bank", lambda i, s=s: i ^ s) for s in range(1, banks)]
    *shares, earlier = lax.optimization_barrier((*shares, earlier))
    mine = jnp.stack(shares)
    theirs = exchange(mine, "tm", lambda i: i ^ 1)

    lanes = order // 128
    out = pl.pallas_call(
        functools.partial(filter_kernel, blocks=float(blocks_here * groups)),
        in_specs=[vmem] * 9,
        out_specs=pl.BlockSpec(memory_space=pl.ANY),
        out_shape=jax.ShapeDtypeStruct((blocks_here * half // 2, 2, lanes * count, 1, 128), f32),
        scratch_shapes=filter_scratch(blocks_here, count, rows, order),
        cost_estimate=pl.CostEstimate(flops=int(6e9), bytes_accessed=int(1.2e7), transcendentals=0),
        compiler_params=limit,
        name="filter",
    )(
        near(mine), near(theirs), near(earlier), near(later), near(folded), near(factor),
        table["twist"], table["inverse"], table["last"],
    )
    split = out.reshape(blocks_here * half * lanes, count, 128)
    return jnp.swapaxes(split, 0, 1).reshape(count, blocks_here * half * order)


def solution(mesh):
    in_specs = (P("tm", "bank"), P("tm"), P(None, "bank", None, None))
    out_specs = P("bank", "tm")
    return jax.shard_map(body, mesh=mesh, in_specs=in_specs, out_specs=out_specs, check_vma=False)
```

time: 38.6 us -> 36.8 us (0.953)
  local copies, waits for them, and re-layouts: 2.22 us -> 0.05 us
  Pallas kernels: 12 us -> 12.7 us
  waiting for transfers between devices: 5.44 us -> 4.89 us
    pallas_call x1, Pallas kernels: 2.81 us -> 5.51 us  [body(): pl.pallas_call(template_kernel, grid=(count,), in_specs=[pl.BlockSpec((2,...]
    unnamed x11, local copies, waits for them, and re-layouts: 2.22 us -> 0.05 us
    pallas_call x1, Pallas kernels: 6.87 us -> 5.03 us  [body(): pl.pallas_call(functools.partial(filter_kernel, blocks=float(blocks_here...]
    ppermute x11, waiting for transfers between devices: 4.93 us -> 4.37 us  [exchange(): return lax.ppermute(values, axis, [(i, pairs_of(i)) for i in range(size)])]
  transfers between devices with their start and end apart: 12 -> 12, of which waited for: 6 -> 6; matrix products, arithmetic and copies ran while one was open for 0% -> 0% of each run, Pallas kernels for 10% -> 17%
where the time goes in v2:
time: 36.8 us; the launch traced here: 36.2 us
  starting transfers between devices  17.2 us (47%)
  Pallas kernels  12.7 us (35%)
  waiting for transfers between devices  4.89 us (13%)
  other arithmetic  1.25 us (3%)
    ppermute x11, starting transfers between devices, exchange(): return lax.ppermute(values, axis, [(i, pairs_of(i)) for i in range(size)])  13.4 us
    pallas_call x1, Pallas kernels, body(): pl.pallas_call(template_kernel, grid=(count,), in_specs=[pl.BlockSpec((2,...  5.51 us
    pallas_call x1, Pallas kernels, body(): pl.pallas_call(functools.partial(filter_kernel, blocks=float(blocks_here...  5.03 us
    ppermute x11, waiting for transfers between devices, exchange(): return lax.ppermute(values, axis, [(i, pairs_of(i)) for i in range(size)])  4.37 us
    ppermute x1, starting transfers between devices, body(): lax.ppermute(last_block, 'tm', [(i, i + 1) for i in range(groups - 1)])  3.8 us
    pallas_call x1, Pallas kernels, body(): pl.pallas_call(functools.partial(spectrum_kernel, shards=banks), in_specs...  1.42 us
    convert_element_type x1, other arithmetic, body(): jnp.where(valid, strain, 0.0).astype(bf16)  1.18 us
  transfers between devices with their start and end apart: 12, of which 6 were waited for; matrix products, arithmetic and copies ran while one was open for 0% of the time, Pallas kernels for 17%

profile of v2, /device:TPU:1, one launch (start us, length us, event | category | flops | bytes accessed | tf_op | source)
XLA Modules:
  0.0 36.2 jit_solution(8895215083207966666)
XLA Ops:
  0.0 1.2 %fusion = bf16[2,32768]{1,0:T(2,128)(2,1)S(1)} fusion(f32[2,32768]{1,0:T(2,128)} %param.8, s32[32768]{0:T(1024)S(1)} %iota_add_fusion, s32[2]{0:T(128)} %param.9), kind=kLoop, calls=%fused_computation.1 | loop fusion | flops 131072 | bytes 524296 | tf_op jit(solution)/shard_map/convert_element_type | solution.py:309
  1.2 0.0 copy-start
  1.2 0.0 copy-start.2
  1.3 0.0 copy-start.3
  1.3 3.0 %collective-permute-start.2 = (bf16[2,64,512]{2,1,0:T(8,128)(2,1)S(1)}, bf16[2,64,512]{2,1,0:T(8,128)(2,1)S(1)}, u32[]{:S(2)}, u32[]{:S(2)}) collective-permute-start(bf16[2,64,512]{2,1,0:T(8,128)(2,1)S(1)} %bitcast.13), channel_id=1, source_target_pairs={{0,3},{1,2},{2,1},{3,0},{4,7},{5,6},{6,5},{7,4},{8,11},{9,10},{10,... | collective-permute-start | bytes 393224 | tf_op jit(solution)/shard_map/ppermute | solution.py:289
  4.3 0.2 collective-permute-start.1
  4.5 0.1 collective-permute-start
  4.7 5.5 %fold_templates.1 = (bf16[4,2,272,512]{3,2,1,0:T(8,128)(2,1)S(1)}, f32[4,8,128]{2,1,0:T(8,128)S(1)}) custom-call(bf16[2,4,512,512]{3,2,1,0:T(8,128)(2,1)} %templates.1), custom_call_target="tpu_custom_call" | custom-call | flops 6000000000 | bytes 6500000 | tf_op jit(solution)/shard_map/fold_templates/pallas_call | solution.py:312
  10.2 0.0 collective-permute-done.2.refs_3_
  10.2 0.9 %collective-permute-done.1.refs_2_ = bf16[2,64,512]{2,1,0:T(8,128)(2,1)S(1)} collective-permute-done((bf16[2,64,512]{2,1,0:T(8,128)(2,1)S(1)}, bf16[2,64,512]{2,1,0:T(8,128)(2,1)S(1)}, u32[]{:S(2)}, u32[]{:S(2)}) %collective-permute-start.1) | collective-permute-done | bytes 131104 | tf_op jit(solution)/shard_map/ppermute | solution.py:289
  11.1 0.0 collective-permute-done.refs_1_
  11.1 0.0 copy-done
  11.1 0.0 copy-done.2
  11.1 0.0 copy-done.3
  11.1 0.0 copy-start.1
  11.1 0.0 copy-start.4
  11.1 1.4 %spectra.1 = (bf16[2,272,512]{2,1,0:T(8,128)(2,1)S(1)}, bf16[2,272,512]{2,1,0:T(8,128)(2,1)S(1)}, bf16[136,128]{1,0:T(8,128)(2,1)S(1)}, bf16[136,128]{1,0:T(8,128)(2,1)S(1)}, bf16[256,512]{1,0:T(8,128)(2,1)S(1)}) custom-call(bf16[2,64,512]{2,1,0:T(8,128)(2,1)S(1)} %bitcast.16, bf16[2,64,512]{2,1,0:T(8,128)(2,1)S(1)} %collective-permute-done.refs_1_, ...), custom_call_target="tpu_custom_call" | custom-call | flops 2000000000 | bytes 5000000 | tf_op jit(solution)/shard_map/spectra/pallas_call | solution.py:333
  12.5 0.8 %collective-permute-start.3 = (bf16[136,128]{1,0:T(8,128)(2,1)S(1)}, bf16[136,128]{1,0:T(8,128)(2,1)S(1)}, u32[]{:S(2)}, u32[]{:S(2)}) collective-permute-start(bf16[136,128]{1,0:T(8,128)(2,1)S(1)} %get-tuple-element.28), channel_id=1, source_target_pairs={{0,4},{4,0},{8,12},{12,8},{16,20},{20,16},{24,28},{28,24},{1,5},{5... | collective-permute-start | bytes 104456 | tf_op jit(solution)/shard_map/ppermute | solution.py:289
  13.4 0.9 %collective-permute-done.3 = bf16[136,128]{1,0:T(8,128)(2,1)S(1)} collective-permute-done((bf16[136,128]{1,0:T(8,128)(2,1)S(1)}, bf16[136,128]{1,0:T(8,128)(2,1)S(1)}, u32[]{:S(2)}, u32[]{:S(2)}) %collective-permute-start.3) | collective-permute-done | bytes 34848 | tf_op jit(solution)/shard_map/ppermute | solution.py:289
  14.2 3.4 %collective-permute-start.6 = (bf16[136,128]{1,0:T(8,128)(2,1)S(1)}, bf16[136,128]{1,0:T(8,128)(2,1)S(1)}, u32[]{:S(2)}, u32[]{:S(2)}) collective-permute-start(bf16[136,128]{1,0:T(8,128)(2,1)S(1)} %add_convert_fusion.1), channel_id=1, source_target_pairs={{0,24},{4,28},{8,16},{12,20},{16,8},{20,12},{24,0},{28,4},{1,25},{... | collective-permute-start | bytes 104456 | tf_op jit(solution)/shard_map/ppermute | solution.py:289
  17.7 0.0 collective-permute-start.5
  17.7 0.4 collective-permute-start.4
  18.0 3.8 %collective-permute-start.10 = (bf16[256,512]{1,0:T(8,128)(2,1)S(1)}, bf16[256,512]{1,0:T(8,128)(2,1)S(1)}, u32[]{:S(2)}, u32[]{:S(2)}) collective-permute-start(bf16[256,512]{1,0:T(8,128)(2,1)S(1)} %get-tuple-element.29), channel_id=1, source_target_pairs={{0,4},{4,8},{8,12},{12,16},{16,20},{20,24},{24,28},{1,5},{5,9},{9,... | collective-permute-start | bytes 786440 | tf_op jit(solution)/shard_map/ppermute | solution.py:356
  21.8 0.0 collective-permute-done.6
  21.9 0.0 collective-permute-done.5
  21.9 0.0 collective-permute-done.4
  21.9 2.2 %collective-permute-start.9 = (bf16[136,128]{1,0:T(8,128)(2,1)S(1)}, bf16[136,128]{1,0:T(8,128)(2,1)S(1)}, u32[]{:S(2)}, u32[]{:S(2)}) collective-permute-start(bf16[136,128]{1,0:T(8,128)(2,1)S(1)} %add_convert_fusion), channel_id=1, source_target_pairs={{0,3},{1,2},{2,1},{3,0},{4,7},{5,6},{6,5},{7,4},{8,11},{9,10},{10,... | collective-permute-start | bytes 104456 | tf_op jit(solution)/shard_map/ppermute | solution.py:289
  24.1 0.2 collective-permute-start.8
  24.4 0.3 collective-permute-start.7
  24.6 0.5 %collective-permute-done.10.samples = bf16[256,512]{1,0:T(8,128)(2,1)S(1)} collective-permute-done((bf16[256,512]{1,0:T(8,128)(2,1)S(1)}, bf16[256,512]{1,0:T(8,128)(2,1)S(1)}, u32[]{:S(2)}, u32[]{:S(2)}) %collective-permute-start.10) | collective-permute-done | bytes 262176 | tf_op jit(solution)/shard_map/ppermute | solution.py:356
  25.1 0.7 %previous.1.earlier = bf16[2,272,512]{2,1,0:T(8,128)(2,1)S(1)} custom-call(bf16[256,512]{1,0:T(8,128)(2,1)S(1)} %collective-permute-done.10.samples, bf16[2,272,512]{2,1,0:T(8,128)(2,1)S(1)} %get-tuple-element.30.kept, bf16[544,256]{1,0:T(8,128)(2,1)S(1)} %copy-done.3, f32[2,272,512]{2,1,0:T(8,128)S(1)} %copy-done, bf16[4,256,256]{2,1,0:T(8,128)(2,1)S(1)} %copy-done.2), custom_call_target="tpu_custom_call" | custom-call | flops 1000000000 | bytes 4000000 | tf_op jit(solution)/shard_map/previous/pallas_call | solution.py:357
  25.9 0.0 collective-permute-done.9
  25.9 1.0 %collective-permute-done.8 = bf16[136,128]{1,0:T(8,128)(2,1)S(1)} collective-permute-done((bf16[136,128]{1,0:T(8,128)(2,1)S(1)}, bf16[136,128]{1,0:T(8,128)(2,1)S(1)}, u32[]{:S(2)}, u32[]{:S(2)}) %collective-permute-start.8) | collective-permute-done | bytes 34848 | tf_op jit(solution)/shard_map/ppermute | solution.py:289
  26.9 0.6 %collective-permute-done.7 = bf16[136,128]{1,0:T(8,128)(2,1)S(1)} collective-permute-done((bf16[136,128]{1,0:T(8,128)(2,1)S(1)}, bf16[136,128]{1,0:T(8,128)(2,1)S(1)}, u32[]{:S(2)}, u32[]{:S(2)}) %collective-permute-start.7) | collective-permute-done | bytes 34848 | tf_op jit(solution)/shard_map/ppermute | solution.py:289
  27.6 2.7 %collective-permute-start.11 = (bf16[4,136,128]{2,1,0:T(8,128)(2,1)S(1)}, bf16[4,136,128]{2,1,0:T(8,128)(2,1)S(1)}, u32[]{:S(2)}, u32[]{:S(2)}) collective-permute-start(bf16[4,136,128]{2,1,0:T(8,128)(2,1)S(1)} %pad_maximum_fusion.mine), channel_id=1, source_target_pairs={{0,4},{4,0},{8,12},{12,8},{16,20},{20,16},{24,28},{28,24},{1,5},{5... | collective-permute-start | bytes 417800 | tf_op jit(solution)/shard_map/ppermute | solution.py:289
  30.2 1.0 %collective-permute-done.11.theirs = bf16[4,136,128]{2,1,0:T(8,128)(2,1)S(1)} collective-permute-done((bf16[4,136,128]{2,1,0:T(8,128)(2,1)S(1)}, bf16[4,136,128]{2,1,0:T(8,128)(2,1)S(1)}, u32[]{:S(2)}, u32[]{:S(2)}) %collective-permute-start.11) | collective-permute-done | bytes 139296 | tf_op jit(solution)/shard_map/ppermute | solution.py:289
  31.2 0.0 copy-done.1
  31.2 0.0 copy-done.4
  31.2 5.0 %filter.1 = f32[256,2,16,1,128]{4,3,2,1,0:T(1,128)} custom-call(bf16[4,136,128]{2,1,0:T(8,128)(2,1)S(1)} %pad_maximum_fusion.mine, bf16[4,136,128]{2,1,0:T(8,128)(2,1)S(1)} %collective-permute-done.11.theirs, bf16[2,272,512]{2,1,0:T(8,128)(2,1)S(1)} %previous.1.earlier, bf16[2,272,512]{2,1,0:T(8,128)(2,1)S(1)} %get-tuple-element.36.later, ...), custom_call_target="tpu_custom_call" | custom-call | flops 6000000000 | bytes 12000000 | tf_op jit(solution)/shard_map/filter/pallas_call | solution.py:373
  (5 shorter events, 0.1 us)
Async XLA Ops:
  1.2 9.8 %copy-start = (f32[2,272,512]{2,1,0:T(8,128)S(1)}, f32[2,272,512]{2,1,0:T(8,128)}, u32[]{:S(2)}) copy-start(f32[2,272,512]{2,1,0:T(8,128)} %constant.19.clone.refs_5_.twist) | copy-start | bytes 3342340
  1.2 9.8 %copy-start.2 = (bf16[4,256,256]{2,1,0:T(8,128)(2,1)S(1)}, bf16[4,256,256]{2,1,0:T(8,128)(2,1)}, u32[]{:S(2)}) copy-start(bf16[4,256,256]{2,1,0:T(8,128)(2,1)} %constant.20.clone.refs_6_.forward) | copy-start | bytes 1572868
  1.3 9.8 %copy-start.3 = (bf16[544,256]{1,0:T(8,128)(2,1)S(1)}, bf16[544,256]{1,0:T(8,128)(2,1)}, u32[]{:S(2)}) copy-start(bf16[544,256]{1,0:T(8,128)(2,1)} %constant.18.clone.refs_4_.first) | copy-start | bytes 835588
  1.3 8.9 %collective-permute-start.2 = (bf16[2,64,512]{2,1,0:T(8,128)(2,1)S(1)}, bf16[2,64,512]{2,1,0:T(8,128)(2,1)S(1)}, u32[]{:S(2)}, u32[]{:S(2)}) collective-permute-start(bf16[2,64,512]{2,1,0:T(8,128)(2,1)S(1)} %bitcast.13), channel_id=1, source_target_pairs={{0,3},{1,2},{2,1},{3,0},{4,7},{5,6},{6,5},{7,4},{8,11},{9,10},{10,... | collective-permute-start | bytes 393224 | tf_op jit(solution)/shard_map/ppermute | solution.py:289
  4.3 6.7 %collective-permute-start.1 = (bf16[2,64,512]{2,1,0:T(8,128)(2,1)S(1)}, bf16[2,64,512]{2,1,0:T(8,128)(2,1)S(1)}, u32[]{:S(2)}, u32[]{:S(2)}) collective-permute-start(bf16[2,64,512]{2,1,0:T(8,128)(2,1)S(1)} %bitcast.14), channel_id=1, source_target_pairs={{0,2},{1,3},{2,0},{3,1},{4,6},{5,7},{6,4},{7,5},{8,10},{9,11},{10,... | collective-permute-start | bytes 393224 | tf_op jit(solution)/shard_map/ppermute | solution.py:289
  4.5 6.5 %collective-permute-start = (bf16[2,64,512]{2,1,0:T(8,128)(2,1)S(1)}, bf16[2,64,512]{2,1,0:T(8,128)(2,1)S(1)}, u32[]{:S(2)}, u32[]{:S(2)}) collective-permute-start(bf16[2,64,512]{2,1,0:T(8,128)(2,1)S(1)} %bitcast.15), channel_id=1, source_target_pairs={{0,1},{1,0},{2,3},{3,2},{4,5},{5,4},{6,7},{7,6},{8,9},{9,8},{10,11... | collective-permute-start | bytes 393224 | tf_op jit(solution)/shard_map/ppermute | solution.py:289
  11.1 20.1 %copy-start.1 = (bf16[4,256,256]{2,1,0:T(8,128)(2,1)S(1)}, bf16[4,256,256]{2,1,0:T(8,128)(2,1)}, u32[]{:S(2)}) copy-start(bf16[4,256,256]{2,1,0:T(8,128)(2,1)} %constant.21.clone.inverse) | copy-start | bytes 1572868
  11.1 20.1 %copy-start.4 = (bf16[2,128,256]{2,1,0:T(8,128)(2,1)S(1)}, bf16[2,128,256]{2,1,0:T(8,128)(2,1)}, u32[]{:S(2)}) copy-start(bf16[2,128,256]{2,1,0:T(8,128)(2,1)} %constant.22.clone.last) | copy-start | bytes 393220
  12.5 1.7 %collective-permute-start.3 = (bf16[136,128]{1,0:T(8,128)(2,1)S(1)}, bf16[136,128]{1,0:T(8,128)(2,1)S(1)}, u32[]{:S(2)}, u32[]{:S(2)}) collective-permute-start(bf16[136,128]{1,0:T(8,128)(2,1)S(1)} %get-tuple-element.28), channel_id=1, source_target_pairs={{0,4},{4,0},{8,12},{12,8},{16,20},{20,16},{24,28},{28,24},{1,5},{5... | collective-permute-start | bytes 104456 | tf_op jit(solution)/shard_map/ppermute | solution.py:289
  14.2 7.6 %collective-permute-start.6 = (bf16[136,128]{1,0:T(8,128)(2,1)S(1)}, bf16[136,128]{1,0:T(8,128)(2,1)S(1)}, u32[]{:S(2)}, u32[]{:S(2)}) collective-permute-start(bf16[136,128]{1,0:T(8,128)(2,1)S(1)} %add_convert_fusion.1), channel_id=1, source_target_pairs={{0,24},{4,28},{8,16},{12,20},{16,8},{20,12},{24,0},{28,4},{1,25},{... | collective-permute-start | bytes 104456 | tf_op jit(solution)/shard_map/ppermute | solution.py:289
  17.7 4.2 %collective-permute-start.5 = (bf16[136,128]{1,0:T(8,128)(2,1)S(1)}, bf16[136,128]{1,0:T(8,128)(2,1)S(1)}, u32[]{:S(2)}, u32[]{:S(2)}) collective-permute-start(bf16[136,128]{1,0:T(8,128)(2,1)S(1)} %add_convert_fusion.1), channel_id=1, source_target_pairs={{0,16},{4,20},{8,24},{12,28},{16,0},{20,4},{24,8},{28,12},{1,17},{... | collective-permute-start | bytes 104456 | tf_op jit(solution)/shard_map/ppermute | solution.py:289
  17.7 4.2 %collective-permute-start.4 = (bf16[136,128]{1,0:T(8,128)(2,1)S(1)}, bf16[136,128]{1,0:T(8,128)(2,1)S(1)}, u32[]{:S(2)}, u32[]{:S(2)}) collective-permute-start(bf16[136,128]{1,0:T(8,128)(2,1)S(1)} %add_convert_fusion.1), channel_id=1, source_target_pairs={{0,8},{4,12},{8,0},{12,4},{16,24},{20,28},{24,16},{28,20},{1,9},{5... | collective-permute-start | bytes 104456 | tf_op jit(solution)/shard_map/ppermute | solution.py:289
  18.0 7.1 %collective-permute-start.10 = (bf16[256,512]{1,0:T(8,128)(2,1)S(1)}, bf16[256,512]{1,0:T(8,128)(2,1)S(1)}, u32[]{:S(2)}, u32[]{:S(2)}) collective-permute-start(bf16[256,512]{1,0:T(8,128)(2,1)S(1)} %get-tuple-element.29), channel_id=1, source_target_pairs={{0,4},{4,8},{8,12},{12,16},{16,20},{20,24},{24,28},{1,5},{5,9},{9,... | collective-permute-start | bytes 786440 | tf_op jit(solution)/shard_map/ppermute | solution.py:356
  21.9 4.0 %collective-permute-start.9 = (bf16[136,128]{1,0:T(8,128)(2,1)S(1)}, bf16[136,128]{1,0:T(8,128)(2,1)S(1)}, u32[]{:S(2)}, u32[]{:S(2)}) collective-permute-start(bf16[136,128]{1,0:T(8,128)(2,1)S(1)} %add_convert_fusion), channel_id=1, source_target_pairs={{0,3},{1,2},{2,1},{3,0},{4,7},{5,6},{6,5},{7,4},{8,11},{9,10},{10,... | collective-permute-start | bytes 104456 | tf_op jit(solution)/shard_map/ppermute | solution.py:289
  24.1 2.8 %collective-permute-start.8 = (bf16[136,128]{1,0:T(8,128)(2,1)S(1)}, bf16[136,128]{1,0:T(8,128)(2,1)S(1)}, u32[]{:S(2)}, u32[]{:S(2)}) collective-permute-start(bf16[136,128]{1,0:T(8,128)(2,1)S(1)} %add_convert_fusion), channel_id=1, source_target_pairs={{0,2},{1,3},{2,0},{3,1},{4,6},{5,7},{6,4},{7,5},{8,10},{9,11},{10,... | collective-permute-start | bytes 104456 | tf_op jit(solution)/shard_map/ppermute | solution.py:289
  24.4 3.2 %collective-permute-start.7 = (bf16[136,128]{1,0:T(8,128)(2,1)S(1)}, bf16[136,128]{1,0:T(8,128)(2,1)S(1)}, u32[]{:S(2)}, u32[]{:S(2)}) collective-permute-start(bf16[136,128]{1,0:T(8,128)(2,1)S(1)} %add_convert_fusion), channel_id=1, source_target_pairs={{0,1},{1,0},{2,3},{3,2},{4,5},{5,4},{6,7},{7,6},{8,9},{9,8},{10,11... | collective-permute-start | bytes 104456 | tf_op jit(solution)/shard_map/ppermute | solution.py:289
  27.6 3.7 %collective-permute-start.11 = (bf16[4,136,128]{2,1,0:T(8,128)(2,1)S(1)}, bf16[4,136,128]{2,1,0:T(8,128)(2,1)S(1)}, u32[]{:S(2)}, u32[]{:S(2)}) collective-permute-start(bf16[4,136,128]{2,1,0:T(8,128)(2,1)S(1)} %pad_maximum_fusion.mine), channel_id=1, source_target_pairs={{0,4},{4,0},{8,12},{12,8},{16,20},{20,16},{24,28},{28,24},{1,5},{5... | collective-permute-start | bytes 417800 | tf_op jit(solution)/shard_map/ppermute | solution.py:289

commit v3 on v2

--- a/solution.py
+++ b/solution.py
@@ -20,10 +20,14 @@
 
 
 def tables(order):
-    half, group = order // 2, order // 4
+    half, group, eighth = order // 2, order // 4, order // 8
+    i, pad = np.arange(group), np.zeros(8, np.int64)
+    middle = np.concatenate([[group], pad[1:]])
+    a = np.concatenate([i[:eighth], half - i[:eighth], middle, i[eighth:], half - i[eighth:], pad])
     rows = half + 16
-    a = np.concatenate([np.arange(group), half - np.arange(group), [group], np.zeros(15, np.int64)])
-    keep = (np.arange(rows) <= half)[:, None]
+    keep = np.ones((rows, 1))
+    keep[group + 1 : group + 8] = 0
+    keep[rows - 8 :] = 0
     turn = 2.0 * math.pi / order
 
     def angle(left, right):
@@ -43,7 +47,8 @@
         c, s = np.cos(angle(w, g)), -np.sin(angle(w, g))
         c[:, 0] = 0.5
         s[:, 0] = (1.0 - 2.0 * parity) * (1.0 - 2.0 * (g % 2))
-        last.append(np.concatenate([c, s], axis=1))
+        sides = [np.concatenate([c[:, h], s[:, h]], axis=1) for h in (slice(0, eighth), slice(eighth, group))]
+        last.append([np.concatenate([sides[core], sides[1 - core]], axis=1) for core in range(2)])
     return dict(
         first=first.astype(bf16),
         twist=np.stack([np.cos(twist), np.sin(twist)]).astype(np.float32),
@@ -114,7 +119,8 @@
 
 def previous_kernel(samples, kept, first, twist, forward, summed):
     group = forward.shape[1] // 2
-    parts = spectrum(samples[...], first, twist, forward)
+    follows = lax.axis_index("tm") > 0
+    parts = spectrum(jnp.where(follows, samples[...].astype(f32), 0.0).astype(bf16), first, twist, forward)
     for place, q in enumerate(group_order):
         x = parts[q]
         cols = slice(place * group, (place + 1) * group)
@@ -150,8 +156,14 @@
             return jnp.where(start, head, dot(flip, whole[at : at + group])).astype(bf16)
 
         turned = pltpu.roll(wide[:8], order - 1, 1)[:1]
-        upper = [whole[:group], flipped(group, wide[half : half + 1]), whole[group : group + 16]]
-        lower = [flipped(half + group, turned), whole[half : half + group], whole[half + group : half + group + 16]]
+        mirror, wrapped = flipped(group, wide[half : half + 1]), flipped(half + group, turned)
+        upper, lower = [], []
+        for h in range(2):
+            near_rows = slice(h * (group // 2), (h + 1) * (group // 2))
+            upper += [whole[near_rows], mirror[near_rows], whole[group + 8 * h : group + 8 * h + 8]]
+            at = half + h * (group // 2)
+            lower += [wrapped[near_rows], whole[at : at + group // 2]]
+            lower += [whole[half + group + 8 * h : half + group + 8 * h + 8]]
         lower = jnp.concatenate(lower)
         if part == 1:
             lower = -lower
@@ -162,36 +174,137 @@
     factor[0] = jnp.broadcast_to(lax.rsqrt(total), factor.shape[1:])
 
 
+def section_rows(folded, white, inverse, block, template, side, here, put):
+    group = inverse.shape[1] // 2
+    half = 2 * group
+    cols = slice(side * half, (side + 1) * half)
+    vr, vi = white[block, 0, :, cols], white[block, 1, :, cols]
+    gr, gi = folded[template, 0, here, cols], folded[template, 1, here, cols]
+    pr = gr * vr + gi * vi
+    pi = gr * vi - gi * vr
+    one, two = (
+        dot(jnp.concatenate([pr[:, part], pi[:, part]], axis=1), inverse[group_order[2 * side + k]])
+        for k, part in enumerate((slice(0, group), slice(group, half)))
+    )
+    plus, minus = one + two, one - two
+    if side == 0:
+        real, imag = (plus[:, :group], minus[:, :group]), (plus[:, group:], minus[:, group:])
+    else:
+        real, imag = (plus[:, :group], two[:, group:] - one[:, group:]), (plus[:, group:], minus[:, :group])
+    put(2 * side, jnp.concatenate(real, axis=1).astype(bf16))
+    put(2 * side + 1, jnp.concatenate(imag, axis=1).astype(bf16))
+
+
+def fill_weights(pieces, weight, blocks):
+    bank = lax.axis_index("bank")
+    chunk = pieces.shape[1]
+    for s in range(pieces.shape[0]):
+        at = pl.multiple_of((bank ^ s) * chunk, 8)
+        weight[pl.ds(at, chunk), :] = lax.rsqrt(pieces[s].astype(f32) / blocks + epsilon)
+
+
+def whiten_rows(spectra, weight, white, block, side, here):
+    chunk, half = white.shape[2], white.shape[3] // 2
+    cols = slice(side * half, (side + 1) * half)
+    tiles = range(side * half // 128, (side + 1) * half // 128)
+    scale = jnp.concatenate([weight[t * chunk : (t + 1) * chunk, :] for t in tiles], axis=1)
+    for part in range(2):
+        white[block, part, :, cols] = (spectra[part, here, cols].astype(f32) * scale).astype(bf16)
+
+
+def turned(sums, turn, at, size):
+    span = slice(at, at + size)
+    half = sums.shape[2]
+    r0, i0, r1, i1 = (sums[plane, span] for plane in range(4))
+    values = []
+    for side, (ir, ii) in enumerate(((r0 + r1, i0 + i1), (r0 - r1, i0 - i1))):
+        cols = slice(side * half, (side + 1) * half)
+        tc, ts = turn[0, span, cols], turn[1, span, cols]
+        values.append((ir * tc - ii * ts, ii * tc + ir * ts))
+    return values
+
+
+def twists(sums, turn, which, part, parts, put):
+    half = sums.shape[2]
+    near_count = half // 4
+    step = 16
+    first = (lax.broadcasted_iota(jnp.int32, (step, half), 0) == 0) & (which == 0)
+    for at in range(part * near_count // parts, (part + 1) * near_count // parts, step):
+        near_rows, far_rows = turned(sums, turn, at, step), turned(sums, turn, near_count + at, step)
+        middle = turned(sums, turn, 2 * near_count, 8) if at == 0 else None
+        for side in range(2):
+            (r0, i0), (r1, i1) = near_rows[side], far_rows[side]
+            for parity in range(2):
+                re, im = (r0 + r1, i0 - i1) if parity == 0 else (r0 - r1, i0 + i1)
+                if at == 0:
+                    row = middle[side][parity][:1].astype(f32)
+                    im = jnp.where(first, jnp.broadcast_to(row, im.shape), im.astype(f32)).astype(bf16)
+                put(parity, side, at, re)
+                put(parity, side, near_count + at, im)
+
+
+def own_rows_kernel(
+    mine, earlier, later, folded, twist, inverse, back, weight, white, turn, even_sums, odd_sums, *, blocks
+):
+    chunk, count = white.shape[2], folded.shape[0]
+    core = lax.rem(lax.axis_index("tm"), 2)
+    here = pl.ds(pl.multiple_of(core * chunk, 8), chunk)
+    fill_weights(mine, weight, blocks)
+    turn[...] = twist[:, here, :].astype(bf16)
+    total = 2 * count
+    for slot in range(total + 1):
+        for j in range(2):
+            if slot < total:
+                block, template = divmod(slot, count)
+                sums = (even_sums, odd_sums)[slot % 2]
+                if template == 0:
+                    whiten_rows((earlier, later)[block], weight, white, block, j, here)
+
+                def put_sums(plane, value):
+                    sums[plane] = value
+
+                section_rows(folded, white, inverse, block, template, j, here, put_sums)
+            if slot > 0:
+
+                def put_back(parity, side, at, value):
+                    back[slot - 1, parity, side, at : at + value.shape[0]] = value
+
+                twists((even_sums, odd_sums)[(slot - 1) % 2], turn, core, j, 2, put_back)
+
+
+def own_scratch(blocks, rows, order):
+    half = order // 2
+    return [
+        pltpu.VMEM((rows // 2 * order // 128, 128), f32),
+        pltpu.VMEM((blocks, 2, rows // 2, order), bf16),
+        pltpu.VMEM((2, rows // 2, order), bf16),
+        pltpu.VMEM((4, rows // 2, half), bf16),
+        pltpu.VMEM((4, rows // 2, half), bf16),
+    ]
+
+
 def filter_scratch(blocks, count, rows, order):
     half, pairs = order // 2, blocks * count
-    return [
-        pltpu.VMEM((rows * order // 128, 128), f32),
-        pltpu.VMEM((blocks, 2, rows, order), bf16),
-        pltpu.VMEM((2, rows, order), bf16),
-        pltpu.VMEM((2, 4, rows, half), bf16),
-        pltpu.VMEM((2, 2, 2, half, half), bf16),
+    return own_scratch(blocks, rows, order) + [
+        pltpu.VMEM((2, 2, half // 2, half), bf16),
+        pltpu.VMEM((2, 2, half // 2, half), bf16),
         pltpu.VMEM((pairs, 2, half // 2, order), f32),
         pltpu.SemaphoreType.DMA((pairs,)),
     ]
 
 
 def filter_kernel(
-    mine, theirs, earlier, later, folded, factor, twist, inverse, last, out,
-    weight, white, turn, sums, back, result, sems, *, blocks
+    theirs, own, earlier, later, folded, factor, twist, inverse, last, out,
+    weight, white, turn, even_sums, odd_sums, even_back, odd_back, result, sems, *, blocks
 ):
-    group = last.shape[1]
+    group = last.shape[2]
     half, order = 2 * group, 4 * group
-    rows = twist.shape[1]
-    count = folded.shape[0]
+    count, chunk = folded.shape[0], white.shape[2]
     lanes = order // 128
-    chunk = mine.shape[1]
-    bank, own = lax.axis_index("bank"), lax.rem(lax.axis_index("tm"), 2)
-    for s in range(mine.shape[0]):
-        for pieces, core in ((mine, own), (theirs, 1 - own)):
-            at = pl.multiple_of(((bank ^ s) * 2 + core) * chunk, 8)
-            total = pieces[s].astype(f32)
-            weight[pl.ds(at, chunk), :] = lax.rsqrt(total / blocks + epsilon)
-    turn[...] = twist[...].astype(bf16)
+    core = lax.rem(lax.axis_index("tm"), 2)
+    there = pl.ds(pl.multiple_of((1 - core) * chunk, 8), chunk)
+    fill_weights(theirs, weight, blocks)
+    turn[...] = twist[:, there, :].astype(bf16)
 
     def copies(slot):
         block, template = divmod(slot, count)
@@ -205,80 +318,45 @@
             for lane in range(lanes)
         ]
 
-    def whiten(block, side):
-        spectra = (earlier, later)[block]
-        cols = slice(side * half, (side + 1) * half)
-        tiles = range(side * half // 128, (side + 1) * half // 128)
-        scale = jnp.concatenate([weight[t * rows : (t + 1) * rows, :] for t in tiles], axis=1)
-        for part in range(2):
-            white[block, part, :, cols] = (spectra[part, :, cols].astype(f32) * scale).astype(bf16)
-
     def products(slot, side):
         block, template = divmod(slot, count)
+        sums = (even_sums, odd_sums)[slot % 2]
         if template == 0:
-            whiten(block, side)
-        cols = slice(side * half, (side + 1) * half)
-        vr, vi = white[block, 0, :, cols], white[block, 1, :, cols]
-        gr, gi = folded[template, 0, :, cols], folded[template, 1, :, cols]
-        pr = gr * vr + gi * vi
-        pi = gr * vi - gi * vr
-        one, two = (
-            dot(jnp.concatenate([pr[:, here], pi[:, here]], axis=1), inverse[group_order[2 * side + k]])
-            for k, here in enumerate((slice(0, group), slice(group, half)))
-        )
-        plus, minus = one + two, one - two
-        if side == 0:
-            real, imag = (plus[:, :group], minus[:, :group]), (plus[:, group:], minus[:, group:])
-        else:
-            real, imag = (plus[:, :group], two[:, group:] - one[:, group:]), (plus[:, group:], minus[:, :group])
-        sums[slot % 2, 2 * side] = jnp.concatenate(real, axis=1).astype(bf16)
-        sums[slot % 2, 2 * side + 1] = jnp.concatenate(imag, axis=1).astype(bf16)
-
-    def turned(slot, at, size):
-        here = slice(at, at + size)
-        r0, i0, r1, i1 = (sums[slot % 2, plane, here] for plane in range(4))
-        values = []
-        for side, (ir, ii) in enumerate(((r0 + r1, i0 + i1), (r0 - r1, i0 - i1))):
-            cols = slice(side * half, (side + 1) * half)
-            tc, ts = turn[0, here, cols], turn[1, here, cols]
-            values.append((ir * tc - ii * ts, ii * tc + ir * ts))
-        return values
-
-    def twists(slot, part, parts):
-        step = 16
-        first = lax.broadcasted_iota(jnp.int32, (step, half), 0) == 0
-        span = group // parts
-        for at in range(part * span, (part + 1) * span, step):
-            near_rows, far_rows = turned(slot, at, step), turned(slot, group + at, step)
-            middle = turned(slot, half, step) if at == 0 else None
-            for side in range(2):
-                (r0, i0), (r1, i1) = near_rows[side], far_rows[side]
-                for parity in range(2):
-                    re, im = (r0 + r1, i0 - i1) if parity == 0 else (r0 - r1, i0 + i1)
-                    if at == 0:
-                        row = middle[side][parity][:1].astype(f32)
-                        im = jnp.where(first, jnp.broadcast_to(row, im.shape), im.astype(f32)).astype(bf16)
-                    back[slot % 2, parity, side, at : at + step] = re
-                    back[slot % 2, parity, side, group + at : group + at + step] = im
+            whiten_rows((earlier, later)[block], weight, white, block, side, there)
+
+        def put(plane, value):
+            sums[plane] = value
+
+        section_rows(folded, white, inverse, block, template, side, there, put)
+
+    def turns(slot, part):
+        back = (even_back, odd_back)[slot % 2]
+
+        def put(parity, side, at, value):
+            back[parity, side, at : at + value.shape[0]] = value
+
+        twists((even_sums, odd_sums)[slot % 2], turn, 1 - core, part, 2, put)
 
     def finish(slot, parity, side):
+        back = (even_back, odd_back)[slot % 2]
         scale = factor[slot % count, 0:1, 0:1]
-        value = dot(last[parity], back[slot % 2, parity, side])
-        result[slot, parity, :, side * half : (side + 1) * half] = value * scale
+        whole = jnp.concatenate([own[slot, parity, side], back[parity, side]], axis=0)
+        result[slot, parity, :, side * half : (side + 1) * half] = dot(last[parity, core], whole) * scale
 
     total = 2 * count
     for step in range(total + 2):
         for j in range(2):
-            if step < total:
-                products(step, j)
+            if 0 <= step - 1 < total:
+                turns(step - 1, j)
             if 0 <= step - 2:
                 finish(step - 2, j, 0)
                 finish(step - 2, j, 1)
-            if 0 <= step - 1 < total:
-                twists(step - 1, j, 2)
-        if 0 <= step - 2:
-            for copy in copies(step - 2):
-                copy.start()
+            if step < total:
+                products(step, j)
+        if step % 2 == 1 and step >= 3:
+            for slot in (step - 3, step - 2):
+                for copy in copies(slot):
+                    copy.start()
     for slot in range(total):
         for copy in copies(slot):
             copy.wait()
@@ -353,7 +431,7 @@
         share = share + exchange(chip, "tm", lambda i, s=step: i ^ (2 * s)).astype(f32)
     share = share.astype(bf16)
 
-    before = lax.ppermute(last_block, "tm", [(i, i + 1) for i in range(groups - 1)])
+    before = lax.ppermute(last_block, "tm", [(i, (i + 1) % groups) for i in range(groups)])
     earlier = pl.pallas_call(
         previous_kernel,
         in_specs=[vmem] * 5,
@@ -370,8 +448,19 @@
     theirs = exchange(mine, "tm", lambda i: i ^ 1)
 
     lanes = order // 128
+    blocks = float(blocks_here * groups)
+    own = pl.pallas_call(
+        functools.partial(own_rows_kernel, blocks=blocks),
+        in_specs=[vmem] * 6,
+        out_specs=vmem,
+        out_shape=pltpu.VMEM((blocks_here * count, 2, 2, half // 2, half), bf16),
+        scratch_shapes=own_scratch(blocks_here, rows, order),
+        cost_estimate=pl.CostEstimate(flops=int(2e9), bytes_accessed=int(6e6), transcendentals=0),
+        compiler_params=limit,
+        name="own_rows",
+    )(near(mine), near(earlier), near(later), near(folded), table["twist"], table["inverse"])
     out = pl.pallas_call(
-        functools.partial(filter_kernel, blocks=float(blocks_here * groups)),
+        functools.partial(filter_kernel, blocks=blocks),
         in_specs=[vmem] * 9,
         out_specs=pl.BlockSpec(memory_space=pl.ANY),
         out_shape=jax.ShapeDtypeStruct((blocks_here * half // 2, 2, lanes * count, 1, 128), f32),
@@ -380,7 +469,7 @@
         compiler_params=limit,
         name="filter",
     )(
-        near(mine), near(theirs), near(earlier), near(later), near(folded), near(factor),
+        near(theirs), near(own), near(earlier), near(later), near(folded), near(factor),
         table["twist"], table["inverse"], table["last"],
     )
     split = out.reshape(blocks_here * half * lanes, count, 128)

time: 36.8 us -> 35.3 us (0.959)
  starting transfers between devices: 17.2 us -> 15.7 us
  waiting for transfers between devices: 4.89 us -> 5.45 us
    ppermute x1, starting transfers between devices: 3.8 us -> 1.9 us  [body(): lax.ppermute(last_block, 'tm', [(i, (i + 1) % groups) for i in range(grou...]
    ppermute x11, waiting for transfers between devices: 4.37 us -> 5.45 us  [exchange(): return lax.ppermute(values, axis, [(i, pairs_of(i)) for i in range(size)])]
    ppermute x1, waiting for transfers between devices: 0.52 us -> 0.01 us  [body(): lax.ppermute(last_block, 'tm', [(i, (i + 1) % groups) for i in range(grou...]
    ppermute x11, starting transfers between devices: 13.4 us -> 13.8 us  [exchange(): return lax.ppermute(values, axis, [(i, pairs_of(i)) for i in range(size)])]
    pallas_call x1 -> x2, Pallas kernels: 5.03 us -> 4.75 us  [the longest x1 3.36 us: body(): pl.pallas_call(functools.partial(filter_kernel, blocks=blocks), in_specs=...]
  transfers between devices with their start and end apart: 12 -> 12, of which waited for: 6 -> 6; matrix products, arithmetic and copies ran while one was open for 0% -> 0% of each run, Pallas kernels for 17% -> 22%
where the time goes in v3:
time: 35.3 us; the launch traced here: 35.1 us
  starting transfers between devices  15.7 us (44%)
  Pallas kernels  12.5 us (35%)
  waiting for transfers between devices  5.45 us (15%)
  other arithmetic  1.25 us (4%)
    ppermute x11, starting transfers between devices, exchange(): return lax.ppermute(values, axis, [(i, pairs_of(i)) for i in range(size)])  13.8 us
    pallas_call x1, Pallas kernels, body(): pl.pallas_call(template_kernel, grid=(count,), in_specs=[pl.BlockSpec((2,...  5.69 us
    ppermute x11, waiting for transfers between devices, exchange(): return lax.ppermute(values, axis, [(i, pairs_of(i)) for i in range(size)])  5.45 us
    pallas_call x1, Pallas kernels, body(): pl.pallas_call(functools.partial(filter_kernel, blocks=blocks), in_specs=...  3.36 us
    ppermute x1, starting transfers between devices, body(): lax.ppermute(last_block, 'tm', [(i, (i + 1) % groups) for i in range(grou...  1.9 us
    pallas_call x1, Pallas kernels, body(): pl.pallas_call(functools.partial(own_rows_kernel, blocks=blocks), in_spec...  1.39 us
    pallas_call x1, Pallas kernels, body(): pl.pallas_call(functools.partial(spectrum_kernel, shards=banks), in_specs...  1.37 us
    convert_element_type x1, other arithmetic, body(): jnp.where(valid, strain, 0.0).astype(bf16)  1.18 us
  transfers between devices with their start and end apart: 12, of which 6 were waited for; matrix products, arithmetic and copies ran while one was open for 0% of the time, Pallas kernels for 22%

profile of v3, /device:TPU:1, one launch (start us, length us, event | category | flops | bytes accessed | tf_op | source)
XLA Modules:
  0.0 35.1 jit_solution(3720364286479658073)
XLA Ops:
  0.0 1.2 %fusion = bf16[2,32768]{1,0:T(2,128)(2,1)S(1)} fusion(f32[2,32768]{1,0:T(2,128)} %param.8, s32[32768]{0:T(1024)S(1)} %iota_add_fusion, s32[2]{0:T(128)} %param.9), kind=kLoop, calls=%fused_computation.1 | loop fusion | flops 131072 | bytes 524296 | tf_op jit(solution)/shard_map/convert_element_type | solution.py:387
  1.2 0.0 copy-start
  1.2 0.0 copy-start.2
  1.3 0.0 copy-start.3
  1.3 3.0 %collective-permute-start.2 = (bf16[2,64,512]{2,1,0:T(8,128)(2,1)S(1)}, bf16[2,64,512]{2,1,0:T(8,128)(2,1)S(1)}, u32[]{:S(2)}, u32[]{:S(2)}) collective-permute-start(bf16[2,64,512]{2,1,0:T(8,128)(2,1)S(1)} %bitcast.13), channel_id=1, source_target_pairs={{0,3},{1,2},{2,1},{3,0},{4,7},{5,6},{6,5},{7,4},{8,11},{9,10},{10,... | collective-permute-start | bytes 393224 | tf_op jit(solution)/shard_map/ppermute | solution.py:367
  4.3 0.2 collective-permute-start.1
  4.5 0.1 collective-permute-start
  4.7 5.7 %fold_templates.1 = (bf16[4,2,272,512]{3,2,1,0:T(8,128)(2,1)S(1)}, f32[4,8,128]{2,1,0:T(8,128)S(1)}) custom-call(bf16[2,4,512,512]{3,2,1,0:T(8,128)(2,1)} %templates.1), custom_call_target="tpu_custom_call" | custom-call | flops 6000000000 | bytes 6500000 | tf_op jit(solution)/shard_map/fold_templates/pallas_call | solution.py:390
  10.4 0.0 collective-permute-done.2.refs_3_
  10.4 0.7 %collective-permute-done.1.refs_2_ = bf16[2,64,512]{2,1,0:T(8,128)(2,1)S(1)} collective-permute-done((bf16[2,64,512]{2,1,0:T(8,128)(2,1)S(1)}, bf16[2,64,512]{2,1,0:T(8,128)(2,1)S(1)}, u32[]{:S(2)}, u32[]{:S(2)}) %collective-permute-start.1) | collective-permute-done | bytes 131104 | tf_op jit(solution)/shard_map/ppermute | solution.py:367
  11.1 0.0 collective-permute-done.refs_1_
  11.1 0.0 copy-done
  11.1 0.0 copy-done.2
  11.1 0.0 copy-done.3
  11.1 1.4 %spectra.1 = (bf16[2,272,512]{2,1,0:T(8,128)(2,1)S(1)}, bf16[2,272,512]{2,1,0:T(8,128)(2,1)S(1)}, bf16[136,128]{1,0:T(8,128)(2,1)S(1)}, bf16[136,128]{1,0:T(8,128)(2,1)S(1)}, bf16[256,512]{1,0:T(8,128)(2,1)S(1)}) custom-call(bf16[2,64,512]{2,1,0:T(8,128)(2,1)S(1)} %bitcast.16, bf16[2,64,512]{2,1,0:T(8,128)(2,1)S(1)} %collective-permute-done.refs_1_, ...), custom_call_target="tpu_custom_call" | custom-call | flops 2000000000 | bytes 5000000 | tf_op jit(solution)/shard_map/spectra/pallas_call | solution.py:411
  12.5 0.0 copy-start.1
  12.5 0.8 %collective-permute-start.3 = (bf16[136,128]{1,0:T(8,128)(2,1)S(1)}, bf16[136,128]{1,0:T(8,128)(2,1)S(1)}, u32[]{:S(2)}, u32[]{:S(2)}) collective-permute-start(bf16[136,128]{1,0:T(8,128)(2,1)S(1)} %get-tuple-element.28), channel_id=1, source_target_pairs={{0,4},{4,0},{8,12},{12,8},{16,20},{20,16},{24,28},{28,24},{1,5},{5... | collective-permute-start | bytes 104456 | tf_op jit(solution)/shard_map/ppermute | solution.py:367
  13.3 0.9 %collective-permute-done.3 = bf16[136,128]{1,0:T(8,128)(2,1)S(1)} collective-permute-done((bf16[136,128]{1,0:T(8,128)(2,1)S(1)}, bf16[136,128]{1,0:T(8,128)(2,1)S(1)}, u32[]{:S(2)}, u32[]{:S(2)}) %collective-permute-start.3) | collective-permute-done | bytes 34848 | tf_op jit(solution)/shard_map/ppermute | solution.py:367
  14.2 3.6 %collective-permute-start.6 = (bf16[136,128]{1,0:T(8,128)(2,1)S(1)}, bf16[136,128]{1,0:T(8,128)(2,1)S(1)}, u32[]{:S(2)}, u32[]{:S(2)}) collective-permute-start(bf16[136,128]{1,0:T(8,128)(2,1)S(1)} %add_convert_fusion.1), channel_id=1, source_target_pairs={{0,24},{4,28},{8,16},{12,20},{16,8},{20,12},{24,0},{28,4},{1,25},{... | collective-permute-start | bytes 104456 | tf_op jit(solution)/shard_map/ppermute | solution.py:367
  17.8 0.0 collective-permute-start.5
  17.8 0.4 %collective-permute-start.4 = (bf16[136,128]{1,0:T(8,128)(2,1)S(1)}, bf16[136,128]{1,0:T(8,128)(2,1)S(1)}, u32[]{:S(2)}, u32[]{:S(2)}) collective-permute-start(bf16[136,128]{1,0:T(8,128)(2,1)S(1)} %add_convert_fusion.1), channel_id=1, source_target_pairs={{0,8},{4,12},{8,0},{12,4},{16,24},{20,28},{24,16},{28,20},{1,9},{5... | collective-permute-start | bytes 104456 | tf_op jit(solution)/shard_map/ppermute | solution.py:367
  18.2 1.9 %collective-permute-start.10 = (bf16[256,512]{1,0:T(8,128)(2,1)S(1)}, bf16[256,512]{1,0:T(8,128)(2,1)S(1)}, u32[]{:S(2)}, u32[]{:S(2)}) collective-permute-start(bf16[256,512]{1,0:T(8,128)(2,1)S(1)} %get-tuple-element.29), channel_id=1, source_target_pairs={{0,4},{4,8},{8,12},{12,16},{16,20},{20,24},{24,28},{28,0},{1,5},{5... | collective-permute-start | bytes 786440 | tf_op jit(solution)/shard_map/ppermute | solution.py:434
  20.1 0.0 collective-permute-done.6
  20.1 1.8 %collective-permute-done.5 = bf16[136,128]{1,0:T(8,128)(2,1)S(1)} collective-permute-done((bf16[136,128]{1,0:T(8,128)(2,1)S(1)}, bf16[136,128]{1,0:T(8,128)(2,1)S(1)}, u32[]{:S(2)}, u32[]{:S(2)}) %collective-permute-start.5) | collective-permute-done | bytes 34848 | tf_op jit(solution)/shard_map/ppermute | solution.py:367
  21.9 0.0 collective-permute-done.4
  21.9 2.2 %collective-permute-start.9 = (bf16[136,128]{1,0:T(8,128)(2,1)S(1)}, bf16[136,128]{1,0:T(8,128)(2,1)S(1)}, u32[]{:S(2)}, u32[]{:S(2)}) collective-permute-start(bf16[136,128]{1,0:T(8,128)(2,1)S(1)} %add_convert_fusion), channel_id=1, source_target_pairs={{0,3},{1,2},{2,1},{3,0},{4,7},{5,6},{6,5},{7,4},{8,11},{9,10},{10,... | collective-permute-start | bytes 104456 | tf_op jit(solution)/shard_map/ppermute | solution.py:367
  24.1 0.2 collective-permute-start.8
  24.4 0.3 collective-permute-start.7
  24.6 0.0 collective-permute-done.10.samples
  24.6 0.7 %previous.1.earlier = bf16[2,272,512]{2,1,0:T(8,128)(2,1)S(1)} custom-call(bf16[256,512]{1,0:T(8,128)(2,1)S(1)} %collective-permute-done.10.samples, bf16[2,272,512]{2,1,0:T(8,128)(2,1)S(1)} %get-tuple-element.30.kept, bf16[544,256]{1,0:T(8,128)(2,1)S(1)} %copy-done.3, f32[2,272,512]{2,1,0:T(8,128)S(1)} %copy-done, bf16[4,256,256]{2,1,0:T(8,128)(2,1)S(1)} %copy-done.2), custom_call_target="tpu_custom_call" | custom-call | flops 1000000000 | bytes 4000000 | tf_op jit(solution)/shard_map/previous/pallas_call | solution.py:435
  25.3 0.6 %collective-permute-done.9 = bf16[136,128]{1,0:T(8,128)(2,1)S(1)} collective-permute-done((bf16[136,128]{1,0:T(8,128)(2,1)S(1)}, bf16[136,128]{1,0:T(8,128)(2,1)S(1)}, u32[]{:S(2)}, u32[]{:S(2)}) %collective-permute-start.9) | collective-permute-done | bytes 34848 | tf_op jit(solution)/shard_map/ppermute | solution.py:367
  25.9 1.0 %collective-permute-done.8 = bf16[136,128]{1,0:T(8,128)(2,1)S(1)} collective-permute-done((bf16[136,128]{1,0:T(8,128)(2,1)S(1)}, bf16[136,128]{1,0:T(8,128)(2,1)S(1)}, u32[]{:S(2)}, u32[]{:S(2)}) %collective-permute-start.8) | collective-permute-done | bytes 34848 | tf_op jit(solution)/shard_map/ppermute | solution.py:367
  26.9 0.5 %collective-permute-done.7 = bf16[136,128]{1,0:T(8,128)(2,1)S(1)} collective-permute-done((bf16[136,128]{1,0:T(8,128)(2,1)S(1)}, bf16[136,128]{1,0:T(8,128)(2,1)S(1)}, u32[]{:S(2)}, u32[]{:S(2)}) %collective-permute-start.7) | collective-permute-done | bytes 34848 | tf_op jit(solution)/shard_map/ppermute | solution.py:367
  27.5 2.9 %collective-permute-start.11 = (bf16[4,136,128]{2,1,0:T(8,128)(2,1)S(1)}, bf16[4,136,128]{2,1,0:T(8,128)(2,1)S(1)}, u32[]{:S(2)}, u32[]{:S(2)}) collective-permute-start(bf16[4,136,128]{2,1,0:T(8,128)(2,1)S(1)} %pad_maximum_fusion.mine), channel_id=1, source_target_pairs={{0,4},{4,0},{8,12},{12,8},{16,20},{20,16},{24,28},{28,24},{1,5},{5... | collective-permute-start | bytes 417800 | tf_op jit(solution)/shard_map/ppermute | solution.py:367
  30.3 0.0 copy-done.1
  30.3 0.0 copy-start.4
  30.3 1.4 %own_rows.1.own = bf16[8,2,2,128,256]{4,3,2,1,0:T(8,128)(2,1)S(1)} custom-call(bf16[4,136,128]{2,1,0:T(8,128)(2,1)S(1)} %pad_maximum_fusion.mine, bf16[2,272,512]{2,1,0:T(8,128)(2,1)S(1)} %previous.1.earlier, bf16[2,272,512]{2,1,0:T(8,128)(2,1)S(1)} %get-tuple-element.36.later, bf16[4,2,272,512]{3,2,1,0:T(8,128)(2,1)S(1)} %get-tuple-element.37.folded, ...), custom_call_target="tpu_custom_call" | custom-call | flops 2000000000 | bytes 6000000 | tf_op jit(solution)/shard_map/own_rows/pallas_call | solution.py:452
  31.7 0.0 collective-permute-done.11.theirs
  31.7 0.0 copy-done.4
  31.8 3.4 %filter.1 = f32[256,2,16,1,128]{4,3,2,1,0:T(1,128)} custom-call(bf16[4,136,128]{2,1,0:T(8,128)(2,1)S(1)} %collective-permute-done.11.theirs, bf16[8,2,2,128,256]{4,3,2,1,0:T(8,128)(2,1)S(1)} %own_rows.1.own, bf16[2,272,512]{2,1,0:T(8,128)(2,1)S(1)} %previous.1.earlier, bf16[2,272,512]{2,1,0:T(8,128)(2,1)S(1)} %get-tuple-element.36.later, ...), custom_call_target="tpu_custom_call" | custom-call | flops 6000000000 | bytes 12000000 | tf_op jit(solution)/shard_map/filter/pallas_call | solution.py:462
  (5 shorter events, 0.1 us)
Async XLA Ops:
  1.2 9.8 %copy-start = (f32[2,272,512]{2,1,0:T(8,128)S(1)}, f32[2,272,512]{2,1,0:T(8,128)}, u32[]{:S(2)}) copy-start(f32[2,272,512]{2,1,0:T(8,128)} %constant.19.clone.refs_5_.twist) | copy-start | bytes 3342340
  1.2 9.8 %copy-start.2 = (bf16[4,256,256]{2,1,0:T(8,128)(2,1)S(1)}, bf16[4,256,256]{2,1,0:T(8,128)(2,1)}, u32[]{:S(2)}) copy-start(bf16[4,256,256]{2,1,0:T(8,128)(2,1)} %constant.20.clone.refs_6_.forward) | copy-start | bytes 1572868
  1.3 9.8 %copy-start.3 = (bf16[544,256]{1,0:T(8,128)(2,1)S(1)}, bf16[544,256]{1,0:T(8,128)(2,1)}, u32[]{:S(2)}) copy-start(bf16[544,256]{1,0:T(8,128)(2,1)} %constant.18.clone.refs_4_.first) | copy-start | bytes 835588
  1.3 9.1 %collective-permute-start.2 = (bf16[2,64,512]{2,1,0:T(8,128)(2,1)S(1)}, bf16[2,64,512]{2,1,0:T(8,128)(2,1)S(1)}, u32[]{:S(2)}, u32[]{:S(2)}) collective-permute-start(bf16[2,64,512]{2,1,0:T(8,128)(2,1)S(1)} %bitcast.13), channel_id=1, source_target_pairs={{0,3},{1,2},{2,1},{3,0},{4,7},{5,6},{6,5},{7,4},{8,11},{9,10},{10,... | collective-permute-start | bytes 393224 | tf_op jit(solution)/shard_map/ppermute | solution.py:367
  4.3 6.7 %collective-permute-start.1 = (bf16[2,64,512]{2,1,0:T(8,128)(2,1)S(1)}, bf16[2,64,512]{2,1,0:T(8,128)(2,1)S(1)}, u32[]{:S(2)}, u32[]{:S(2)}) collective-permute-start(bf16[2,64,512]{2,1,0:T(8,128)(2,1)S(1)} %bitcast.14), channel_id=1, source_target_pairs={{0,2},{1,3},{2,0},{3,1},{4,6},{5,7},{6,4},{7,5},{8,10},{9,11},{10,... | collective-permute-start | bytes 393224 | tf_op jit(solution)/shard_map/ppermute | solution.py:367
  4.5 6.5 %collective-permute-start = (bf16[2,64,512]{2,1,0:T(8,128)(2,1)S(1)}, bf16[2,64,512]{2,1,0:T(8,128)(2,1)S(1)}, u32[]{:S(2)}, u32[]{:S(2)}) collective-permute-start(bf16[2,64,512]{2,1,0:T(8,128)(2,1)S(1)} %bitcast.15), channel_id=1, source_target_pairs={{0,1},{1,0},{2,3},{3,2},{4,5},{5,4},{6,7},{7,6},{8,9},{9,8},{10,11... | collective-permute-start | bytes 393224 | tf_op jit(solution)/shard_map/ppermute | solution.py:367
  12.5 17.9 %copy-start.1 = (bf16[4,256,256]{2,1,0:T(8,128)(2,1)S(1)}, bf16[4,256,256]{2,1,0:T(8,128)(2,1)}, u32[]{:S(2)}) copy-start(bf16[4,256,256]{2,1,0:T(8,128)(2,1)} %constant.21.clone.inverse) | copy-start | bytes 1572868
  12.5 1.7 %collective-permute-start.3 = (bf16[136,128]{1,0:T(8,128)(2,1)S(1)}, bf16[136,128]{1,0:T(8,128)(2,1)S(1)}, u32[]{:S(2)}, u32[]{:S(2)}) collective-permute-start(bf16[136,128]{1,0:T(8,128)(2,1)S(1)} %get-tuple-element.28), channel_id=1, source_target_pairs={{0,4},{4,0},{8,12},{12,8},{16,20},{20,16},{24,28},{28,24},{1,5},{5... | collective-permute-start | bytes 104456 | tf_op jit(solution)/shard_map/ppermute | solution.py:367
  14.2 5.9 %collective-permute-start.6 = (bf16[136,128]{1,0:T(8,128)(2,1)S(1)}, bf16[136,128]{1,0:T(8,128)(2,1)S(1)}, u32[]{:S(2)}, u32[]{:S(2)}) collective-permute-start(bf16[136,128]{1,0:T(8,128)(2,1)S(1)} %add_convert_fusion.1), channel_id=1, source_target_pairs={{0,24},{4,28},{8,16},{12,20},{16,8},{20,12},{24,0},{28,4},{1,25},{... | collective-permute-start | bytes 104456 | tf_op jit(solution)/shard_map/ppermute | solution.py:367
  17.8 4.1 %collective-permute-start.5 = (bf16[136,128]{1,0:T(8,128)(2,1)S(1)}, bf16[136,128]{1,0:T(8,128)(2,1)S(1)}, u32[]{:S(2)}, u32[]{:S(2)}) collective-permute-start(bf16[136,128]{1,0:T(8,128)(2,1)S(1)} %add_convert_fusion.1), channel_id=1, source_target_pairs={{0,16},{4,20},{8,24},{12,28},{16,0},{20,4},{24,8},{28,12},{1,17},{... | collective-permute-start | bytes 104456 | tf_op jit(solution)/shard_map/ppermute | solution.py:367
  17.8 4.1 %collective-permute-start.4 = (bf16[136,128]{1,0:T(8,128)(2,1)S(1)}, bf16[136,128]{1,0:T(8,128)(2,1)S(1)}, u32[]{:S(2)}, u32[]{:S(2)}) collective-permute-start(bf16[136,128]{1,0:T(8,128)(2,1)S(1)} %add_convert_fusion.1), channel_id=1, source_target_pairs={{0,8},{4,12},{8,0},{12,4},{16,24},{20,28},{24,16},{28,20},{1,9},{5... | collective-permute-start | bytes 104456 | tf_op jit(solution)/shard_map/ppermute | solution.py:367
  18.2 6.5 %collective-permute-start.10 = (bf16[256,512]{1,0:T(8,128)(2,1)S(1)}, bf16[256,512]{1,0:T(8,128)(2,1)S(1)}, u32[]{:S(2)}, u32[]{:S(2)}) collective-permute-start(bf16[256,512]{1,0:T(8,128)(2,1)S(1)} %get-tuple-element.29), channel_id=1, source_target_pairs={{0,4},{4,8},{8,12},{12,16},{16,20},{20,24},{24,28},{28,0},{1,5},{5... | collective-permute-start | bytes 786440 | tf_op jit(solution)/shard_map/ppermute | solution.py:434
  21.9 4.0 %collective-permute-start.9 = (bf16[136,128]{1,0:T(8,128)(2,1)S(1)}, bf16[136,128]{1,0:T(8,128)(2,1)S(1)}, u32[]{:S(2)}, u32[]{:S(2)}) collective-permute-start(bf16[136,128]{1,0:T(8,128)(2,1)S(1)} %add_convert_fusion), channel_id=1, source_target_pairs={{0,3},{1,2},{2,1},{3,0},{4,7},{5,6},{6,5},{7,4},{8,11},{9,10},{10,... | collective-permute-start | bytes 104456 | tf_op jit(solution)/shard_map/ppermute | solution.py:367
  24.1 2.8 %collective-permute-start.8 = (bf16[136,128]{1,0:T(8,128)(2,1)S(1)}, bf16[136,128]{1,0:T(8,128)(2,1)S(1)}, u32[]{:S(2)}, u32[]{:S(2)}) collective-permute-start(bf16[136,128]{1,0:T(8,128)(2,1)S(1)} %add_convert_fusion), channel_id=1, source_target_pairs={{0,2},{1,3},{2,0},{3,1},{4,6},{5,7},{6,4},{7,5},{8,10},{9,11},{10,... | collective-permute-start | bytes 104456 | tf_op jit(solution)/shard_map/ppermute | solution.py:367
  24.4 3.1 %collective-permute-start.7 = (bf16[136,128]{1,0:T(8,128)(2,1)S(1)}, bf16[136,128]{1,0:T(8,128)(2,1)S(1)}, u32[]{:S(2)}, u32[]{:S(2)}) collective-permute-start(bf16[136,128]{1,0:T(8,128)(2,1)S(1)} %add_convert_fusion), channel_id=1, source_target_pairs={{0,1},{1,0},{2,3},{3,2},{4,5},{5,4},{6,7},{7,6},{8,9},{9,8},{10,11... | collective-permute-start | bytes 104456 | tf_op jit(solution)/shard_map/ppermute | solution.py:367
  27.5 4.3 %collective-permute-start.11 = (bf16[4,136,128]{2,1,0:T(8,128)(2,1)S(1)}, bf16[4,136,128]{2,1,0:T(8,128)(2,1)S(1)}, u32[]{:S(2)}, u32[]{:S(2)}) collective-permute-start(bf16[4,136,128]{2,1,0:T(8,128)(2,1)S(1)} %pad_maximum_fusion.mine), channel_id=1, source_target_pairs={{0,4},{4,0},{8,12},{12,8},{16,20},{20,16},{24,28},{28,24},{1,5},{5... | collective-permute-start | bytes 417800 | tf_op jit(solution)/shard_map/ppermute | solution.py:367
  30.3 1.4 %copy-start.4 = (bf16[2,2,128,256]{3,2,1,0:T(8,128)(2,1)S(1)}, bf16[2,2,128,256]{3,2,1,0:T(8,128)(2,1)}, u32[]{:S(2)}) copy-start(bf16[2,2,128,256]{3,2,1,0:T(8,128)(2,1)} %constant.22.clone.last) | copy-start | bytes 786436

commit v4 on v3

--- a/solution.py
+++ b/solution.py
@@ -56,6 +56,21 @@
         inverse=np.stack(inverse).astype(bf16),
         last=np.stack(last).astype(bf16),
     )
+
+
+def gate_kernel(lengths, strain, gated):
+    blocks, count, order = gated.shape
+    lanes = order // 128
+    start = lax.axis_index("bank") * (count * order)
+    row = lax.broadcasted_iota(jnp.int32, (count, 128), 0)
+    column = lax.broadcasted_iota(jnp.int32, (count, 128), 1)
+    for block in range(blocks):
+        for lane in range(lanes):
+            x = strain[pl.ds(lane * blocks + block, count, stride=lanes * blocks), :]
+            position = start + row * order + lane * 128 + column
+            gated[block, :, lane * 128 : (lane + 1) * 128] = jnp.where(
+                position < lengths[block], x, 0.0
+            ).astype(bf16)
 
 
 def quarters(value):
@@ -109,11 +124,13 @@
         total = total[:, :group] + total[:, group:]
         lanes = group // 128
         for lane in range(lanes):
-            row = (place * lanes + lane) * rows
-            power[row : row + rows, :] = total[:, lane * 128 : (lane + 1) * 128]
+            for h in range(2):
+                row = (h * 4 * lanes + place * lanes + lane) * (rows // 2)
+                piece = total[h * (rows // 2) : (h + 1) * (rows // 2), lane * 128 : (lane + 1) * 128]
+                power[row : row + rows // 2, :] = piece
     chunk = mine.shape[0]
     for dest, which in ((mine, core), (other, 1 - core)):
-        at = pl.multiple_of((bank * 2 + which) * chunk, 8)
+        at = pl.multiple_of(which * (power.shape[0] // 2) + bank * chunk, 8)
         dest[...] = power[pl.ds(at, chunk), :].astype(bf16)
 
 
@@ -371,20 +388,30 @@
     return pltpu.with_memory_space_constraint(value, pltpu.VMEM)
 
 
+def far(value):
+    return pltpu.with_memory_space_constraint(value, pltpu.HBM)
+
+
 def body(strain, lengths, templates):
     blocks_here, local = strain.shape
     count, order = templates.shape[1], templates.shape[-1]
     half = order // 2
     rows = half + 16
     banks, groups = lax.axis_size("bank"), lax.axis_size("tm")
-    bank = lax.axis_index("bank")
     table = tables(order)
     vmem = pl.BlockSpec(memory_space=pltpu.VMEM)
     limit = pltpu.CompilerParams(vmem_limit_bytes=20 * 1024 * 1024)
 
-    index = bank * local + jnp.arange(local, dtype=jnp.int32)
-    valid = index[None, :] < lengths[:, None]
-    gated = jnp.where(valid, strain, 0.0).astype(bf16).reshape(blocks_here, local // order, order)
+    rowwise = jnp.swapaxes(strain.reshape(blocks_here, local // 128, 128), 0, 1)
+    gated = pl.pallas_call(
+        gate_kernel,
+        in_specs=[pl.BlockSpec(memory_space=pltpu.SMEM), vmem],
+        out_specs=vmem,
+        out_shape=pltpu.VMEM((blocks_here, local // order, order), bf16),
+        cost_estimate=pl.CostEstimate(flops=int(1e6), bytes_accessed=int(4e5), transcendentals=0),
+        compiler_params=limit,
+        name="gate",
+    )(far(lengths), far(rowwise.reshape(blocks_here * local // 128, 128)))
     pieces = [gated] + [exchange(gated, "bank", lambda i, s=s: i ^ s) for s in range(1, banks)]
 
     folded, factor = pl.pallas_call(
@@ -403,7 +430,7 @@
         cost_estimate=pl.CostEstimate(flops=int(6e9), bytes_accessed=int(6.5e6), transcendentals=0),
         compiler_params=limit,
         name="fold_templates",
-    )(pltpu.with_memory_space_constraint(templates, pltpu.HBM))
+    )(far(templates))
     *pieces, factor = lax.optimization_barrier((*pieces, factor))
 
     plane = pltpu.VMEM((2, rows, order), bf16)

time: 35.3 us -> 35.1 us (level)
  other arithmetic: 1.25 us -> 0.06 us
  Pallas kernels: 12.5 us -> 13.6 us
    convert_element_type x1 -> x0, other arithmetic: 1.18 us -> none  [body(): jnp.where(valid, strain, 0.0).astype(bf16)]
    pallas_call x0 -> x1, Pallas kernels: none -> 1.02 us  [body(): pl.pallas_call(gate_kernel, in_specs=[pl.BlockSpec(memory_space=pltpu.SME...]
where the time goes in v4:
time: 35.1 us; the launch traced here: 34.9 us
  starting transfers between devices  15.7 us (45%)
  Pallas kernels  13.6 us (39%)
  waiting for transfers between devices  5.46 us (16%)
    ppermute x11, starting transfers between devices, exchange(): return lax.ppermute(values, axis, [(i, pairs_of(i)) for i in range(size)])  13.8 us
    pallas_call x1, Pallas kernels, body(): pl.pallas_call(template_kernel, grid=(count,), in_specs=[pl.BlockSpec((2,...  5.68 us
    ppermute x11, waiting for transfers between devices, exchange(): return lax.ppermute(values, axis, [(i, pairs_of(i)) for i in range(size)])  5.45 us
    pallas_call x1, Pallas kernels, body(): pl.pallas_call(functools.partial(filter_kernel, blocks=blocks), in_specs=...  3.36 us
    ppermute x1, starting transfers between devices, body(): lax.ppermute(last_block, 'tm', [(i, (i + 1) % groups) for i in range(grou...  1.9 us
    pallas_call x1, Pallas kernels, body(): pl.pallas_call(functools.partial(own_rows_kernel, blocks=blocks), in_spec...  1.39 us
    pallas_call x1, Pallas kernels, body(): pl.pallas_call(functools.partial(spectrum_kernel, shards=banks), in_specs...  1.37 us
    pallas_call x1, Pallas kernels, body(): pl.pallas_call(gate_kernel, in_specs=[pl.BlockSpec(memory_space=pltpu.SME...  1.02 us
  transfers between devices with their start and end apart: 12, of which 6 were waited for; matrix products, arithmetic and copies ran while one was open for 0% of the time, Pallas kernels for 22%

profile of v4, /device:TPU:1, one launch (start us, length us, event | category | flops | bytes accessed | tf_op | source)
XLA Modules:
  0.0 34.9 jit_solution(17020893939217280115)
XLA Ops:
  0.0 1.0 %gate.1.refs_0_ = bf16[2,64,512]{2,1,0:T(8,128)(2,1)S(1)} custom-call(s32[2]{0:T(128)} %lengths.1, f32[512,128]{1,0:T(8,128)} %bitcast.14), custom_call_target="tpu_custom_call" | custom-call | flops 1000000 | bytes 400000 | tf_op jit(solution)/shard_map/gate/pallas_call | solution.py:406
  1.0 0.0 copy-start
  1.0 0.0 copy-start.2
  1.1 0.0 copy-start.3
  1.1 3.0 %collective-permute-start.2 = (bf16[2,64,512]{2,1,0:T(8,128)(2,1)S(1)}, bf16[2,64,512]{2,1,0:T(8,128)(2,1)S(1)}, u32[]{:S(2)}, u32[]{:S(2)}) collective-permute-start(bf16[2,64,512]{2,1,0:T(8,128)(2,1)S(1)} %gate.1.refs_0_), channel_id=1, source_target_pairs={{0,3},{1,2},{2,1},{3,0},{4,7},{5,6},{6,5},{7,4},{8,11},{9,10},{10,... | collective-permute-start | bytes 393224 | tf_op jit(solution)/shard_map/ppermute | solution.py:384
  4.1 0.2 collective-permute-start.1
  4.3 0.1 collective-permute-start
  4.5 5.7 %fold_templates.1 = (bf16[4,2,272,512]{3,2,1,0:T(8,128)(2,1)S(1)}, f32[4,8,128]{2,1,0:T(8,128)S(1)}) custom-call(bf16[2,4,512,512]{3,2,1,0:T(8,128)(2,1)} %templates.1), custom_call_target="tpu_custom_call" | custom-call | flops 6000000000 | bytes 6500000 | tf_op jit(solution)/shard_map/fold_templates/pallas_call | solution.py:417
  10.2 0.0 collective-permute-done.2.refs_3_
  10.2 0.7 %collective-permute-done.1.refs_2_ = bf16[2,64,512]{2,1,0:T(8,128)(2,1)S(1)} collective-permute-done((bf16[2,64,512]{2,1,0:T(8,128)(2,1)S(1)}, bf16[2,64,512]{2,1,0:T(8,128)(2,1)S(1)}, u32[]{:S(2)}, u32[]{:S(2)}) %collective-permute-start.1) | collective-permute-done | bytes 131104 | tf_op jit(solution)/shard_map/ppermute | solution.py:384
  10.9 0.0 collective-permute-done.refs_1_
  10.9 0.0 copy-done
  10.9 0.0 copy-done.2
  10.9 0.0 copy-done.3
  10.9 1.4 %spectra.1 = (bf16[2,272,512]{2,1,0:T(8,128)(2,1)S(1)}, bf16[2,272,512]{2,1,0:T(8,128)(2,1)S(1)}, bf16[136,128]{1,0:T(8,128)(2,1)S(1)}, bf16[136,128]{1,0:T(8,128)(2,1)S(1)}, bf16[256,512]{1,0:T(8,128)(2,1)S(1)}) custom-call(bf16[2,64,512]{2,1,0:T(8,128)(2,1)S(1)} %gate.1.refs_0_, bf16[2,64,512]{2,1,0:T(8,128)(2,1)S(1)} %collective-permute-done.refs_1_, ...), custom_call_target="tpu_custom_call" | custom-call | flops 2000000000 | bytes 5000000 | tf_op jit(solution)/shard_map/spectra/pallas_call | solution.py:438
  12.3 0.0 copy-start.1
  12.3 0.8 %collective-permute-start.3 = (bf16[136,128]{1,0:T(8,128)(2,1)S(1)}, bf16[136,128]{1,0:T(8,128)(2,1)S(1)}, u32[]{:S(2)}, u32[]{:S(2)}) collective-permute-start(bf16[136,128]{1,0:T(8,128)(2,1)S(1)} %get-tuple-element.28), channel_id=1, source_target_pairs={{0,4},{4,0},{8,12},{12,8},{16,20},{20,16},{24,28},{28,24},{1,5},{5... | collective-permute-start | bytes 104456 | tf_op jit(solution)/shard_map/ppermute | solution.py:384
  13.1 0.9 %collective-permute-done.3 = bf16[136,128]{1,0:T(8,128)(2,1)S(1)} collective-permute-done((bf16[136,128]{1,0:T(8,128)(2,1)S(1)}, bf16[136,128]{1,0:T(8,128)(2,1)S(1)}, u32[]{:S(2)}, u32[]{:S(2)}) %collective-permute-start.3) | collective-permute-done | bytes 34848 | tf_op jit(solution)/shard_map/ppermute | solution.py:384
  14.0 3.6 %collective-permute-start.6 = (bf16[136,128]{1,0:T(8,128)(2,1)S(1)}, bf16[136,128]{1,0:T(8,128)(2,1)S(1)}, u32[]{:S(2)}, u32[]{:S(2)}) collective-permute-start(bf16[136,128]{1,0:T(8,128)(2,1)S(1)} %add_convert_fusion.1), channel_id=1, source_target_pairs={{0,24},{4,28},{8,16},{12,20},{16,8},{20,12},{24,0},{28,4},{1,25},{... | collective-permute-start | bytes 104456 | tf_op jit(solution)/shard_map/ppermute | solution.py:384
  17.6 0.0 collective-permute-start.5
  17.6 0.4 %collective-permute-start.4 = (bf16[136,128]{1,0:T(8,128)(2,1)S(1)}, bf16[136,128]{1,0:T(8,128)(2,1)S(1)}, u32[]{:S(2)}, u32[]{:S(2)}) collective-permute-start(bf16[136,128]{1,0:T(8,128)(2,1)S(1)} %add_convert_fusion.1), channel_id=1, source_target_pairs={{0,8},{4,12},{8,0},{12,4},{16,24},{20,28},{24,16},{28,20},{1,9},{5... | collective-permute-start | bytes 104456 | tf_op jit(solution)/shard_map/ppermute | solution.py:384
  18.0 1.9 %collective-permute-start.10 = (bf16[256,512]{1,0:T(8,128)(2,1)S(1)}, bf16[256,512]{1,0:T(8,128)(2,1)S(1)}, u32[]{:S(2)}, u32[]{:S(2)}) collective-permute-start(bf16[256,512]{1,0:T(8,128)(2,1)S(1)} %get-tuple-element.29), channel_id=1, source_target_pairs={{0,4},{4,8},{8,12},{12,16},{16,20},{20,24},{24,28},{28,0},{1,5},{5... | collective-permute-start | bytes 786440 | tf_op jit(solution)/shard_map/ppermute | solution.py:461
  19.9 0.0 collective-permute-done.6
  19.9 1.8 %collective-permute-done.5 = bf16[136,128]{1,0:T(8,128)(2,1)S(1)} collective-permute-done((bf16[136,128]{1,0:T(8,128)(2,1)S(1)}, bf16[136,128]{1,0:T(8,128)(2,1)S(1)}, u32[]{:S(2)}, u32[]{:S(2)}) %collective-permute-start.5) | collective-permute-done | bytes 34848 | tf_op jit(solution)/shard_map/ppermute | solution.py:384
  21.7 0.0 collective-permute-done.4
  21.7 2.2 %collective-permute-start.9 = (bf16[136,128]{1,0:T(8,128)(2,1)S(1)}, bf16[136,128]{1,0:T(8,128)(2,1)S(1)}, u32[]{:S(2)}, u32[]{:S(2)}) collective-permute-start(bf16[136,128]{1,0:T(8,128)(2,1)S(1)} %add_convert_fusion), channel_id=1, source_target_pairs={{0,3},{1,2},{2,1},{3,0},{4,7},{5,6},{6,5},{7,4},{8,11},{9,10},{10,... | collective-permute-start | bytes 104456 | tf_op jit(solution)/shard_map/ppermute | solution.py:384
  23.9 0.2 collective-permute-start.8
  24.2 0.3 collective-permute-start.7
  24.4 0.0 collective-permute-done.10.samples
  24.4 0.7 %previous.1.earlier = bf16[2,272,512]{2,1,0:T(8,128)(2,1)S(1)} custom-call(bf16[256,512]{1,0:T(8,128)(2,1)S(1)} %collective-permute-done.10.samples, bf16[2,272,512]{2,1,0:T(8,128)(2,1)S(1)} %get-tuple-element.30.kept, bf16[544,256]{1,0:T(8,128)(2,1)S(1)} %copy-done.3, f32[2,272,512]{2,1,0:T(8,128)S(1)} %copy-done, bf16[4,256,256]{2,1,0:T(8,128)(2,1)S(1)} %copy-done.2), custom_call_target="tpu_custom_call" | custom-call | flops 1000000000 | bytes 4000000 | tf_op jit(solution)/shard_map/previous/pallas_call | solution.py:462
  25.1 0.6 %collective-permute-done.9 = bf16[136,128]{1,0:T(8,128)(2,1)S(1)} collective-permute-done((bf16[136,128]{1,0:T(8,128)(2,1)S(1)}, bf16[136,128]{1,0:T(8,128)(2,1)S(1)}, u32[]{:S(2)}, u32[]{:S(2)}) %collective-permute-start.9) | collective-permute-done | bytes 34848 | tf_op jit(solution)/shard_map/ppermute | solution.py:384
  25.7 1.0 %collective-permute-done.8 = bf16[136,128]{1,0:T(8,128)(2,1)S(1)} collective-permute-done((bf16[136,128]{1,0:T(8,128)(2,1)S(1)}, bf16[136,128]{1,0:T(8,128)(2,1)S(1)}, u32[]{:S(2)}, u32[]{:S(2)}) %collective-permute-start.8) | collective-permute-done | bytes 34848 | tf_op jit(solution)/shard_map/ppermute | solution.py:384
  26.7 0.5 %collective-permute-done.7 = bf16[136,128]{1,0:T(8,128)(2,1)S(1)} collective-permute-done((bf16[136,128]{1,0:T(8,128)(2,1)S(1)}, bf16[136,128]{1,0:T(8,128)(2,1)S(1)}, u32[]{:S(2)}, u32[]{:S(2)}) %collective-permute-start.7) | collective-permute-done | bytes 34848 | tf_op jit(solution)/shard_map/ppermute | solution.py:384
  27.3 2.9 %collective-permute-start.11 = (bf16[4,136,128]{2,1,0:T(8,128)(2,1)S(1)}, bf16[4,136,128]{2,1,0:T(8,128)(2,1)S(1)}, u32[]{:S(2)}, u32[]{:S(2)}) collective-permute-start(bf16[4,136,128]{2,1,0:T(8,128)(2,1)S(1)} %pad_maximum_fusion.mine), channel_id=1, source_target_pairs={{0,4},{4,0},{8,12},{12,8},{16,20},{20,16},{24,28},{28,24},{1,5},{5... | collective-permute-start | bytes 417800 | tf_op jit(solution)/shard_map/ppermute | solution.py:384
  30.1 0.0 copy-done.1
  30.1 0.0 copy-start.4
  30.1 1.4 %own_rows.1.own = bf16[8,2,2,128,256]{4,3,2,1,0:T(8,128)(2,1)S(1)} custom-call(bf16[4,136,128]{2,1,0:T(8,128)(2,1)S(1)} %pad_maximum_fusion.mine, bf16[2,272,512]{2,1,0:T(8,128)(2,1)S(1)} %previous.1.earlier, bf16[2,272,512]{2,1,0:T(8,128)(2,1)S(1)} %get-tuple-element.36.later, bf16[4,2,272,512]{3,2,1,0:T(8,128)(2,1)S(1)} %get-tuple-element.37.folded, ...), custom_call_target="tpu_custom_call" | custom-call | flops 2000000000 | bytes 6000000 | tf_op jit(solution)/shard_map/own_rows/pallas_call | solution.py:479
  31.5 0.0 collective-permute-done.11.theirs
  31.5 0.0 copy-done.4
  31.6 3.4 %filter.1 = f32[256,2,16,1,128]{4,3,2,1,0:T(1,128)} custom-call(bf16[4,136,128]{2,1,0:T(8,128)(2,1)S(1)} %collective-permute-done.11.theirs, bf16[8,2,2,128,256]{4,3,2,1,0:T(8,128)(2,1)S(1)} %own_rows.1.own, bf16[2,272,512]{2,1,0:T(8,128)(2,1)S(1)} %previous.1.earlier, bf16[2,272,512]{2,1,0:T(8,128)(2,1)S(1)} %get-tuple-element.36.later, ...), custom_call_target="tpu_custom_call" | custom-call | flops 6000000000 | bytes 12000000 | tf_op jit(solution)/shard_map/filter/pallas_call | solution.py:489
  (3 shorter events, 0.1 us)
Async XLA Ops:
  1.0 9.8 %copy-start = (f32[2,272,512]{2,1,0:T(8,128)S(1)}, f32[2,272,512]{2,1,0:T(8,128)}, u32[]{:S(2)}) copy-start(f32[2,272,512]{2,1,0:T(8,128)} %constant.11.clone.refs_5_.twist) | copy-start | bytes 3342340
  1.0 9.8 %copy-start.2 = (bf16[4,256,256]{2,1,0:T(8,128)(2,1)S(1)}, bf16[4,256,256]{2,1,0:T(8,128)(2,1)}, u32[]{:S(2)}) copy-start(bf16[4,256,256]{2,1,0:T(8,128)(2,1)} %constant.12.clone.refs_6_.forward) | copy-start | bytes 1572868
  1.1 9.8 %copy-start.3 = (bf16[544,256]{1,0:T(8,128)(2,1)S(1)}, bf16[544,256]{1,0:T(8,128)(2,1)}, u32[]{:S(2)}) copy-start(bf16[544,256]{1,0:T(8,128)(2,1)} %constant.10.clone.refs_4_.first) | copy-start | bytes 835588
  1.1 9.1 %collective-permute-start.2 = (bf16[2,64,512]{2,1,0:T(8,128)(2,1)S(1)}, bf16[2,64,512]{2,1,0:T(8,128)(2,1)S(1)}, u32[]{:S(2)}, u32[]{:S(2)}) collective-permute-start(bf16[2,64,512]{2,1,0:T(8,128)(2,1)S(1)} %gate.1.refs_0_), channel_id=1, source_target_pairs={{0,3},{1,2},{2,1},{3,0},{4,7},{5,6},{6,5},{7,4},{8,11},{9,10},{10,... | collective-permute-start | bytes 393224 | tf_op jit(solution)/shard_map/ppermute | solution.py:384
  4.1 6.7 %collective-permute-start.1 = (bf16[2,64,512]{2,1,0:T(8,128)(2,1)S(1)}, bf16[2,64,512]{2,1,0:T(8,128)(2,1)S(1)}, u32[]{:S(2)}, u32[]{:S(2)}) collective-permute-start(bf16[2,64,512]{2,1,0:T(8,128)(2,1)S(1)} %gate.1.refs_0_), channel_id=1, source_target_pairs={{0,2},{1,3},{2,0},{3,1},{4,6},{5,7},{6,4},{7,5},{8,10},{9,11},{10,... | collective-permute-start | bytes 393224 | tf_op jit(solution)/shard_map/ppermute | solution.py:384
  4.3 6.5 %collective-permute-start = (bf16[2,64,512]{2,1,0:T(8,128)(2,1)S(1)}, bf16[2,64,512]{2,1,0:T(8,128)(2,1)S(1)}, u32[]{:S(2)}, u32[]{:S(2)}) collective-permute-start(bf16[2,64,512]{2,1,0:T(8,128)(2,1)S(1)} %gate.1.refs_0_), channel_id=1, source_target_pairs={{0,1},{1,0},{2,3},{3,2},{4,5},{5,4},{6,7},{7,6},{8,9},{9,8},{10,11... | collective-permute-start | bytes 393224 | tf_op jit(solution)/shard_map/ppermute | solution.py:384
  12.3 17.9 %copy-start.1 = (bf16[4,256,256]{2,1,0:T(8,128)(2,1)S(1)}, bf16[4,256,256]{2,1,0:T(8,128)(2,1)}, u32[]{:S(2)}) copy-start(bf16[4,256,256]{2,1,0:T(8,128)(2,1)} %constant.13.clone.inverse) | copy-start | bytes 1572868
  12.3 1.7 %collective-permute-start.3 = (bf16[136,128]{1,0:T(8,128)(2,1)S(1)}, bf16[136,128]{1,0:T(8,128)(2,1)S(1)}, u32[]{:S(2)}, u32[]{:S(2)}) collective-permute-start(bf16[136,128]{1,0:T(8,128)(2,1)S(1)} %get-tuple-element.28), channel_id=1, source_target_pairs={{0,4},{4,0},{8,12},{12,8},{16,20},{20,16},{24,28},{28,24},{1,5},{5... | collective-permute-start | bytes 104456 | tf_op jit(solution)/shard_map/ppermute | solution.py:384
  14.0 5.9 %collective-permute-start.6 = (bf16[136,128]{1,0:T(8,128)(2,1)S(1)}, bf16[136,128]{1,0:T(8,128)(2,1)S(1)}, u32[]{:S(2)}, u32[]{:S(2)}) collective-permute-start(bf16[136,128]{1,0:T(8,128)(2,1)S(1)} %add_convert_fusion.1), channel_id=1, source_target_pairs={{0,24},{4,28},{8,16},{12,20},{16,8},{20,12},{24,0},{28,4},{1,25},{... | collective-permute-start | bytes 104456 | tf_op jit(solution)/shard_map/ppermute | solution.py:384
  17.6 4.1 %collective-permute-start.5 = (bf16[136,128]{1,0:T(8,128)(2,1)S(1)}, bf16[136,128]{1,0:T(8,128)(2,1)S(1)}, u32[]{:S(2)}, u32[]{:S(2)}) collective-permute-start(bf16[136,128]{1,0:T(8,128)(2,1)S(1)} %add_convert_fusion.1), channel_id=1, source_target_pairs={{0,16},{4,20},{8,24},{12,28},{16,0},{20,4},{24,8},{28,12},{1,17},{... | collective-permute-start | bytes 104456 | tf_op jit(solution)/shard_map/ppermute | solution.py:384
  17.6 4.1 %collective-permute-start.4 = (bf16[136,128]{1,0:T(8,128)(2,1)S(1)}, bf16[136,128]{1,0:T(8,128)(2,1)S(1)}, u32[]{:S(2)}, u32[]{:S(2)}) collective-permute-start(bf16[136,128]{1,0:T(8,128)(2,1)S(1)} %add_convert_fusion.1), channel_id=1, source_target_pairs={{0,8},{4,12},{8,0},{12,4},{16,24},{20,28},{24,16},{28,20},{1,9},{5... | collective-permute-start | bytes 104456 | tf_op jit(solution)/shard_map/ppermute | solution.py:384
  18.0 6.5 %collective-permute-start.10 = (bf16[256,512]{1,0:T(8,128)(2,1)S(1)}, bf16[256,512]{1,0:T(8,128)(2,1)S(1)}, u32[]{:S(2)}, u32[]{:S(2)}) collective-permute-start(bf16[256,512]{1,0:T(8,128)(2,1)S(1)} %get-tuple-element.29), channel_id=1, source_target_pairs={{0,4},{4,8},{8,12},{12,16},{16,20},{20,24},{24,28},{28,0},{1,5},{5... | collective-permute-start | bytes 786440 | tf_op jit(solution)/shard_map/ppermute | solution.py:461
  21.7 4.0 %collective-permute-start.9 = (bf16[136,128]{1,0:T(8,128)(2,1)S(1)}, bf16[136,128]{1,0:T(8,128)(2,1)S(1)}, u32[]{:S(2)}, u32[]{:S(2)}) collective-permute-start(bf16[136,128]{1,0:T(8,128)(2,1)S(1)} %add_convert_fusion), channel_id=1, source_target_pairs={{0,3},{1,2},{2,1},{3,0},{4,7},{5,6},{6,5},{7,4},{8,11},{9,10},{10,... | collective-permute-start | bytes 104456 | tf_op jit(solution)/shard_map/ppermute | solution.py:384
  23.9 2.8 %collective-permute-start.8 = (bf16[136,128]{1,0:T(8,128)(2,1)S(1)}, bf16[136,128]{1,0:T(8,128)(2,1)S(1)}, u32[]{:S(2)}, u32[]{:S(2)}) collective-permute-start(bf16[136,128]{1,0:T(8,128)(2,1)S(1)} %add_convert_fusion), channel_id=1, source_target_pairs={{0,2},{1,3},{2,0},{3,1},{4,6},{5,7},{6,4},{7,5},{8,10},{9,11},{10,... | collective-permute-start | bytes 104456 | tf_op jit(solution)/shard_map/ppermute | solution.py:384
  24.2 3.1 %collective-permute-start.7 = (bf16[136,128]{1,0:T(8,128)(2,1)S(1)}, bf16[136,128]{1,0:T(8,128)(2,1)S(1)}, u32[]{:S(2)}, u32[]{:S(2)}) collective-permute-start(bf16[136,128]{1,0:T(8,128)(2,1)S(1)} %add_convert_fusion), channel_id=1, source_target_pairs={{0,1},{1,0},{2,3},{3,2},{4,5},{5,4},{6,7},{7,6},{8,9},{9,8},{10,11... | collective-permute-start | bytes 104456 | tf_op jit(solution)/shard_map/ppermute | solution.py:384
  27.3 4.3 %collective-permute-start.11 = (bf16[4,136,128]{2,1,0:T(8,128)(2,1)S(1)}, bf16[4,136,128]{2,1,0:T(8,128)(2,1)S(1)}, u32[]{:S(2)}, u32[]{:S(2)}) collective-permute-start(bf16[4,136,128]{2,1,0:T(8,128)(2,1)S(1)} %pad_maximum_fusion.mine), channel_id=1, source_target_pairs={{0,4},{4,0},{8,12},{12,8},{16,20},{20,16},{24,28},{28,24},{1,5},{5... | collective-permute-start | bytes 417800 | tf_op jit(solution)/shard_map/ppermute | solution.py:384
  30.1 1.4 %copy-start.4 = (bf16[2,2,128,256]{3,2,1,0:T(8,128)(2,1)S(1)}, bf16[2,2,128,256]{3,2,1,0:T(8,128)(2,1)}, u32[]{:S(2)}) copy-start(bf16[2,2,128,256]{3,2,1,0:T(8,128)(2,1)} %constant.14.clone.last) | copy-start | bytes 786436

commit v5 on v4

--- a/solution.py
+++ b/solution.py
@@ -454,7 +454,7 @@
     partner = exchange(other, "tm", lambda i: i ^ 1)
     chip = (mine.astype(f32) + partner.astype(f32)).astype(bf16)
     share = chip.astype(f32)
-    for step in range(1, groups // 2):
+    for step in sorted(range(1, groups // 2), key=lambda d: (d ^ 1) if d > 1 else d):
         share = share + exchange(chip, "tm", lambda i, s=step: i ^ (2 * s)).astype(f32)
     share = share.astype(bf16)
 

time: 35.1 us -> 35 us (level)
  waiting for transfers between devices: 5.46 us -> 4.33 us
  starting transfers between devices: 15.7 us -> 16.7 us
    ppermute x11, waiting for transfers between devices: 5.45 us -> 4.33 us  [exchange(): return lax.ppermute(values, axis, [(i, pairs_of(i)) for i in range(size)])]
    ppermute x11, starting transfers between devices: 13.8 us -> 14.4 us  [exchange(): return lax.ppermute(values, axis, [(i, pairs_of(i)) for i in range(size)])]
    ppermute x1, starting transfers between devices: 1.9 us -> 2.31 us  [body(): lax.ppermute(last_block, 'tm', [(i, (i + 1) % groups) for i in range(grou...]
where the time goes in v5:
time: 35 us; the launch traced here: 34.8 us
  starting transfers between devices  16.7 us (48%)
  Pallas kernels  13.6 us (39%)
  waiting for transfers between devices  4.33 us (12%)
    ppermute x11, starting transfers between devices, exchange(): return lax.ppermute(values, axis, [(i, pairs_of(i)) for i in range(size)])  14.4 us
    pallas_call x1, Pallas kernels, body(): pl.pallas_call(template_kernel, grid=(count,), in_specs=[pl.BlockSpec((2,...  5.68 us
    ppermute x11, waiting for transfers between devices, exchange(): return lax.ppermute(values, axis, [(i, pairs_of(i)) for i in range(size)])  4.33 us
    pallas_call x1, Pallas kernels, body(): pl.pallas_call(functools.partial(filter_kernel, blocks=blocks), in_specs=...  3.36 us
    ppermute x1, starting transfers between devices, body(): lax.ppermute(last_block, 'tm', [(i, (i + 1) % groups) for i in range(grou...  2.31 us
    pallas_call x1, Pallas kernels, body(): pl.pallas_call(functools.partial(own_rows_kernel, blocks=blocks), in_spec...  1.4 us
    pallas_call x1, Pallas kernels, body(): pl.pallas_call(functools.partial(spectrum_kernel, shards=banks), in_specs...  1.37 us
    pallas_call x1, Pallas kernels, body(): pl.pallas_call(gate_kernel, in_specs=[pl.BlockSpec(memory_space=pltpu.SME...  1.02 us
  transfers between devices with their start and end apart: 12, of which 6 were waited for; matrix products, arithmetic and copies ran while one was open for 0% of the time, Pallas kernels for 22%

profile of v5, /device:TPU:1, one launch (start us, length us, event | category | flops | bytes accessed | tf_op | source)
XLA Modules:
  0.0 34.8 jit_solution(7360827225941167464)
XLA Ops:
  0.0 1.0 %gate.1.refs_0_ = bf16[2,64,512]{2,1,0:T(8,128)(2,1)S(1)} custom-call(s32[2]{0:T(128)} %lengths.1, f32[512,128]{1,0:T(8,128)} %bitcast.14), custom_call_target="tpu_custom_call" | custom-call | flops 1000000 | bytes 400000 | tf_op jit(solution)/shard_map/gate/pallas_call | solution.py:406
  1.0 0.0 copy-start
  1.0 0.0 copy-start.2
  1.1 0.0 copy-start.3
  1.1 3.0 %collective-permute-start.2 = (bf16[2,64,512]{2,1,0:T(8,128)(2,1)S(1)}, bf16[2,64,512]{2,1,0:T(8,128)(2,1)S(1)}, u32[]{:S(2)}, u32[]{:S(2)}) collective-permute-start(bf16[2,64,512]{2,1,0:T(8,128)(2,1)S(1)} %gate.1.refs_0_), channel_id=1, source_target_pairs={{0,3},{1,2},{2,1},{3,0},{4,7},{5,6},{6,5},{7,4},{8,11},{9,10},{10,... | collective-permute-start | bytes 393224 | tf_op jit(solution)/shard_map/ppermute | solution.py:384
  4.1 0.2 collective-permute-start.1
  4.3 0.1 collective-permute-start
  4.5 5.7 %fold_templates.1 = (bf16[4,2,272,512]{3,2,1,0:T(8,128)(2,1)S(1)}, f32[4,8,128]{2,1,0:T(8,128)S(1)}) custom-call(bf16[2,4,512,512]{3,2,1,0:T(8,128)(2,1)} %templates.1), custom_call_target="tpu_custom_call" | custom-call | flops 6000000000 | bytes 6500000 | tf_op jit(solution)/shard_map/fold_templates/pallas_call | solution.py:417
  10.2 0.0 collective-permute-done.2.refs_3_
  10.2 0.7 %collective-permute-done.1.refs_2_ = bf16[2,64,512]{2,1,0:T(8,128)(2,1)S(1)} collective-permute-done((bf16[2,64,512]{2,1,0:T(8,128)(2,1)S(1)}, bf16[2,64,512]{2,1,0:T(8,128)(2,1)S(1)}, u32[]{:S(2)}, u32[]{:S(2)}) %collective-permute-start.1) | collective-permute-done | bytes 131104 | tf_op jit(solution)/shard_map/ppermute | solution.py:384
  10.9 0.0 collective-permute-done.refs_1_
  10.9 0.0 copy-done
  10.9 0.0 copy-done.2
  10.9 0.0 copy-done.3
  10.9 1.4 %spectra.1 = (bf16[2,272,512]{2,1,0:T(8,128)(2,1)S(1)}, bf16[2,272,512]{2,1,0:T(8,128)(2,1)S(1)}, bf16[136,128]{1,0:T(8,128)(2,1)S(1)}, bf16[136,128]{1,0:T(8,128)(2,1)S(1)}, bf16[256,512]{1,0:T(8,128)(2,1)S(1)}) custom-call(bf16[2,64,512]{2,1,0:T(8,128)(2,1)S(1)} %gate.1.refs_0_, bf16[2,64,512]{2,1,0:T(8,128)(2,1)S(1)} %collective-permute-done.refs_1_, ...), custom_call_target="tpu_custom_call" | custom-call | flops 2000000000 | bytes 5000000 | tf_op jit(solution)/shard_map/spectra/pallas_call | solution.py:438
  12.3 0.0 copy-start.1
  12.3 0.8 %collective-permute-start.3 = (bf16[136,128]{1,0:T(8,128)(2,1)S(1)}, bf16[136,128]{1,0:T(8,128)(2,1)S(1)}, u32[]{:S(2)}, u32[]{:S(2)}) collective-permute-start(bf16[136,128]{1,0:T(8,128)(2,1)S(1)} %get-tuple-element.28), channel_id=1, source_target_pairs={{0,4},{4,0},{8,12},{12,8},{16,20},{20,16},{24,28},{28,24},{1,5},{5... | collective-permute-start | bytes 104456 | tf_op jit(solution)/shard_map/ppermute | solution.py:384
  13.1 0.9 %collective-permute-done.3 = bf16[136,128]{1,0:T(8,128)(2,1)S(1)} collective-permute-done((bf16[136,128]{1,0:T(8,128)(2,1)S(1)}, bf16[136,128]{1,0:T(8,128)(2,1)S(1)}, u32[]{:S(2)}, u32[]{:S(2)}) %collective-permute-start.3) | collective-permute-done | bytes 34848 | tf_op jit(solution)/shard_map/ppermute | solution.py:384
  14.0 2.6 %collective-permute-start.6 = (bf16[136,128]{1,0:T(8,128)(2,1)S(1)}, bf16[136,128]{1,0:T(8,128)(2,1)S(1)}, u32[]{:S(2)}, u32[]{:S(2)}) collective-permute-start(bf16[136,128]{1,0:T(8,128)(2,1)S(1)} %add_convert_fusion.1), channel_id=1, source_target_pairs={{0,16},{4,20},{8,24},{12,28},{16,0},{20,4},{24,8},{28,12},{1,17},{... | collective-permute-start | bytes 104456 | tf_op jit(solution)/shard_map/ppermute | solution.py:384
  16.6 1.1 %collective-permute-start.5 = (bf16[136,128]{1,0:T(8,128)(2,1)S(1)}, bf16[136,128]{1,0:T(8,128)(2,1)S(1)}, u32[]{:S(2)}, u32[]{:S(2)}) collective-permute-start(bf16[136,128]{1,0:T(8,128)(2,1)S(1)} %add_convert_fusion.1), channel_id=1, source_target_pairs={{0,24},{4,28},{8,16},{12,20},{16,8},{20,12},{24,0},{28,4},{1,25},{... | collective-permute-start | bytes 104456 | tf_op jit(solution)/shard_map/ppermute | solution.py:384
  17.7 0.2 collective-permute-start.4
  17.9 2.3 %collective-permute-start.10 = (bf16[256,512]{1,0:T(8,128)(2,1)S(1)}, bf16[256,512]{1,0:T(8,128)(2,1)S(1)}, u32[]{:S(2)}, u32[]{:S(2)}) collective-permute-start(bf16[256,512]{1,0:T(8,128)(2,1)S(1)} %get-tuple-element.29), channel_id=1, source_target_pairs={{0,4},{4,8},{8,12},{12,16},{16,20},{20,24},{24,28},{28,0},{1,5},{5... | collective-permute-start | bytes 786440 | tf_op jit(solution)/shard_map/ppermute | solution.py:461
  20.2 0.0 collective-permute-done.6
  20.2 1.0 %collective-permute-done.5 = bf16[136,128]{1,0:T(8,128)(2,1)S(1)} collective-permute-done((bf16[136,128]{1,0:T(8,128)(2,1)S(1)}, bf16[136,128]{1,0:T(8,128)(2,1)S(1)}, u32[]{:S(2)}, u32[]{:S(2)}) %collective-permute-start.5) | collective-permute-done | bytes 34848 | tf_op jit(solution)/shard_map/ppermute | solution.py:384
  21.2 0.0 collective-permute-done.4
  21.2 2.2 %collective-permute-start.9 = (bf16[136,128]{1,0:T(8,128)(2,1)S(1)}, bf16[136,128]{1,0:T(8,128)(2,1)S(1)}, u32[]{:S(2)}, u32[]{:S(2)}) collective-permute-start(bf16[136,128]{1,0:T(8,128)(2,1)S(1)} %add_convert_fusion), channel_id=1, source_target_pairs={{0,3},{1,2},{2,1},{3,0},{4,7},{5,6},{6,5},{7,4},{8,11},{9,10},{10,... | collective-permute-start | bytes 104456 | tf_op jit(solution)/shard_map/ppermute | solution.py:384
  23.4 0.2 collective-permute-start.8
  23.7 0.3 collective-permute-start.7
  23.9 0.0 collective-permute-done.10.samples
  23.9 0.7 %previous.1.earlier = bf16[2,272,512]{2,1,0:T(8,128)(2,1)S(1)} custom-call(bf16[256,512]{1,0:T(8,128)(2,1)S(1)} %collective-permute-done.10.samples, bf16[2,272,512]{2,1,0:T(8,128)(2,1)S(1)} %get-tuple-element.30.kept, bf16[544,256]{1,0:T(8,128)(2,1)S(1)} %copy-done.3, f32[2,272,512]{2,1,0:T(8,128)S(1)} %copy-done, bf16[4,256,256]{2,1,0:T(8,128)(2,1)S(1)} %copy-done.2), custom_call_target="tpu_custom_call" | custom-call | flops 1000000000 | bytes 4000000 | tf_op jit(solution)/shard_map/previous/pallas_call | solution.py:462
  24.6 0.6 %collective-permute-done.9 = bf16[136,128]{1,0:T(8,128)(2,1)S(1)} collective-permute-done((bf16[136,128]{1,0:T(8,128)(2,1)S(1)}, bf16[136,128]{1,0:T(8,128)(2,1)S(1)}, u32[]{:S(2)}, u32[]{:S(2)}) %collective-permute-start.9) | collective-permute-done | bytes 34848 | tf_op jit(solution)/shard_map/ppermute | solution.py:384
  25.2 1.0 %collective-permute-done.8 = bf16[136,128]{1,0:T(8,128)(2,1)S(1)} collective-permute-done((bf16[136,128]{1,0:T(8,128)(2,1)S(1)}, bf16[136,128]{1,0:T(8,128)(2,1)S(1)}, u32[]{:S(2)}, u32[]{:S(2)}) %collective-permute-start.8) | collective-permute-done | bytes 34848 | tf_op jit(solution)/shard_map/ppermute | solution.py:384
  26.2 0.2 collective-permute-done.7
  26.5 3.5 %collective-permute-start.11 = (bf16[4,136,128]{2,1,0:T(8,128)(2,1)S(1)}, bf16[4,136,128]{2,1,0:T(8,128)(2,1)S(1)}, u32[]{:S(2)}, u32[]{:S(2)}) collective-permute-start(bf16[4,136,128]{2,1,0:T(8,128)(2,1)S(1)} %pad_maximum_fusion.mine), channel_id=1, source_target_pairs={{0,4},{4,0},{8,12},{12,8},{16,20},{20,16},{24,28},{28,24},{1,5},{5... | collective-permute-start | bytes 417800 | tf_op jit(solution)/shard_map/ppermute | solution.py:384
  30.0 0.0 copy-done.1
  30.0 0.0 copy-start.4
  30.0 1.4 %own_rows.1.own = bf16[8,2,2,128,256]{4,3,2,1,0:T(8,128)(2,1)S(1)} custom-call(bf16[4,136,128]{2,1,0:T(8,128)(2,1)S(1)} %pad_maximum_fusion.mine, bf16[2,272,512]{2,1,0:T(8,128)(2,1)S(1)} %previous.1.earlier, bf16[2,272,512]{2,1,0:T(8,128)(2,1)S(1)} %get-tuple-element.36.later, bf16[4,2,272,512]{3,2,1,0:T(8,128)(2,1)S(1)} %get-tuple-element.37.folded, ...), custom_call_target="tpu_custom_call" | custom-call | flops 2000000000 | bytes 6000000 | tf_op jit(solution)/shard_map/own_rows/pallas_call | solution.py:479
  31.4 0.0 collective-permute-done.11.theirs
  31.4 0.0 copy-done.4
  31.5 3.4 %filter.1 = f32[256,2,16,1,128]{4,3,2,1,0:T(1,128)} custom-call(bf16[4,136,128]{2,1,0:T(8,128)(2,1)S(1)} %collective-permute-done.11.theirs, bf16[8,2,2,128,256]{4,3,2,1,0:T(8,128)(2,1)S(1)} %own_rows.1.own, bf16[2,272,512]{2,1,0:T(8,128)(2,1)S(1)} %previous.1.earlier, bf16[2,272,512]{2,1,0:T(8,128)(2,1)S(1)} %get-tuple-element.36.later, ...), custom_call_target="tpu_custom_call" | custom-call | flops 6000000000 | bytes 12000000 | tf_op jit(solution)/shard_map/filter/pallas_call | solution.py:489
  (3 shorter events, 0.1 us)
Async XLA Ops:
  1.0 9.8 %copy-start = (f32[2,272,512]{2,1,0:T(8,128)S(1)}, f32[2,272,512]{2,1,0:T(8,128)}, u32[]{:S(2)}) copy-start(f32[2,272,512]{2,1,0:T(8,128)} %constant.11.clone.refs_5_.twist) | copy-start | bytes 3342340
  1.0 9.8 %copy-start.2 = (bf16[4,256,256]{2,1,0:T(8,128)(2,1)S(1)}, bf16[4,256,256]{2,1,0:T(8,128)(2,1)}, u32[]{:S(2)}) copy-start(bf16[4,256,256]{2,1,0:T(8,128)(2,1)} %constant.12.clone.refs_6_.forward) | copy-start | bytes 1572868
  1.1 9.8 %copy-start.3 = (bf16[544,256]{1,0:T(8,128)(2,1)S(1)}, bf16[544,256]{1,0:T(8,128)(2,1)}, u32[]{:S(2)}) copy-start(bf16[544,256]{1,0:T(8,128)(2,1)} %constant.10.clone.refs_4_.first) | copy-start | bytes 835588
  1.1 9.1 %collective-permute-start.2 = (bf16[2,64,512]{2,1,0:T(8,128)(2,1)S(1)}, bf16[2,64,512]{2,1,0:T(8,128)(2,1)S(1)}, u32[]{:S(2)}, u32[]{:S(2)}) collective-permute-start(bf16[2,64,512]{2,1,0:T(8,128)(2,1)S(1)} %gate.1.refs_0_), channel_id=1, source_target_pairs={{0,3},{1,2},{2,1},{3,0},{4,7},{5,6},{6,5},{7,4},{8,11},{9,10},{10,... | collective-permute-start | bytes 393224 | tf_op jit(solution)/shard_map/ppermute | solution.py:384
  4.1 6.7 %collective-permute-start.1 = (bf16[2,64,512]{2,1,0:T(8,128)(2,1)S(1)}, bf16[2,64,512]{2,1,0:T(8,128)(2,1)S(1)}, u32[]{:S(2)}, u32[]{:S(2)}) collective-permute-start(bf16[2,64,512]{2,1,0:T(8,128)(2,1)S(1)} %gate.1.refs_0_), channel_id=1, source_target_pairs={{0,2},{1,3},{2,0},{3,1},{4,6},{5,7},{6,4},{7,5},{8,10},{9,11},{10,... | collective-permute-start | bytes 393224 | tf_op jit(solution)/shard_map/ppermute | solution.py:384
  4.3 6.5 %collective-permute-start = (bf16[2,64,512]{2,1,0:T(8,128)(2,1)S(1)}, bf16[2,64,512]{2,1,0:T(8,128)(2,1)S(1)}, u32[]{:S(2)}, u32[]{:S(2)}) collective-permute-start(bf16[2,64,512]{2,1,0:T(8,128)(2,1)S(1)} %gate.1.refs_0_), channel_id=1, source_target_pairs={{0,1},{1,0},{2,3},{3,2},{4,5},{5,4},{6,7},{7,6},{8,9},{9,8},{10,11... | collective-permute-start | bytes 393224 | tf_op jit(solution)/shard_map/ppermute | solution.py:384
  12.3 17.8 %copy-start.1 = (bf16[4,256,256]{2,1,0:T(8,128)(2,1)S(1)}, bf16[4,256,256]{2,1,0:T(8,128)(2,1)}, u32[]{:S(2)}) copy-start(bf16[4,256,256]{2,1,0:T(8,128)(2,1)} %constant.13.clone.inverse) | copy-start | bytes 1572868
  12.3 1.7 %collective-permute-start.3 = (bf16[136,128]{1,0:T(8,128)(2,1)S(1)}, bf16[136,128]{1,0:T(8,128)(2,1)S(1)}, u32[]{:S(2)}, u32[]{:S(2)}) collective-permute-start(bf16[136,128]{1,0:T(8,128)(2,1)S(1)} %get-tuple-element.28), channel_id=1, source_target_pairs={{0,4},{4,0},{8,12},{12,8},{16,20},{20,16},{24,28},{28,24},{1,5},{5... | collective-permute-start | bytes 104456 | tf_op jit(solution)/shard_map/ppermute | solution.py:384
  14.0 6.2 %collective-permute-start.6 = (bf16[136,128]{1,0:T(8,128)(2,1)S(1)}, bf16[136,128]{1,0:T(8,128)(2,1)S(1)}, u32[]{:S(2)}, u32[]{:S(2)}) collective-permute-start(bf16[136,128]{1,0:T(8,128)(2,1)S(1)} %add_convert_fusion.1), channel_id=1, source_target_pairs={{0,16},{4,20},{8,24},{12,28},{16,0},{20,4},{24,8},{28,12},{1,17},{... | collective-permute-start | bytes 104456 | tf_op jit(solution)/shard_map/ppermute | solution.py:384
  16.6 4.6 %collective-permute-start.5 = (bf16[136,128]{1,0:T(8,128)(2,1)S(1)}, bf16[136,128]{1,0:T(8,128)(2,1)S(1)}, u32[]{:S(2)}, u32[]{:S(2)}) collective-permute-start(bf16[136,128]{1,0:T(8,128)(2,1)S(1)} %add_convert_fusion.1), channel_id=1, source_target_pairs={{0,24},{4,28},{8,16},{12,20},{16,8},{20,12},{24,0},{28,4},{1,25},{... | collective-permute-start | bytes 104456 | tf_op jit(solution)/shard_map/ppermute | solution.py:384
  17.7 3.5 %collective-permute-start.4 = (bf16[136,128]{1,0:T(8,128)(2,1)S(1)}, bf16[136,128]{1,0:T(8,128)(2,1)S(1)}, u32[]{:S(2)}, u32[]{:S(2)}) collective-permute-start(bf16[136,128]{1,0:T(8,128)(2,1)S(1)} %add_convert_fusion.1), channel_id=1, source_target_pairs={{0,8},{4,12},{8,0},{12,4},{16,24},{20,28},{24,16},{28,20},{1,9},{5... | collective-permute-start | bytes 104456 | tf_op jit(solution)/shard_map/ppermute | solution.py:384
  17.9 6.0 %collective-permute-start.10 = (bf16[256,512]{1,0:T(8,128)(2,1)S(1)}, bf16[256,512]{1,0:T(8,128)(2,1)S(1)}, u32[]{:S(2)}, u32[]{:S(2)}) collective-permute-start(bf16[256,512]{1,0:T(8,128)(2,1)S(1)} %get-tuple-element.29), channel_id=1, source_target_pairs={{0,4},{4,8},{8,12},{12,16},{16,20},{20,24},{24,28},{28,0},{1,5},{5... | collective-permute-start | bytes 786440 | tf_op jit(solution)/shard_map/ppermute | solution.py:461
  21.2 4.0 %collective-permute-start.9 = (bf16[136,128]{1,0:T(8,128)(2,1)S(1)}, bf16[136,128]{1,0:T(8,128)(2,1)S(1)}, u32[]{:S(2)}, u32[]{:S(2)}) collective-permute-start(bf16[136,128]{1,0:T(8,128)(2,1)S(1)} %add_convert_fusion), channel_id=1, source_target_pairs={{0,3},{1,2},{2,1},{3,0},{4,7},{5,6},{6,5},{7,4},{8,11},{9,10},{10,... | collective-permute-start | bytes 104456 | tf_op jit(solution)/shard_map/ppermute | solution.py:384
  23.4 2.8 %collective-permute-start.8 = (bf16[136,128]{1,0:T(8,128)(2,1)S(1)}, bf16[136,128]{1,0:T(8,128)(2,1)S(1)}, u32[]{:S(2)}, u32[]{:S(2)}) collective-permute-start(bf16[136,128]{1,0:T(8,128)(2,1)S(1)} %add_convert_fusion), channel_id=1, source_target_pairs={{0,2},{1,3},{2,0},{3,1},{4,6},{5,7},{6,4},{7,5},{8,10},{9,11},{10,... | collective-permute-start | bytes 104456 | tf_op jit(solution)/shard_map/ppermute | solution.py:384
  23.7 2.8 %collective-permute-start.7 = (bf16[136,128]{1,0:T(8,128)(2,1)S(1)}, bf16[136,128]{1,0:T(8,128)(2,1)S(1)}, u32[]{:S(2)}, u32[]{:S(2)}) collective-permute-start(bf16[136,128]{1,0:T(8,128)(2,1)S(1)} %add_convert_fusion), channel_id=1, source_target_pairs={{0,1},{1,0},{2,3},{3,2},{4,5},{5,4},{6,7},{7,6},{8,9},{9,8},{10,11... | collective-permute-start | bytes 104456 | tf_op jit(solution)/shard_map/ppermute | solution.py:384
  26.5 5.0 %collective-permute-start.11 = (bf16[4,136,128]{2,1,0:T(8,128)(2,1)S(1)}, bf16[4,136,128]{2,1,0:T(8,128)(2,1)S(1)}, u32[]{:S(2)}, u32[]{:S(2)}) collective-permute-start(bf16[4,136,128]{2,1,0:T(8,128)(2,1)S(1)} %pad_maximum_fusion.mine), channel_id=1, source_target_pairs={{0,4},{4,0},{8,12},{12,8},{16,20},{20,16},{24,28},{28,24},{1,5},{5... | collective-permute-start | bytes 417800 | tf_op jit(solution)/shard_map/ppermute | solution.py:384
  30.0 1.4 %copy-start.4 = (bf16[2,2,128,256]{3,2,1,0:T(8,128)(2,1)S(1)}, bf16[2,2,128,256]{3,2,1,0:T(8,128)(2,1)}, u32[]{:S(2)}) copy-start(bf16[2,2,128,256]{3,2,1,0:T(8,128)(2,1)} %constant.14.clone.last) | copy-start | bytes 786436

commit v6 on v5

--- a/solution.py
+++ b/solution.py
@@ -134,7 +134,8 @@
         dest[...] = power[pl.ds(at, chunk), :].astype(bf16)
 
 
-def previous_kernel(samples, kept, first, twist, forward, summed):
+def previous_kernel(samples, kept, first, twist, forward, summed, narrow):
+    narrow[...] = twist[...].astype(bf16)
     group = forward.shape[1] // 2
     follows = lax.axis_index("tm") > 0
     parts = spectrum(jnp.where(follows, samples[...].astype(f32), 0.0).astype(bf16), first, twist, forward)
@@ -261,13 +262,13 @@
 
 
 def own_rows_kernel(
-    mine, earlier, later, folded, twist, inverse, back, weight, white, turn, even_sums, odd_sums, *, blocks
+    mine, earlier, later, folded, twist, inverse, back, weight, white, even_sums, odd_sums, *, blocks
 ):
     chunk, count = white.shape[2], folded.shape[0]
     core = lax.rem(lax.axis_index("tm"), 2)
     here = pl.ds(pl.multiple_of(core * chunk, 8), chunk)
     fill_weights(mine, weight, blocks)
-    turn[...] = twist[:, here, :].astype(bf16)
+    turn = twist.at[:, here]
     total = 2 * count
     for slot in range(total + 1):
         for j in range(2):
@@ -294,7 +295,6 @@
     return [
         pltpu.VMEM((rows // 2 * order // 128, 128), f32),
         pltpu.VMEM((blocks, 2, rows // 2, order), bf16),
-        pltpu.VMEM((2, rows // 2, order), bf16),
         pltpu.VMEM((4, rows // 2, half), bf16),
         pltpu.VMEM((4, rows // 2, half), bf16),
     ]
@@ -312,7 +312,7 @@
 
 def filter_kernel(
     theirs, own, earlier, later, folded, factor, twist, inverse, last, out,
-    weight, white, turn, even_sums, odd_sums, even_back, odd_back, result, sems, *, blocks
+    weight, white, even_sums, odd_sums, even_back, odd_back, result, sems, *, blocks
 ):
     group = last.shape[2]
     half, order = 2 * group, 4 * group
@@ -321,7 +321,7 @@
     core = lax.rem(lax.axis_index("tm"), 2)
     there = pl.ds(pl.multiple_of((1 - core) * chunk, 8), chunk)
     fill_weights(theirs, weight, blocks)
-    turn[...] = twist[:, there, :].astype(bf16)
+    turn = twist.at[:, there]
 
     def copies(slot):
         block, template = divmod(slot, count)
@@ -459,11 +459,11 @@
     share = share.astype(bf16)
 
     before = lax.ppermute(last_block, "tm", [(i, (i + 1) % groups) for i in range(groups)])
-    earlier = pl.pallas_call(
+    earlier, narrow = pl.pallas_call(
         previous_kernel,
         in_specs=[vmem] * 5,
-        out_specs=vmem,
-        out_shape=plane,
+        out_specs=[vmem] * 2,
+        out_shape=[plane, plane],
         cost_estimate=pl.CostEstimate(flops=int(1e9), bytes_accessed=int(4e6), transcendentals=0),
         compiler_params=limit,
         name="previous",
@@ -485,7 +485,7 @@
         cost_estimate=pl.CostEstimate(flops=int(2e9), bytes_accessed=int(6e6), transcendentals=0),
         compiler_params=limit,
         name="own_rows",
-    )(near(mine), near(earlier), near(later), near(folded), table["twist"], table["inverse"])
+    )(near(mine), near(earlier), near(later), near(folded), near(narrow), table["inverse"])
     out = pl.pallas_call(
         functools.partial(filter_kernel, blocks=blocks),
         in_specs=[vmem] * 9,
@@ -497,7 +497,7 @@
         name="filter",
     )(
         near(theirs), near(own), near(earlier), near(later), near(folded), near(factor),
-        table["twist"], table["inverse"], table["last"],
+        near(narrow), table["inverse"], table["last"],
     )
     split = out.reshape(blocks_here * half * lanes, count, 128)
     return jnp.swapaxes(split, 0, 1).reshape(count, blocks_here * half * order)

time: 35 us -> 35.2 us (level)
  transfers between devices with their start and end apart: 12 -> 12, of which waited for: 6 -> 6; matrix products, arithmetic and copies ran while one was open for 0% -> 0% of each run, Pallas kernels for 22% -> 23%
where the time goes in v6:
time: 35.2 us; the launch traced here: 35 us
  starting transfers between devices  16.7 us (47%)
  Pallas kernels  13.8 us (39%)
  waiting for transfers between devices  4.3 us (12%)
    ppermute x11, starting transfers between devices, exchange(): return lax.ppermute(values, axis, [(i, pairs_of(i)) for i in range(size)])  14.4 us
    pallas_call x1, Pallas kernels, body(): pl.pallas_call(template_kernel, grid=(count,), in_specs=[pl.BlockSpec((2,...  5.68 us
    ppermute x11, waiting for transfers between devices, exchange(): return lax.ppermute(values, axis, [(i, pairs_of(i)) for i in range(size)])  4.3 us
    pallas_call x1, Pallas kernels, body(): pl.pallas_call(functools.partial(filter_kernel, blocks=blocks), in_specs=...  3.37 us
    ppermute x1, starting transfers between devices, body(): lax.ppermute(last_block, 'tm', [(i, (i + 1) % groups) for i in range(grou...  2.31 us
    pallas_call x1, Pallas kernels, body(): pl.pallas_call(functools.partial(own_rows_kernel, blocks=blocks), in_spec...  1.5 us
    pallas_call x1, Pallas kernels, body(): pl.pallas_call(functools.partial(spectrum_kernel, shards=banks), in_specs...  1.42 us
    pallas_call x1, Pallas kernels, body(): pl.pallas_call(gate_kernel, in_specs=[pl.BlockSpec(memory_space=pltpu.SME...  1.02 us
  transfers between devices with their start and end apart: 12, of which 6 were waited for; matrix products, arithmetic and copies ran while one was open for 0% of the time, Pallas kernels for 23%

profile of v6, /device:TPU:1, one launch (start us, length us, event | category | flops | bytes accessed | tf_op | source)
XLA Modules:
  0.0 35.0 jit_solution(12541639474111206808)
XLA Ops:
  0.0 1.0 %gate.1.refs_0_ = bf16[2,64,512]{2,1,0:T(8,128)(2,1)S(1)} custom-call(s32[2]{0:T(128)} %lengths.1, f32[512,128]{1,0:T(8,128)} %bitcast.14), custom_call_target="tpu_custom_call" | custom-call | flops 1000000 | bytes 400000 | tf_op jit(solution)/shard_map/gate/pallas_call | solution.py:406
  1.0 0.0 copy-start
  1.0 0.0 copy-start.2
  1.1 0.0 copy-start.3
  1.1 3.0 %collective-permute-start.2 = (bf16[2,64,512]{2,1,0:T(8,128)(2,1)S(1)}, bf16[2,64,512]{2,1,0:T(8,128)(2,1)S(1)}, u32[]{:S(2)}, u32[]{:S(2)}) collective-permute-start(bf16[2,64,512]{2,1,0:T(8,128)(2,1)S(1)} %gate.1.refs_0_), channel_id=1, source_target_pairs={{0,3},{1,2},{2,1},{3,0},{4,7},{5,6},{6,5},{7,4},{8,11},{9,10},{10,... | collective-permute-start | bytes 393224 | tf_op jit(solution)/shard_map/ppermute | solution.py:384
  4.1 0.2 collective-permute-start.1
  4.3 0.1 collective-permute-start
  4.5 5.7 %fold_templates.1 = (bf16[4,2,272,512]{3,2,1,0:T(8,128)(2,1)S(1)}, f32[4,8,128]{2,1,0:T(8,128)S(1)}) custom-call(bf16[2,4,512,512]{3,2,1,0:T(8,128)(2,1)} %templates.1), custom_call_target="tpu_custom_call" | custom-call | flops 6000000000 | bytes 6500000 | tf_op jit(solution)/shard_map/fold_templates/pallas_call | solution.py:417
  10.2 0.0 collective-permute-done.2.refs_3_
  10.2 0.7 %collective-permute-done.1.refs_2_ = bf16[2,64,512]{2,1,0:T(8,128)(2,1)S(1)} collective-permute-done((bf16[2,64,512]{2,1,0:T(8,128)(2,1)S(1)}, bf16[2,64,512]{2,1,0:T(8,128)(2,1)S(1)}, u32[]{:S(2)}, u32[]{:S(2)}) %collective-permute-start.1) | collective-permute-done | bytes 131104 | tf_op jit(solution)/shard_map/ppermute | solution.py:384
  10.9 0.0 collective-permute-done.refs_1_
  10.9 0.0 copy-done
  10.9 0.0 copy-done.2
  10.9 0.0 copy-done.3
  10.9 1.4 %spectra.1 = (bf16[2,272,512]{2,1,0:T(8,128)(2,1)S(1)}, bf16[2,272,512]{2,1,0:T(8,128)(2,1)S(1)}, bf16[136,128]{1,0:T(8,128)(2,1)S(1)}, bf16[136,128]{1,0:T(8,128)(2,1)S(1)}, bf16[256,512]{1,0:T(8,128)(2,1)S(1)}) custom-call(bf16[2,64,512]{2,1,0:T(8,128)(2,1)S(1)} %gate.1.refs_0_, bf16[2,64,512]{2,1,0:T(8,128)(2,1)S(1)} %collective-permute-done.refs_1_, ...), custom_call_target="tpu_custom_call" | custom-call | flops 2000000000 | bytes 5000000 | tf_op jit(solution)/shard_map/spectra/pallas_call | solution.py:438
  12.3 0.0 copy-start.1
  12.3 0.8 %collective-permute-start.3 = (bf16[136,128]{1,0:T(8,128)(2,1)S(1)}, bf16[136,128]{1,0:T(8,128)(2,1)S(1)}, u32[]{:S(2)}, u32[]{:S(2)}) collective-permute-start(bf16[136,128]{1,0:T(8,128)(2,1)S(1)} %get-tuple-element.30), channel_id=1, source_target_pairs={{0,4},{4,0},{8,12},{12,8},{16,20},{20,16},{24,28},{28,24},{1,5},{5... | collective-permute-start | bytes 104456 | tf_op jit(solution)/shard_map/ppermute | solution.py:384
  13.2 0.9 %collective-permute-done.3 = bf16[136,128]{1,0:T(8,128)(2,1)S(1)} collective-permute-done((bf16[136,128]{1,0:T(8,128)(2,1)S(1)}, bf16[136,128]{1,0:T(8,128)(2,1)S(1)}, u32[]{:S(2)}, u32[]{:S(2)}) %collective-permute-start.3) | collective-permute-done | bytes 34848 | tf_op jit(solution)/shard_map/ppermute | solution.py:384
  14.0 2.6 %collective-permute-start.6 = (bf16[136,128]{1,0:T(8,128)(2,1)S(1)}, bf16[136,128]{1,0:T(8,128)(2,1)S(1)}, u32[]{:S(2)}, u32[]{:S(2)}) collective-permute-start(bf16[136,128]{1,0:T(8,128)(2,1)S(1)} %add_convert_fusion.1), channel_id=1, source_target_pairs={{0,16},{4,20},{8,24},{12,28},{16,0},{20,4},{24,8},{28,12},{1,17},{... | collective-permute-start | bytes 104456 | tf_op jit(solution)/shard_map/ppermute | solution.py:384
  16.6 1.1 %collective-permute-start.5 = (bf16[136,128]{1,0:T(8,128)(2,1)S(1)}, bf16[136,128]{1,0:T(8,128)(2,1)S(1)}, u32[]{:S(2)}, u32[]{:S(2)}) collective-permute-start(bf16[136,128]{1,0:T(8,128)(2,1)S(1)} %add_convert_fusion.1), channel_id=1, source_target_pairs={{0,24},{4,28},{8,16},{12,20},{16,8},{20,12},{24,0},{28,4},{1,25},{... | collective-permute-start | bytes 104456 | tf_op jit(solution)/shard_map/ppermute | solution.py:384
  17.7 0.2 collective-permute-start.4
  17.9 2.3 %collective-permute-start.10 = (bf16[256,512]{1,0:T(8,128)(2,1)S(1)}, bf16[256,512]{1,0:T(8,128)(2,1)S(1)}, u32[]{:S(2)}, u32[]{:S(2)}) collective-permute-start(bf16[256,512]{1,0:T(8,128)(2,1)S(1)} %get-tuple-element.31), channel_id=1, source_target_pairs={{0,4},{4,8},{8,12},{12,16},{16,20},{20,24},{24,28},{28,0},{1,5},{5... | collective-permute-start | bytes 786440 | tf_op jit(solution)/shard_map/ppermute | solution.py:461
  20.2 0.0 collective-permute-done.6
  20.2 1.0 %collective-permute-done.5 = bf16[136,128]{1,0:T(8,128)(2,1)S(1)} collective-permute-done((bf16[136,128]{1,0:T(8,128)(2,1)S(1)}, bf16[136,128]{1,0:T(8,128)(2,1)S(1)}, u32[]{:S(2)}, u32[]{:S(2)}) %collective-permute-start.5) | collective-permute-done | bytes 34848 | tf_op jit(solution)/shard_map/ppermute | solution.py:384
  21.2 0.0 collective-permute-done.4
  21.3 2.2 %collective-permute-start.9 = (bf16[136,128]{1,0:T(8,128)(2,1)S(1)}, bf16[136,128]{1,0:T(8,128)(2,1)S(1)}, u32[]{:S(2)}, u32[]{:S(2)}) collective-permute-start(bf16[136,128]{1,0:T(8,128)(2,1)S(1)} %add_convert_fusion), channel_id=1, source_target_pairs={{0,3},{1,2},{2,1},{3,0},{4,7},{5,6},{6,5},{7,4},{8,11},{9,10},{10,... | collective-permute-start | bytes 104456 | tf_op jit(solution)/shard_map/ppermute | solution.py:384
  23.5 0.2 collective-permute-start.8
  23.7 0.3 collective-permute-start.7
  24.0 0.0 collective-permute-done.10.samples
  24.0 0.8 %previous.1 = (bf16[2,272,512]{2,1,0:T(8,128)(2,1)S(1)}, bf16[2,272,512]{2,1,0:T(8,128)(2,1)S(1)}) custom-call(bf16[256,512]{1,0:T(8,128)(2,1)S(1)} %collective-permute-done.10.samples, bf16[2,272,512]{2,1,0:T(8,128)(2,1)S(1)} %get-tuple-element.32.kept, bf16[544,256]{1,0:T(8,128)(2,1)S(1)} %copy-done.3, f32[2,272,512]{2,1,0:T(8,128)S(1)} %copy-done, ...), custom_call_target="tpu_custom_call" | custom-call | flops 1000000000 | bytes 4000000 | tf_op jit(solution)/shard_map/previous/pallas_call | solution.py:462
  24.7 0.6 %collective-permute-done.9 = bf16[136,128]{1,0:T(8,128)(2,1)S(1)} collective-permute-done((bf16[136,128]{1,0:T(8,128)(2,1)S(1)}, bf16[136,128]{1,0:T(8,128)(2,1)S(1)}, u32[]{:S(2)}, u32[]{:S(2)}) %collective-permute-start.9) | collective-permute-done | bytes 34848 | tf_op jit(solution)/shard_map/ppermute | solution.py:384
  25.3 1.0 %collective-permute-done.8 = bf16[136,128]{1,0:T(8,128)(2,1)S(1)} collective-permute-done((bf16[136,128]{1,0:T(8,128)(2,1)S(1)}, bf16[136,128]{1,0:T(8,128)(2,1)S(1)}, u32[]{:S(2)}, u32[]{:S(2)}) %collective-permute-start.8) | collective-permute-done | bytes 34848 | tf_op jit(solution)/shard_map/ppermute | solution.py:384
  26.3 0.2 collective-permute-done.7
  26.5 3.5 %collective-permute-start.11 = (bf16[4,136,128]{2,1,0:T(8,128)(2,1)S(1)}, bf16[4,136,128]{2,1,0:T(8,128)(2,1)S(1)}, u32[]{:S(2)}, u32[]{:S(2)}) collective-permute-start(bf16[4,136,128]{2,1,0:T(8,128)(2,1)S(1)} %pad_maximum_fusion.mine), channel_id=1, source_target_pairs={{0,4},{4,0},{8,12},{12,8},{16,20},{20,16},{24,28},{28,24},{1,5},{5... | collective-permute-start | bytes 417800 | tf_op jit(solution)/shard_map/ppermute | solution.py:384
  30.1 0.0 copy-done.1
  30.1 0.0 copy-start.4
  30.1 1.5 %own_rows.1.own = bf16[8,2,2,128,256]{4,3,2,1,0:T(8,128)(2,1)S(1)} custom-call(bf16[4,136,128]{2,1,0:T(8,128)(2,1)S(1)} %pad_maximum_fusion.mine, bf16[2,272,512]{2,1,0:T(8,128)(2,1)S(1)} %get-tuple-element.38.earlier, bf16[2,272,512]{2,1,0:T(8,128)(2,1)S(1)} %get-tuple-element.39.later, bf16[4,2,272,512]{3,2,1,0:T(8,128)(2,1)S(1)} %get-tuple-element.40.folded, ...), custom_call_target="tpu_custom_call" | custom-call | flops 2000000000 | bytes 6000000 | tf_op jit(solution)/shard_map/own_rows/pallas_call | solution.py:479
  31.6 0.0 collective-permute-done.11.theirs
  31.6 0.0 copy-done.4
  31.6 3.4 %filter.1 = f32[256,2,16,1,128]{4,3,2,1,0:T(1,128)} custom-call(bf16[4,136,128]{2,1,0:T(8,128)(2,1)S(1)} %collective-permute-done.11.theirs, bf16[8,2,2,128,256]{4,3,2,1,0:T(8,128)(2,1)S(1)} %own_rows.1.own, bf16[2,272,512]{2,1,0:T(8,128)(2,1)S(1)} %get-tuple-element.38.earlier, bf16[2,272,512]{2,1,0:T(8,128)(2,1)S(1)} %get-tuple-element.39.later, ...), custom_call_target="tpu_custom_call" | custom-call | flops 6000000000 | bytes 12000000 | tf_op jit(solution)/shard_map/filter/pallas_call | solution.py:489
  (3 shorter events, 0.1 us)
Async XLA Ops:
  1.0 9.8 %copy-start = (f32[2,272,512]{2,1,0:T(8,128)S(1)}, f32[2,272,512]{2,1,0:T(8,128)}, u32[]{:S(2)}) copy-start(f32[2,272,512]{2,1,0:T(8,128)} %constant.11.clone.refs_5_.twist) | copy-start | bytes 3342340
  1.0 9.8 %copy-start.2 = (bf16[4,256,256]{2,1,0:T(8,128)(2,1)S(1)}, bf16[4,256,256]{2,1,0:T(8,128)(2,1)}, u32[]{:S(2)}) copy-start(bf16[4,256,256]{2,1,0:T(8,128)(2,1)} %constant.12.clone.refs_6_.forward) | copy-start | bytes 1572868
  1.1 9.8 %copy-start.3 = (bf16[544,256]{1,0:T(8,128)(2,1)S(1)}, bf16[544,256]{1,0:T(8,128)(2,1)}, u32[]{:S(2)}) copy-start(bf16[544,256]{1,0:T(8,128)(2,1)} %constant.10.clone.refs_4_.first) | copy-start | bytes 835588
  1.1 9.1 %collective-permute-start.2 = (bf16[2,64,512]{2,1,0:T(8,128)(2,1)S(1)}, bf16[2,64,512]{2,1,0:T(8,128)(2,1)S(1)}, u32[]{:S(2)}, u32[]{:S(2)}) collective-permute-start(bf16[2,64,512]{2,1,0:T(8,128)(2,1)S(1)} %gate.1.refs_0_), channel_id=1, source_target_pairs={{0,3},{1,2},{2,1},{3,0},{4,7},{5,6},{6,5},{7,4},{8,11},{9,10},{10,... | collective-permute-start | bytes 393224 | tf_op jit(solution)/shard_map/ppermute | solution.py:384
  4.1 6.7 %collective-permute-start.1 = (bf16[2,64,512]{2,1,0:T(8,128)(2,1)S(1)}, bf16[2,64,512]{2,1,0:T(8,128)(2,1)S(1)}, u32[]{:S(2)}, u32[]{:S(2)}) collective-permute-start(bf16[2,64,512]{2,1,0:T(8,128)(2,1)S(1)} %gate.1.refs_0_), channel_id=1, source_target_pairs={{0,2},{1,3},{2,0},{3,1},{4,6},{5,7},{6,4},{7,5},{8,10},{9,11},{10,... | collective-permute-start | bytes 393224 | tf_op jit(solution)/shard_map/ppermute | solution.py:384
  4.3 6.5 %collective-permute-start = (bf16[2,64,512]{2,1,0:T(8,128)(2,1)S(1)}, bf16[2,64,512]{2,1,0:T(8,128)(2,1)S(1)}, u32[]{:S(2)}, u32[]{:S(2)}) collective-permute-start(bf16[2,64,512]{2,1,0:T(8,128)(2,1)S(1)} %gate.1.refs_0_), channel_id=1, source_target_pairs={{0,1},{1,0},{2,3},{3,2},{4,5},{5,4},{6,7},{7,6},{8,9},{9,8},{10,11... | collective-permute-start | bytes 393224 | tf_op jit(solution)/shard_map/ppermute | solution.py:384
  12.3 17.8 %copy-start.1 = (bf16[4,256,256]{2,1,0:T(8,128)(2,1)S(1)}, bf16[4,256,256]{2,1,0:T(8,128)(2,1)}, u32[]{:S(2)}) copy-start(bf16[4,256,256]{2,1,0:T(8,128)(2,1)} %constant.13.clone.inverse) | copy-start | bytes 1572868
  12.3 1.7 %collective-permute-start.3 = (bf16[136,128]{1,0:T(8,128)(2,1)S(1)}, bf16[136,128]{1,0:T(8,128)(2,1)S(1)}, u32[]{:S(2)}, u32[]{:S(2)}) collective-permute-start(bf16[136,128]{1,0:T(8,128)(2,1)S(1)} %get-tuple-element.30), channel_id=1, source_target_pairs={{0,4},{4,0},{8,12},{12,8},{16,20},{20,16},{24,28},{28,24},{1,5},{5... | collective-permute-start | bytes 104456 | tf_op jit(solution)/shard_map/ppermute | solution.py:384
  14.0 6.2 %collective-permute-start.6 = (bf16[136,128]{1,0:T(8,128)(2,1)S(1)}, bf16[136,128]{1,0:T(8,128)(2,1)S(1)}, u32[]{:S(2)}, u32[]{:S(2)}) collective-permute-start(bf16[136,128]{1,0:T(8,128)(2,1)S(1)} %add_convert_fusion.1), channel_id=1, source_target_pairs={{0,16},{4,20},{8,24},{12,28},{16,0},{20,4},{24,8},{28,12},{1,17},{... | collective-permute-start | bytes 104456 | tf_op jit(solution)/shard_map/ppermute | solution.py:384
  16.6 4.6 %collective-permute-start.5 = (bf16[136,128]{1,0:T(8,128)(2,1)S(1)}, bf16[136,128]{1,0:T(8,128)(2,1)S(1)}, u32[]{:S(2)}, u32[]{:S(2)}) collective-permute-start(bf16[136,128]{1,0:T(8,128)(2,1)S(1)} %add_convert_fusion.1), channel_id=1, source_target_pairs={{0,24},{4,28},{8,16},{12,20},{16,8},{20,12},{24,0},{28,4},{1,25},{... | collective-permute-start | bytes 104456 | tf_op jit(solution)/shard_map/ppermute | solution.py:384
  17.7 3.5 %collective-permute-start.4 = (bf16[136,128]{1,0:T(8,128)(2,1)S(1)}, bf16[136,128]{1,0:T(8,128)(2,1)S(1)}, u32[]{:S(2)}, u32[]{:S(2)}) collective-permute-start(bf16[136,128]{1,0:T(8,128)(2,1)S(1)} %add_convert_fusion.1), channel_id=1, source_target_pairs={{0,8},{4,12},{8,0},{12,4},{16,24},{20,28},{24,16},{28,20},{1,9},{5... | collective-permute-start | bytes 104456 | tf_op jit(solution)/shard_map/ppermute | solution.py:384
  17.9 6.0 %collective-permute-start.10 = (bf16[256,512]{1,0:T(8,128)(2,1)S(1)}, bf16[256,512]{1,0:T(8,128)(2,1)S(1)}, u32[]{:S(2)}, u32[]{:S(2)}) collective-permute-start(bf16[256,512]{1,0:T(8,128)(2,1)S(1)} %get-tuple-element.31), channel_id=1, source_target_pairs={{0,4},{4,8},{8,12},{12,16},{16,20},{20,24},{24,28},{28,0},{1,5},{5... | collective-permute-start | bytes 786440 | tf_op jit(solution)/shard_map/ppermute | solution.py:461
  21.3 4.0 %collective-permute-start.9 = (bf16[136,128]{1,0:T(8,128)(2,1)S(1)}, bf16[136,128]{1,0:T(8,128)(2,1)S(1)}, u32[]{:S(2)}, u32[]{:S(2)}) collective-permute-start(bf16[136,128]{1,0:T(8,128)(2,1)S(1)} %add_convert_fusion), channel_id=1, source_target_pairs={{0,3},{1,2},{2,1},{3,0},{4,7},{5,6},{6,5},{7,4},{8,11},{9,10},{10,... | collective-permute-start | bytes 104456 | tf_op jit(solution)/shard_map/ppermute | solution.py:384
  23.5 2.8 %collective-permute-start.8 = (bf16[136,128]{1,0:T(8,128)(2,1)S(1)}, bf16[136,128]{1,0:T(8,128)(2,1)S(1)}, u32[]{:S(2)}, u32[]{:S(2)}) collective-permute-start(bf16[136,128]{1,0:T(8,128)(2,1)S(1)} %add_convert_fusion), channel_id=1, source_target_pairs={{0,2},{1,3},{2,0},{3,1},{4,6},{5,7},{6,4},{7,5},{8,10},{9,11},{10,... | collective-permute-start | bytes 104456 | tf_op jit(solution)/shard_map/ppermute | solution.py:384
  23.7 2.8 %collective-permute-start.7 = (bf16[136,128]{1,0:T(8,128)(2,1)S(1)}, bf16[136,128]{1,0:T(8,128)(2,1)S(1)}, u32[]{:S(2)}, u32[]{:S(2)}) collective-permute-start(bf16[136,128]{1,0:T(8,128)(2,1)S(1)} %add_convert_fusion), channel_id=1, source_target_pairs={{0,1},{1,0},{2,3},{3,2},{4,5},{5,4},{6,7},{7,6},{8,9},{9,8},{10,11... | collective-permute-start | bytes 104456 | tf_op jit(solution)/shard_map/ppermute | solution.py:384
  26.5 5.1 %collective-permute-start.11 = (bf16[4,136,128]{2,1,0:T(8,128)(2,1)S(1)}, bf16[4,136,128]{2,1,0:T(8,128)(2,1)S(1)}, u32[]{:S(2)}, u32[]{:S(2)}) collective-permute-start(bf16[4,136,128]{2,1,0:T(8,128)(2,1)S(1)} %pad_maximum_fusion.mine), channel_id=1, source_target_pairs={{0,4},{4,0},{8,12},{12,8},{16,20},{20,16},{24,28},{28,24},{1,5},{5... | collective-permute-start | bytes 417800 | tf_op jit(solution)/shard_map/ppermute | solution.py:384
  30.1 1.5 %copy-start.4 = (bf16[2,2,128,256]{3,2,1,0:T(8,128)(2,1)S(1)}, bf16[2,2,128,256]{3,2,1,0:T(8,128)(2,1)}, u32[]{:S(2)}) copy-start(bf16[2,2,128,256]{3,2,1,0:T(8,128)(2,1)} %constant.14.clone.last) | copy-start | bytes 786436
